TPU v7x, 32 devices: a whole 2x2x4 slice. The times are simulated.
32 devices in a mesh: wide: 8 (over z, x), narrow: 4 (over y, core).
Axes of the slice: x: 2, y: 2, z: 4, core: 2. Of those that a mesh axis runs over, the one named last changes fastest.
Arguments:
- text_in: bfloat16 [2, 32, 4, 108, 768], P(None, ('wide', 'narrow')), may hold values from -6 to 6
- memory_in: bfloat16 [2, 32, 10, 768], P(None, ('wide', 'narrow')), may hold values from -6 to 6
- counts: int32 [2, 32], P(None, ('wide', 'narrow')), may hold values from 2 to 4
- last_len: int32 [2, 32], P(None, ('wide', 'narrow')), may hold values from 1 to 108
- cot_text: bfloat16 [2, 32, 4, 108, 768], P(None, ('wide', 'narrow')), may hold values from -6 to 6
- cot_memory: bfloat16 [2, 32, 10, 768], P(None, ('wide', 'narrow')), may hold values from -6 to 6
- qkv_weight: bfloat16 [2, 3, 768, 768], P(None, None, 'wide', 'narrow'), may hold values from -0.21875 to 0.21875
- out_weight: bfloat16 [2, 768, 768], P(None, 'wide', 'narrow'), may hold values from -0.875 to 0.875
- up_weight: bfloat16 [2, 768, 3072], P(None, 'wide', 'narrow'), may hold values from -0.21875 to 0.21875
- down_weight: bfloat16 [2, 3072, 768], P(None, 'wide', 'narrow'), may hold values from -0.109375 to 0.109375
- biases: bfloat16 [2, 4, 768], P(None, 'narrow', 'wide'), may hold values from -3 to 3
- up_bias: bfloat16 [2, 3072], P(None, ('wide', 'narrow')), may hold values from -3 to 3
- norm_params: bfloat16 [2, 4, 768], P(None, 'narrow', 'wide'), may hold values from -1.2 to 1.5, as said below
Outputs:
- text_out: bfloat16 [2, 32, 4, 108, 768], P(None, ('wide', 'narrow'))
- memory_out: bfloat16 [2, 32, 10, 768], P(None, ('wide', 'narrow'))
- text_grad: bfloat16 [2, 32, 4, 108, 768], P(None, ('wide', 'narrow'))
- memory_grad: bfloat16 [2, 32, 10, 768], P(None, ('wide', 'narrow'))
- grad_qkv: float32 [2, 3, 768, 768], P(None, None, 'wide', 'narrow')
- grad_out: float32 [2, 768, 768], P(None, 'wide', 'narrow')
- grad_up: float32 [2, 768, 3072], P(None, 'wide', 'narrow')
- grad_down: float32 [2, 3072, 768], P(None, 'wide', 'narrow')
- grad_biases: float32 [2, 4, 768], P(None, 'narrow', 'wide')
- grad_up_bias: float32 [2, 3072], P(None, ('wide', 'narrow'))
- grad_norm: float32 [2, 4, 768], P(None, 'narrow', 'wide')
Inputs may be any that keep to these rules, and one draw needn't show every extreme that they name: `norm_params`: rows 0 and 2 of each layer are positive gains, rows 1 and 3 shifts.
All inputs are finite; a program needn't handle non-finite values.
Results may differ from a plain program's by a relative error of at most 0.03.
Values may be sent and summed in bfloat16 or wider, within the bound.
A program may use at most 448 MiB of HBM per device.

v0:
```python
import jax
import jax.numpy as jnp
from jax import lax
from jax.sharding import PartitionSpec as P

HEADS = 12
HD = 64
MEM = 10
TEXT = 108
SEGS = 4
MB = 2
LAYERS = 2


eps = 1e-12


def norm_rows(stream, norm_gain, norm_shift):
    center = stream - jnp.mean(stream, axis=-1, keepdims=True)
    spread = jnp.mean(center * center, axis=-1, keepdims=True)
    return center * lax.rsqrt(spread + eps) * norm_gain + norm_shift


def gelu_exact(values):
    return jax.nn.gelu(values, approximate=False)


def fetch_forward(pieces):
    triple, output_w, expand_w, reduce_w, shifts, inner_b, norm_gains = pieces
    triple, output_w, expand_w, reduce_w, shifts, inner_b, norm_gains = (
        lax.all_gather(triple, "narrow", axis=2, tiled=True),
        lax.all_gather(output_w, "narrow", axis=1, tiled=True),
        lax.all_gather(expand_w, "narrow", axis=1, tiled=True),
        lax.all_gather(reduce_w, "narrow", axis=1, tiled=True),
        lax.all_gather(shifts, "narrow", axis=0, tiled=True),
        lax.all_gather(inner_b, "narrow", axis=0, tiled=True),
        lax.all_gather(norm_gains, "narrow", axis=0, tiled=True),
    )
    return tuple(
        (
            lax.all_gather(triple, "wide", axis=1, tiled=True),
            lax.all_gather(output_w, "wide", axis=0, tiled=True),
            lax.all_gather(expand_w, "wide", axis=0, tiled=True),
            lax.all_gather(reduce_w, "wide", axis=0, tiled=True),
            lax.all_gather(shifts, "wide", axis=1, tiled=True),
            lax.all_gather(inner_b, "wide", axis=0, tiled=True),
            lax.all_gather(norm_gains, "wide", axis=1, tiled=True),
        )
    )


def fetch_backward(pieces):
    triple, output_w, expand_w, reduce_w, shifts, inner_b, norm_gains = pieces
    triple, output_w, expand_w, reduce_w, shifts, inner_b, norm_gains = (
        lax.all_gather(triple, "narrow", axis=2, tiled=True),
        lax.all_gather(output_w, "narrow", axis=1, tiled=True),
        lax.all_gather(expand_w, "narrow", axis=1, tiled=True),
        lax.all_gather(reduce_w, "narrow", axis=1, tiled=True),
        lax.all_gather(shifts, "narrow", axis=0, tiled=True),
        lax.all_gather(inner_b, "narrow", axis=0, tiled=True),
        lax.all_gather(norm_gains, "narrow", axis=0, tiled=True),
    )
    return tuple(
        (
            lax.all_gather(triple, "wide", axis=1, tiled=True),
            lax.all_gather(output_w, "wide", axis=0, tiled=True),
            lax.all_gather(expand_w, "wide", axis=0, tiled=True),
            lax.all_gather(reduce_w, "wide", axis=0, tiled=True),
            lax.all_gather(shifts, "wide", axis=1, tiled=True),
            lax.all_gather(inner_b, "wide", axis=0, tiled=True),
            lax.all_gather(norm_gains, "wide", axis=1, tiled=True),
        )
    )


def split_inner(grad_inner):
    wide_count = lax.axis_size("wide")
    narrow_count = lax.axis_size("narrow")
    layer_count, inner_width = grad_inner.shape
    return grad_inner.reshape(
        layer_count, wide_count, narrow_count, inner_width // (wide_count * narrow_count)
    )


def reduce_end(sums):
    grad_triple, grad_output, grad_expand, grad_reduce, grad_shifts, grad_inner, grad_gains = sums
    grad_inner = split_inner(grad_inner)
    grad_triple, grad_output, grad_expand, grad_reduce, grad_shifts, grad_inner, grad_gains = (
        lax.psum_scatter(
            grad_triple.astype(jnp.bfloat16), "narrow", scatter_dimension=3, tiled=True
        ).astype(jnp.float32),
        lax.psum_scatter(
            grad_output.astype(jnp.bfloat16), "narrow", scatter_dimension=2, tiled=True
        ).astype(jnp.float32),
        lax.psum_scatter(
            grad_expand.astype(jnp.bfloat16), "narrow", scatter_dimension=2, tiled=True
        ).astype(jnp.float32),
        lax.psum_scatter(
            grad_reduce.astype(jnp.bfloat16), "narrow", scatter_dimension=2, tiled=True
        ).astype(jnp.float32),
        lax.psum_scatter(
            grad_shifts.astype(jnp.bfloat16), "narrow", scatter_dimension=1, tiled=True
        ).astype(jnp.float32),
        lax.psum_scatter(
            grad_inner.astype(jnp.bfloat16), "narrow", scatter_dimension=2, tiled=True
        ).astype(jnp.float32),
        lax.psum_scatter(
            grad_gains.astype(jnp.bfloat16), "narrow", scatter_dimension=1, tiled=True
        ).astype(jnp.float32),
    )
    grad_triple, grad_output, grad_expand, grad_reduce, grad_shifts, grad_inner, grad_gains = (
        lax.psum_scatter(grad_triple, "wide", scatter_dimension=2, tiled=True),
        lax.psum_scatter(grad_output, "wide", scatter_dimension=1, tiled=True),
        lax.psum_scatter(grad_expand, "wide", scatter_dimension=1, tiled=True),
        lax.psum_scatter(grad_reduce, "wide", scatter_dimension=1, tiled=True),
        lax.psum_scatter(grad_shifts, "wide", scatter_dimension=2, tiled=True),
        lax.psum_scatter(grad_inner, "wide", scatter_dimension=1, tiled=True),
        lax.psum_scatter(grad_gains, "wide", scatter_dimension=2, tiled=True),
    )
    grad_inner = grad_inner.reshape(grad_inner.shape[0], grad_inner.shape[3])
    return (grad_triple, grad_output, grad_expand, grad_reduce, grad_shifts, grad_inner, grad_gains)


def segment_masks(seg_index, count_rows, length_rows):
    positions = jnp.arange(TEXT, dtype=jnp.int32)
    whole_seg = seg_index < count_rows - 1
    last_seg = seg_index == count_rows - 1
    text_valid = whole_seg[:, None] | last_seg[:, None] & (
        positions[None, :] < length_rows[:, None]
    )
    memory_ones = jnp.ones((count_rows.shape[0], MEM), dtype=jnp.bool_)
    key_valid = jnp.concatenate([memory_ones, text_valid, memory_ones], axis=1)
    return (text_valid, key_valid, seg_index < count_rows)


def attention_scores(query_rows, key_rows, key_valid, head_shape):
    scores = jnp.einsum(
        "iqhd,ikhd->ihqk",
        query_rows.reshape(head_shape),
        key_rows.reshape(head_shape),
        preferred_element_type=jnp.float32,
    ) * HD ** (-0.5)
    return jnp.where(key_valid[:, None, None, :], scores, -1e30)


def layer_forward(stream, key_valid, weights):
    triple, output_w, expand_w, reduce_w, shifts, inner_b, norm_gains = weights
    item_count, seg_rows, model_width = stream.shape
    rows_flat = stream.reshape(item_count * seg_rows, model_width)
    rows_low = rows_flat.astype(jnp.bfloat16)
    query_rows = (
        jnp.dot(rows_low, triple[0], preferred_element_type=jnp.float32) + shifts[0]
    ).astype(jnp.bfloat16)
    key_rows = jnp.dot(rows_low, triple[1], preferred_element_type=jnp.float32).astype(jnp.bfloat16)
    value_rows = (
        jnp.dot(rows_low, triple[2], preferred_element_type=jnp.float32) + shifts[1]
    ).astype(jnp.bfloat16)
    head_shape = (item_count, seg_rows, HEADS, HD)
    scores = attention_scores(query_rows, key_rows, key_valid, head_shape)
    score_max = jnp.max(scores, axis=-1, keepdims=True)
    exp_scores = jnp.exp(scores - score_max)
    exp_total = jnp.sum(exp_scores, axis=-1, keepdims=True)
    attn_probs = exp_scores / exp_total
    log_total = score_max + jnp.log(exp_total)
    context = jnp.einsum(
        "ihqk,ikhd->iqhd",
        attn_probs.astype(jnp.bfloat16),
        value_rows.reshape(head_shape),
        preferred_element_type=jnp.float32,
    )
    context = context.reshape(item_count * seg_rows, model_width).astype(jnp.bfloat16)
    first_sum = rows_flat + (
        jnp.dot(context, output_w, preferred_element_type=jnp.float32) + shifts[2]
    )
    normed = norm_rows(first_sum, norm_gains[0], norm_gains[1])
    inner_pre = (
        jnp.dot(normed.astype(jnp.bfloat16), expand_w, preferred_element_type=jnp.float32) + inner_b
    )
    hidden = gelu_exact(inner_pre).astype(jnp.bfloat16)
    second_sum = normed + (
        jnp.dot(hidden, reduce_w, preferred_element_type=jnp.float32) + shifts[3]
    )
    result = norm_rows(second_sum, norm_gains[2], norm_gains[3])
    kept = (
        rows_flat,
        query_rows,
        key_rows,
        value_rows,
        log_total,
        context,
        first_sum,
        normed,
        inner_pre,
        second_sum,
    )
    return (result.reshape(item_count, seg_rows, model_width), kept)


def layer_backward(grad_out, kept, key_valid, weights):
    triple, output_w, expand_w, reduce_w, shifts, inner_b, norm_gains = weights
    (
        rows_flat,
        query_rows,
        key_rows,
        value_rows,
        log_total,
        context,
        first_sum,
        normed,
        inner_pre,
        second_sum,
    ) = kept
    item_count, seg_rows, model_width = grad_out.shape
    head_shape = (item_count, seg_rows, HEADS, HD)
    gain_values = norm_gains.astype(jnp.float32)
    _, pull_second = jax.vjp(norm_rows, second_sum, gain_values[2], gain_values[3])
    grad_second, grad_gain_two, grad_shift_two = pull_second(
        grad_out.reshape(item_count * seg_rows, model_width)
    )
    grad_ffn = grad_second.astype(jnp.bfloat16)
    hidden = gelu_exact(inner_pre).astype(jnp.bfloat16)
    grad_reduce = jnp.dot(hidden.T, grad_ffn, preferred_element_type=jnp.float32)
    grad_bias_ffn = jnp.sum(grad_ffn.astype(jnp.float32), axis=0)
    grad_hidden = jnp.dot(grad_ffn, reduce_w.T, preferred_element_type=jnp.float32)
    _, pull_gelu = jax.vjp(gelu_exact, inner_pre)
    grad_inner = pull_gelu(grad_hidden)[0].astype(jnp.bfloat16)
    grad_expand = jnp.dot(
        normed.astype(jnp.bfloat16).T, grad_inner, preferred_element_type=jnp.float32
    )
    grad_inner_bias = jnp.sum(grad_inner.astype(jnp.float32), axis=0)
    grad_normed = grad_second + jnp.dot(grad_inner, expand_w.T, preferred_element_type=jnp.float32)
    _, pull_first = jax.vjp(norm_rows, first_sum, gain_values[0], gain_values[1])
    grad_first, grad_gain_one, grad_shift_one = pull_first(grad_normed)
    grad_attn = grad_first.astype(jnp.bfloat16)
    grad_output = jnp.dot(context.T, grad_attn, preferred_element_type=jnp.float32)
    grad_bias_attn = jnp.sum(grad_attn.astype(jnp.float32), axis=0)
    grad_context = (
        jnp.dot(grad_attn, output_w.T, preferred_element_type=jnp.float32)
        .astype(jnp.bfloat16)
        .reshape(head_shape)
    )
    scores = attention_scores(query_rows, key_rows, key_valid, head_shape)
    attn_probs = jnp.exp(scores - log_total)
    grad_probs = jnp.einsum(
        "iqhd,ikhd->ihqk",
        grad_context,
        value_rows.reshape(head_shape),
        preferred_element_type=jnp.float32,
    )
    grad_scores = attn_probs * (
        grad_probs - jnp.sum(attn_probs * grad_probs, axis=-1, keepdims=True)
    )
    grad_scores = grad_scores.astype(jnp.bfloat16)
    score_scale = HD ** (-0.5)
    grad_query = (
        (
            jnp.einsum(
                "ihqk,ikhd->iqhd",
                grad_scores,
                key_rows.reshape(head_shape),
                preferred_element_type=jnp.float32,
            )
            * score_scale
        )
        .astype(jnp.bfloat16)
        .reshape(item_count * seg_rows, model_width)
    )
    grad_key = (
        (
            jnp.einsum(
                "ihqk,iqhd->ikhd",
                grad_scores,
                query_rows.reshape(head_shape),
                preferred_element_type=jnp.float32,
            )
            * score_scale
        )
        .astype(jnp.bfloat16)
        .reshape(item_count * seg_rows, model_width)
    )
    grad_value = (
        jnp.einsum(
            "ihqk,iqhd->ikhd",
            attn_probs.astype(jnp.bfloat16),
            grad_context,
            preferred_element_type=jnp.float32,
        )
        .astype(jnp.bfloat16)
        .reshape(item_count * seg_rows, model_width)
    )
    rows_low = rows_flat.astype(jnp.bfloat16)
    grad_triple = jnp.stack(
        [
            jnp.dot(rows_low.T, grad_query, preferred_element_type=jnp.float32),
            jnp.dot(rows_low.T, grad_key, preferred_element_type=jnp.float32),
            jnp.dot(rows_low.T, grad_value, preferred_element_type=jnp.float32),
        ]
    )
    grad_rows = (
        grad_first
        + jnp.dot(grad_query, triple[0].T, preferred_element_type=jnp.float32)
        + jnp.dot(grad_key, triple[1].T, preferred_element_type=jnp.float32)
        + jnp.dot(grad_value, triple[2].T, preferred_element_type=jnp.float32)
    )
    grad_shifts = jnp.stack(
        [
            jnp.sum(grad_query.astype(jnp.float32), axis=0),
            jnp.sum(grad_value.astype(jnp.float32), axis=0),
            grad_bias_attn,
            grad_bias_ffn,
        ]
    )
    grad_gains = jnp.stack([grad_gain_one, grad_shift_one, grad_gain_two, grad_shift_two])
    layer_grads = (
        grad_triple,
        grad_output,
        grad_expand,
        grad_reduce,
        grad_shifts,
        grad_inner_bias,
        grad_gains,
    )
    return (grad_rows.reshape(item_count, seg_rows, model_width), layer_grads)


def shards(
    text_in,
    memory_in,
    counts,
    last_len,
    cot_text,
    cot_memory,
    qkv_weight,
    out_weight,
    up_weight,
    down_weight,
    biases,
    up_bias,
    norm_params,
):

    def layer_shards(layer_index):
        return (
            qkv_weight[layer_index],
            out_weight[layer_index],
            up_weight[layer_index],
            down_weight[layer_index],
            biases[layer_index],
            up_bias[layer_index],
            norm_params[layer_index],
        )

    text_results, memory_results, text_grads, memory_grads = ([], [], [], [])
    grand_total = None
    seg_ids = jnp.arange(SEGS, dtype=jnp.int32)
    for batch_index in range(MB):
        count_rows = counts[batch_index]
        length_rows = last_len[batch_index]
        forward_weights = [
            fetch_forward(layer_shards(layer_index)) for layer_index in range(LAYERS)
        ]

        def forward_step(memory, inputs):
            text_seg, seg_index = inputs
            text_valid, key_valid, active = segment_masks(seg_index, count_rows, length_rows)
            stream = jnp.concatenate([memory, text_seg.astype(jnp.float32), memory], axis=1)
            kept_layers = []
            for layer_index in range(LAYERS):
                stream, kept = layer_forward(stream, key_valid, forward_weights[layer_index])
                kept_layers.append(kept)
            text_result = jnp.where(
                text_valid[:, :, None], stream[:, MEM : MEM + TEXT], jnp.zeros((), jnp.float32)
            )
            memory_next = jnp.where(active[:, None, None], stream[:, MEM + TEXT :], memory)
            return (memory_next, (text_result.astype(jnp.bfloat16), tuple(kept_layers)))

        memory_start = memory_in[batch_index].astype(jnp.float32)
        memory_end, (text_seq, kept_seq) = lax.scan(
            forward_step, memory_start, (jnp.moveaxis(text_in[batch_index], 1, 0), seg_ids)
        )
        text_results.append(jnp.moveaxis(text_seq, 0, 1))
        memory_results.append(memory_end.astype(jnp.bfloat16))
        backward_weights = [
            fetch_backward(layer_shards(layer_index)) for layer_index in range(LAYERS)
        ]

        def backward_step(carry, inputs):
            grad_memory, layer_sums = carry
            cot_seg, seg_index, kept_layers = inputs
            text_valid, key_valid, active = segment_masks(seg_index, count_rows, length_rows)
            read_zeros = jnp.zeros(grad_memory.shape, jnp.float32)
            grad_text_rows = jnp.where(
                text_valid[:, :, None], cot_seg.astype(jnp.float32), jnp.zeros((), jnp.float32)
            )
            grad_write_rows = jnp.where(active[:, None, None], grad_memory, read_zeros)
            grad_stream = jnp.concatenate([read_zeros, grad_text_rows, grad_write_rows], axis=1)
            new_sums = list(layer_sums)
            for layer_index in reversed(range(LAYERS)):
                grad_stream, layer_grads = layer_backward(
                    grad_stream, kept_layers[layer_index], key_valid, backward_weights[layer_index]
                )
                new_sums[layer_index] = jax.tree.map(jnp.add, layer_sums[layer_index], layer_grads)
            grad_memory_prev = (
                jnp.where(active[:, None, None], read_zeros, grad_memory)
                + grad_stream[:, :MEM]
                + grad_stream[:, MEM + TEXT :]
            )
            return (
                (grad_memory_prev, tuple(new_sums)),
                grad_stream[:, MEM : MEM + TEXT].astype(jnp.bfloat16),
            )

        zero_sums = tuple(
            (
                tuple((jnp.zeros(piece.shape, jnp.float32) for piece in layer_weights))
                for layer_weights in backward_weights
            )
        )
        carry_start = (cot_memory[batch_index].astype(jnp.float32), zero_sums)
        (grad_memory_end, layer_sums), grad_text_seq = lax.scan(
            backward_step,
            carry_start,
            (jnp.moveaxis(cot_text[batch_index], 1, 0), seg_ids, kept_seq),
            reverse=True,
        )
        text_grads.append(jnp.moveaxis(grad_text_seq, 0, 1))
        memory_grads.append(grad_memory_end.astype(jnp.bfloat16))
        batch_sums = tuple(
            (
                jnp.stack([layer_sums[layer_index][part_index] for layer_index in range(LAYERS)])
                for part_index in range(7)
            )
        )
        grand_total = (
            batch_sums if grand_total is None else jax.tree.map(jnp.add, grand_total, batch_sums)
        )
    grand_total = reduce_end(grand_total)
    return (
        jnp.stack(text_results),
        jnp.stack(memory_results),
        jnp.stack(text_grads),
        jnp.stack(memory_grads),
        grand_total[0],
        grand_total[1],
        grand_total[2],
        grand_total[3],
        grand_total[4],
        grand_total[5],
        grand_total[6],
    )


def solution(mesh):
    return jax.shard_map(
        shards,
        mesh=mesh,
        in_specs=(
            P(None, ("wide", "narrow"), None, None, None),
            P(None, ("wide", "narrow"), None, None),
            P(None, ("wide", "narrow")),
            P(None, ("wide", "narrow")),
            P(None, ("wide", "narrow"), None, None, None),
            P(None, ("wide", "narrow"), None, None),
            P(None, None, "wide", "narrow"),
            P(None, "wide", "narrow"),
            P(None, "wide", "narrow"),
            P(None, "wide", "narrow"),
            P(None, "narrow", "wide"),
            P(None, ("wide", "narrow")),
            P(None, "narrow", "wide"),
        ),
        out_specs=(
            P(None, ("wide", "narrow"), None, None, None),
            P(None, ("wide", "narrow"), None, None),
            P(None, ("wide", "narrow"), None, None, None),
            P(None, ("wide", "narrow"), None, None),
            P(None, None, "wide", "narrow"),
            P(None, "wide", "narrow"),
            P(None, "wide", "narrow"),
            P(None, "wide", "narrow"),
            P(None, "narrow", "wide"),
            P(None, ("wide", "narrow")),
            P(None, "narrow", "wide"),
        ),
        check_vma=False,
    )
```

profile of v0, /device:TPU:0, one launch (start us, length us, event | category | flops | bytes accessed | tf_op | source)
XLA Modules:
  0.0 3129.2 jit_solution(5421440256455020235)
XLA Ops:
  95.3 26.7 all-gather.25
  122.1 26.7 all-gather.11
  169.7 31.8 %all-gather.21 = bf16[4,1,768]{0,1,2:T(2,128)(2,1)S(1)} all-gather(bf16[4,1,96]{0,1,2:T(2,128)(2,1)S(1)} %copy.460), channel_id=23, replica_groups=mesh['wide'=8,'narrow'=4] {'wide'}, dimensions={2}, use_global_device_ids=true | all-gather | bytes 6912 | tf_op jit(solution)/shard_map/all_gather | solution.py:47
  201.7 32.1 %all-gather.17 = bf16[4,1,768]{0,1,2:T(2,128)(2,1)S(1)} all-gather(bf16[4,1,96]{0,1,2:T(2,128)(2,1)S(1)} %copy.455), channel_id=19, replica_groups=mesh['wide'=8,'narrow'=4] {'wide'}, dimensions={2}, use_global_device_ids=true | all-gather | bytes 6912 | tf_op jit(solution)/shard_map/all_gather | solution.py:45
  234.1 31.6 %all-gather.7 = bf16[4,1,768]{0,1,2:T(2,128)(2,1)S(1)} all-gather(bf16[4,1,96]{0,1,2:T(2,128)(2,1)S(1)} %copy.450), channel_id=9, replica_groups=mesh['wide'=8,'narrow'=4] {'wide'}, dimensions={2}, use_global_device_ids=true | all-gather | bytes 6912 | tf_op jit(solution)/shard_map/all_gather | solution.py:47
  266.0 32.2 %all-gather.3 = bf16[4,1,768]{0,1,2:T(2,128)(2,1)S(1)} all-gather(bf16[4,1,96]{0,1,2:T(2,128)(2,1)S(1)} %copy.444), channel_id=5, replica_groups=mesh['wide'=8,'narrow'=4] {'wide'}, dimensions={2}, use_global_device_ids=true | all-gather | bytes 6912 | tf_op jit(solution)/shard_map/all_gather | solution.py:45
  317.5 20.7 all-gather.37.cloned.1.call-done
  338.1 66.0 %all-gather.45.cloned.1.call-done = bf16[1,3,768,768]{3,2,1,0:T(8,128)(2,1)} async-done(((bf16[1,3,96,768]{3,2,1,0:T(8,128)(2,1)}), bf16[1,3,768,768]{3,2,1,0:T(8,128)(2,1)}) %all-gather.45.cloned.1.call-update) | async-done | bytes 3538960 | tf_op jit(solution)/shard_map/all_gather | solution.py:41
  404.1 80.3 %all-gather.49.cloned.1.call-done = bf16[1,768,3072]{2,1,0:T(8,128)(2,1)} async-done(((bf16[1,96,3072]{2,1,0:T(8,128)(2,1)}), bf16[1,768,3072]{2,1,0:T(8,128)(2,1)}) %all-gather.49.cloned.1.call-update) | async-done | bytes 4718608 | tf_op jit(solution)/shard_map/all_gather | solution.py:43
  484.4 79.9 %all-gather.41.cloned.1.call-done = bf16[1,768,3072]{2,1,0:T(8,128)(2,1)} async-done(((bf16[1,96,3072]{2,1,0:T(8,128)(2,1)}), bf16[1,768,3072]{2,1,0:T(8,128)(2,1)}) %all-gather.41.cloned.1.call-update) | async-done | bytes 4718608 | tf_op jit(solution)/shard_map/all_gather | solution.py:43
  586.6 236.1 %while.199 = (s32[]{:T(128)}, f32[1,10,768]{2,1,0:T(8,128)S(1)}, bf16[4,1,108,768]{3,2,1,0:T(8,128)(2,1)}, bf16[4,128,768]{2,1,0:T(8,128)(2,1)}, bf16[4,128,768]...) while((s32[]{:T(128)}, f32[1,10,768]{2,1,0:T(8,128)S(1)}, ...), condition=%wide.region_27.28_spmd, body=%wide.region_14.27_spmd.sunk | while | flops 3791095296 | bytes 147678608 | solution.py:378
  845.0 248.3 %while.198 = (s32[]{:T(128)}, f32[1,10,768]{2,1,0:T(8,128)S(1)}, bf16[4,1,108,768]{3,2,1,0:T(8,128)(2,1)}, bf16[4,128,768]{2,1,0:T(8,128)(2,1)}, bf16[4,128,768]...) while((s32[]{:T(128)}, f32[1,10,768]{2,1,0:T(8,128)S(1)}, ...), condition=%wide.region_13.14_spmd, body=%wide.region_0.13_spmd.sunk | while | flops 3791095296 | bytes 147678608 | solution.py:378
  1094.2 604.6 %while.201 = (s32[]{:T(128)}, f32[1,10,768]{2,1,0:T(8,128)}, f32[3,768,768]{2,1,0:T(8,128)}, f32[768,768]{1,0:T(8,128)}, f32[768,3072]{1,0:T(8,128)}, /*index=5*...) while((s32[]{:T(128)}, f32[1,10,768]{2,1,0:T(8,128)}, ...), condition=%wide.region_105.106_spmd.clone, body=%wide.region_67.105_spmd.clone.sunk | while | flops 7661838336 | bytes 556537408 | solution.py:420
  1192.0 10.8 maximum_add_fusion.28
  1226.1 10.8 select_add_fusion.39
  1334.7 16.0 maximum_add_fusion.28
  1374.6 15.8 select_add_fusion.39
  1488.2 16.0 maximum_add_fusion.28
  1517.6 10.6 select_add_fusion.43
  1528.3 15.8 select_add_fusion.39
  1641.9 16.0 maximum_add_fusion.28
  1681.7 15.8 select_add_fusion.39
  1699.7 616.9 %while.200 = (s32[]{:T(128)}, f32[1,10,768]{2,1,0:T(8,128)S(1)}, f32[3,768,768]{2,1,0:T(8,128)}, f32[768,768]{1,0:T(8,128)}, f32[768,3072]{1,0:T(8,128)}, /*inde...) while((s32[]{:T(128)}, f32[1,10,768]{2,1,0:T(8,128)S(1)}, ...), condition=%wide.region_66.67_spmd.clone, body=%wide.region_28.66_spmd.clone.sunk | while | flops 7661838336 | bytes 556316224 | solution.py:420
  1804.6 10.8 maximum_add_fusion.25
  1838.4 10.9 select_add_fusion.32
  1946.7 15.9 maximum_add_fusion.25
  1976.0 10.6 select_add_fusion.36
  1986.6 15.8 select_add_fusion.32
  2099.9 15.9 maximum_add_fusion.25
  2139.7 15.8 select_add_fusion.32
  2252.9 15.9 maximum_add_fusion.25
  2292.9 15.8 select_add_fusion.32
  2330.3 13.8 fusion.762
  2344.1 16.2 copy.527
  2360.3 18.9 reshape.2431
  2379.3 19.2 fusion.760
  2437.2 16.2 fusion.761
  2454.5 11.8 all-reduce.5
  2489.0 35.0 %reduce-scatter.24.cloned.1.call-done = bf16[2,768,768]{2,1,0:T(8,128)(2,1)} async-done(((bf16[2,768,3072]{2,1,0:T(8,128)(2,1)}), bf16[2,768,768]{2,1,0:T(8,128)(2,1)}) %reduce-scatter.24.cloned.1.call-update) | async-done | bytes 2359312 | tf_op jit(solution)/shard_map/reduce_scatter | solution.py:95
  2528.4 76.0 %reduce-scatter.28.cloned.1.call-done = bf16[2,3072,192]{1,2,0:T(8,128)(2,1)} async-done(((bf16[2,3072,768]{1,2,0:T(8,128)(2,1)}), bf16[2,3072,192]{1,2,0:T(8,128)(2,1)}) %reduce-scatter.28.cloned.1.call-update) | async-done | bytes 2359312 | tf_op jit(solution)/shard_map/reduce_scatter | solution.py:98
  2617.1 52.9 %reduce-scatter.40.cloned.1.call-done = f32[96,2]{1,0:T(8,128)} async-done(((f32[768,2]{1,0:T(8,128)}), f32[96,2]{1,0:T(8,128)}) %reduce-scatter.40.cloned.1.call-update) | async-done | bytes 784
  2671.5 62.7 %reduce-scatter.38.cloned.1.call-done = f32[96,2]{1,0:T(8,128)} async-done(((f32[768,2]{1,0:T(8,128)}), f32[96,2]{1,0:T(8,128)}) %reduce-scatter.38.cloned.1.call-update) | async-done | bytes 784
  2735.8 19.3 reduce-scatter.32.cloned.1.call-done
  2755.8 21.8 all-reduce.3
  2778.8 45.9 %reduce-scatter.22.cloned.1.call-done = f32[2,96,192]{2,1,0:T(8,128)} async-done(((f32[2,768,192]{2,1,0:T(8,128)}), f32[2,96,192]{2,1,0:T(8,128)}) %reduce-scatter.22.cloned.1.call-update) | async-done | bytes 147472 | tf_op jit(solution)/shard_map/reduce_scatter | solution.py:113
  2824.7 98.5 %reduce-scatter.20.cloned.1.call-done = f32[2,3,96,192]{3,2,1,0:T(8,128)} async-done(((f32[2,3,768,192]{3,2,1,0:T(8,128)}), f32[2,3,96,192]{3,2,1,0:T(8,128)}) %reduce-scatter.20.cloned.1.call-update) | async-done | bytes 442384 | tf_op jit(solution)/shard_map/reduce_scatter | solution.py:112
  2923.2 99.4 %reduce-scatter.26.cloned.1.call-done = f32[2,96,768]{2,1,0:T(8,128)} async-done(((f32[2,768,768]{2,1,0:T(8,128)}), f32[2,96,768]{2,1,0:T(8,128)}) %reduce-scatter.26.cloned.1.call-update) | async-done | bytes 589840 | tf_op jit(solution)/shard_map/reduce_scatter | solution.py:114
  3022.7 99.6 %reduce-scatter.30.cloned.1.call-done = f32[2,384,192]{1,2,0:T(8,128)} async-done(((f32[2,3072,192]{1,2,0:T(8,128)}), f32[2,384,192]{1,2,0:T(8,128)}) %reduce-scatter.30.cloned.1.call-update) | async-done | bytes 589840 | tf_op jit(solution)/shard_map/reduce_scatter | solution.py:115
  (4137 shorter events, 1633.0 us)
Async XLA Ops:
  7.2 296.8 %all-gather.51.cloned.1.call-start = ((), (), s32[]{:S(2)}) async-start(), calls=%async_computation.25 | async-start | bytes 5308416 | tf_op jit(solution)/shard_map/all_gather | solution.py:44
  17.8 293.0 %all-gather.43.cloned.1.call-start = ((), (), s32[]{:S(2)}) async-start(), calls=%async_computation.21 | async-start | bytes 5308416 | tf_op jit(solution)/shard_map/all_gather | solution.py:44
  25.9 291.5 %all-gather.39.cloned.1.call-start = ((), (), s32[]{:S(2)}) async-start(), calls=%async_computation.19 | async-start | bytes 1327104 | tf_op jit(solution)/shard_map/all_gather | solution.py:42
  33.6 283.8 %all-gather.47.cloned.1.call-start = ((), (), s32[]{:S(2)}) async-start(), calls=%async_computation.23 | async-start | bytes 1327104 | tf_op jit(solution)/shard_map/all_gather | solution.py:42
  41.3 296.8 %all-gather.37.cloned.1.call-start = ((), (), s32[]{:S(2)}) async-start(), calls=%async_computation.18 | async-start | bytes 3981312 | tf_op jit(solution)/shard_map/all_gather | solution.py:41
  51.5 352.7 %all-gather.45.cloned.1.call-start = ((), (), s32[]{:S(2)}) async-start(), calls=%async_computation.22 | async-start | bytes 3981312 | tf_op jit(solution)/shard_map/all_gather | solution.py:41
  61.6 422.8 %all-gather.49.cloned.1.call-start = ((), (), s32[]{:S(2)}) async-start(), calls=%async_computation.24 | async-start | bytes 5308416 | tf_op jit(solution)/shard_map/all_gather | solution.py:43
  69.8 494.5 %all-gather.41.cloned.1.call-start = ((), (), s32[]{:S(2)}) async-start(), calls=%async_computation.20 | async-start | bytes 5308416 | tf_op jit(solution)/shard_map/all_gather | solution.py:43
  77.9 2395.2 %reduce-scatter.36.cloned.1.call-start = ((), (), s32[]{:S(2)}) async-start(), calls=%async_computation.27 | async-start | bytes 2949120
  82.8 66.1 %copy-start.283 = (bf16[2,1,96]{2,0,1:T(2,128)(2,1)S(1)}, bf16[2,1,96]{2,0,1:T(2,128)(2,1)}, u32[]{:S(2)}) copy-start(bf16[2,1,96]{2,0,1:T(2,128)(2,1)} %param.31) | copy-start | bytes 1156
  82.8 71.3 %copy-start.284 = (bf16[2,1,96]{2,0,1:T(2,128)(2,1)S(1)}, bf16[2,1,96]{2,0,1:T(2,128)(2,1)}, u32[]{:S(2)}) copy-start(bf16[2,1,96]{2,0,1:T(2,128)(2,1)} %param.33) | copy-start | bytes 1156
  201.5 97.1 %copy-start.285 = (s32[2,1]{0,1:T(1,128)S(1)}, s32[2,1]{0,1:T(1,128)}, u32[]{:S(2)}) copy-start(s32[2,1]{0,1:T(1,128)} %param.24) | copy-start | bytes 28
  201.5 97.7 %copy-start.205 = (bf16[2,1,10,768]{3,0,2,1:T(2,128)(2,1)S(1)}, bf16[2,1,10,768]{3,0,2,1:T(2,128)(2,1)}, u32[]{:S(2)}) copy-start(bf16[2,1,10,768]{3,0,2,1:T(2,128)(2,1)} %param.22) | copy-start | bytes 92164
  201.5 97.7 %copy-start.206 = (bf16[2,1,10,768]{3,0,2,1:T(2,128)(2,1)S(1)}, bf16[2,1,10,768]{3,0,2,1:T(2,128)(2,1)}, u32[]{:S(2)}) copy-start(bf16[2,1,10,768]{3,0,2,1:T(2,128)(2,1)} %param.26) | copy-start | bytes 92164
  201.7 98.8 %copy-start.111 = (bf16[2,1,4,108,768]{4,2,3,1,0:T(4,128)(2,1)S(1)}, bf16[2,1,4,108,768]{4,2,3,1,0:T(4,128)(2,1)}, u32[]{:S(2)}) copy-start(bf16[2,1,4,108,768]{4,2,3,1,0:T(4,128)(2,1)} %param.21) | copy-start | bytes 3981316
  1094.2 605.5 %copy-start.84 = (f32[1,10,768]{2,1,0:T(8,128)S(1)}, f32[1,10,768]{2,1,0:T(8,128)}, u32[]{:S(2)}) copy-start(f32[1,10,768]{2,1,0:T(8,128)} %get-tuple-element.7067) | copy-start | bytes 92164
  1094.2 605.5 %copy-start.151 = (f32[4,768]{1,0:T(4,128)S(1)}, f32[4,768]{1,0:T(4,128)}, u32[]{:S(2)}) copy-start(f32[4,768]{1,0:T(4,128)} %custom-call.13) | copy-start | bytes 36868
  1105.8 29.2 copy-start.215
  1107.0 28.0 copy-start.250
  1248.3 29.2 copy-start.215
  1249.5 28.0 copy-start.250
  1332.9 21.7 slice-start.25
  1402.0 29.2 copy-start.215
  1403.2 28.0 copy-start.250
  1486.3 21.7 slice-start.25
  1555.4 29.2 copy-start.215
  1556.7 28.0 copy-start.250
  1640.0 21.7 slice-start.25
  1717.8 30.2 copy-start.216
  1718.0 30.0 copy-start.251
  1860.0 30.2 copy-start.216
  1860.3 29.9 copy-start.251
  1944.7 21.7 slice-start.19
  2013.0 30.2 copy-start.216
  2013.3 30.0 copy-start.251
  2166.3 30.2 copy-start.216
  2166.5 30.0 copy-start.251
  2251.0 21.7 slice-start.19
  2330.2 146.9 %reduce-scatter.34.cloned.1.call-start = ((), (), s32[]{:S(2)}) async-start(), calls=%async_computation.26 | async-start | bytes 8847360
  2379.2 144.8 %reduce-scatter.24.cloned.1.call-start = ((), (), s32[]{:S(2)}) async-start(), calls=%async_computation.13 | async-start | bytes 11796480 | tf_op jit(solution)/shard_map/reduce_scatter | solution.py:95
  2398.5 205.9 %reduce-scatter.28.cloned.1.call-start = ((), (), s32[]{:S(2)}) async-start(), calls=%async_computation.15 | async-start | bytes 11796480 | tf_op jit(solution)/shard_map/reduce_scatter | solution.py:98
  2453.5 216.4 %reduce-scatter.40.cloned.1.call-start = ((), (), s32[]{:S(2)}) async-start(), calls=%async_computation.29 | async-start | bytes 442368
  2470.4 263.8 %reduce-scatter.38.cloned.1.call-start = ((), (), s32[]{:S(2)}) async-start(), calls=%async_computation.28 | async-start | bytes 442368
  2472.4 282.7 %reduce-scatter.32.cloned.1.call-start = ((), (), s32[]{:S(2)}) async-start(), calls=%async_computation.17 | async-start | bytes 20480 | tf_op jit(solution)/shard_map/reduce_scatter | solution.py:104
  2473.1 351.6 %reduce-scatter.22.cloned.1.call-start = ((), (), s32[]{:S(2)}) async-start(), calls=%async_computation.12 | async-start | bytes 1769472 | tf_op jit(solution)/shard_map/reduce_scatter | solution.py:113
  2477.0 446.2 %reduce-scatter.20.cloned.1.call-start = ((), (), s32[]{:S(2)}) async-start(), calls=%async_computation.11 | async-start | bytes 5308416 | tf_op jit(solution)/shard_map/reduce_scatter | solution.py:112
  2488.9 533.7 %reduce-scatter.26.cloned.1.call-start = ((), (), s32[]{:S(2)}) async-start(), calls=%async_computation.14 | async-start | bytes 5308416 | tf_op jit(solution)/shard_map/reduce_scatter | solution.py:114
  2528.1 594.1 %reduce-scatter.30.cloned.1.call-start = ((), (), s32[]{:S(2)}) async-start(), calls=%async_computation.16 | async-start | bytes 5308416 | tf_op jit(solution)/shard_map/reduce_scatter | solution.py:115
  (1183 other events, 5143.1 us)
Sparse Core Ops, SparseCore 0:
  17.9 81.4 all-gather.50
  101.4 80.8 all-gather.42
  185.0 41.5 all-gather.38
  229.2 42.0 all-gather.46
  273.9 64.2 all-gather.36
  340.8 63.3 all-gather.44
  406.3 78.0 all-gather.48
  486.6 77.6 all-gather.40
  2330.4 32.7 reduce-scatter.35
  2379.4 64.1 reduce-scatter.33
  2446.2 77.7 reduce-scatter.23
  2526.4 77.9 reduce-scatter.27
  2607.7 62.1 reduce-scatter.39
  2673.0 61.1 reduce-scatter.37
  2736.4 18.6 reduce-scatter.31
  2758.9 65.6 reduce-scatter.21
  2828.7 94.4 reduce-scatter.19
  2927.3 95.3 reduce-scatter.25
  3026.9 95.2 reduce-scatter.29
where the time goes:
time: 3150 us; the launch traced here: 3130 us
  matrix products  951 us (30%)
  waiting for transfers between devices  836 us (27%)
  local copies, waits for them, and re-layouts  473 us (15%)
  other arithmetic  455 us (14%)
  blocking collectives  306 us (10%)
  loops' own time  89 us (3%)
    dot_general x16, matrix products, layer_backward(): jnp.dot(hidden.T, grad_ffn, preferred_element_type=jnp.float32)  200 us
    all_gather x2, waiting for transfers between devices, fetch_forward(): lax.all_gather(expand_w, 'wide', axis=0, tiled=True)  160 us
    add x32, other arithmetic, backward_step(): jax.tree.map(jnp.add, layer_sums[layer_index], layer_grads)  129 us
    dot_general x16, matrix products, layer_backward(): jnp.dot(grad_ffn, reduce_w.T, preferred_element_type=jnp.float32)  127 us
    unnamed x23, waiting for transfers between devices  116 us
    reduce_scatter x1, waiting for transfers between devices, reduce_end(): lax.psum_scatter(grad_reduce, 'wide', scatter_dimension=1, tiled=True)  99.6 us
    reduce_scatter x1, waiting for transfers between devices, reduce_end(): lax.psum_scatter(grad_expand, 'wide', scatter_dimension=1, tiled=True)  99.4 us
    reduce_scatter x1, waiting for transfers between devices, reduce_end(): lax.psum_scatter(grad_triple, 'wide', scatter_dimension=2, tiled=True)  98.5 us

commit v1 on v0

v1 whole, which is shorter than its diff:
```python
import functools

import jax
import jax.numpy as jnp
from jax import lax
from jax.experimental import pallas as pl
from jax.experimental.pallas import tpu as pltpu
from jax.sharding import PartitionSpec as P

HEADS = 12
HD = 64
MEM = 10
TEXT = 108
SEGS = 4
MB = 2
LAYERS = 2
SEG = TEXT + 2 * MEM
TAIL = 104
ROWS = MB * SEG
EPS = 1e-12
BF = jnp.bfloat16
F32 = jnp.float32
NEG = -1e30
RSQRT2 = 0.7071067811865476
RSQRT2PI = 0.3989422804014327
VMEM_LIMIT = 66_000_000
FT = 512


def dot(a, b):
    return lax.dot_general(a, b, (((1,), (0,)), ((), ())), preferred_element_type=F32)


def dot_rt(a, b):
    return lax.dot_general(a, b, (((1,), (1,)), ((), ())), preferred_element_type=F32)


def dot_lt(a, b):
    return lax.dot_general(a, b, (((0,), (0,)), ((), ())), preferred_element_type=F32)


def row_ids(shape):
    return lax.broadcasted_iota(jnp.int32, shape, 0)


def lane_ids(shape):
    return lax.broadcasted_iota(jnp.int32, shape, 1)


def valid_rows(seg, count, length):
    return jnp.where(seg < count - 1, TEXT, jnp.where(seg == count - 1, length, 0))


def colsum(v):
    rows, cols = v.shape
    return jnp.sum(v.reshape(rows // 8, 8, cols), axis=0)


def fwd_kernel(
    counts, lens, text, mem0, wqkv, wo, wup, wdn, bias, ubias, norm,
    text_out, mem_out, a_out, qkv_out, p_out, c_out, y_out, g_out, gp_out, xh1_out, xh2_out, rs_out,
    x_ref, mem_ref, y_ref, acc_ref,
):
    seg = pl.program_id(0)
    layer = pl.program_id(1)
    d = x_ref.shape[-1]

    @pl.when((seg == 0) & (layer == 0))
    def _():
        mem_ref[...] = mem0[...]

    @pl.when(layer == 0)
    def _():
        for i in range(MB):
            x_ref[i * SEG : i * SEG + TEXT, :] = text[i, 0].astype(F32)
            tail = slice(i * SEG + TAIL, (i + 1) * SEG)
            now = x_ref[tail, :]
            x_ref[tail, :] = jnp.where(row_ids(now.shape) < TEXT - TAIL, now, mem_ref[i])

    xb = x_ref[...].astype(BF)
    a_out[0] = xb
    qkv_out[0, :, 0:d] = (dot(xb, wqkv[layer, 0]) + bias[layer, 0:1, :]).astype(BF)
    qkv_out[0, :, d : 2 * d] = dot(xb, wqkv[layer, 1]).astype(BF)
    qkv_out[0, :, 2 * d : 3 * d] = (dot(xb, wqkv[layer, 2]) + bias[layer, 1:2, :]).astype(BF)

    low_half = lane_ids((SEG, 128)) < HD
    lanes = lane_ids((1, SEG))
    for i in range(MB):
        vr = valid_rows(seg, counts[i], lens[i])
        keep = (lanes < vr) | (lanes >= TEXT)
        r0 = i * SEG
        for pair in range(HEADS // 2):
            c0 = pair * 128
            q = qkv_out[0, r0 : r0 + SEG, c0 : c0 + 128]
            k = qkv_out[0, r0 : r0 + SEG, d + c0 : d + c0 + 128]
            v = qkv_out[0, r0 : r0 + SEG, 2 * d + c0 : 2 * d + c0 + 128]
            zero = jnp.zeros_like(q)
            q2 = jnp.concatenate([jnp.where(low_half, q, zero), jnp.where(low_half, zero, q)], axis=0)
            s = dot_rt(q2, k) * (HD ** -0.5)
            s = jnp.where(keep, s, NEG)
            e = jnp.exp(s - jnp.max(s, axis=-1, keepdims=True))
            p = (e / jnp.sum(e, axis=-1, keepdims=True)).astype(BF)
            u0 = (i * (HEADS // 2) + pair) * 2 * SEG
            p_out[0, u0 : u0 + 2 * SEG, :] = p
            c2 = dot(p, v)
            c_out[0, r0 : r0 + SEG, c0 : c0 + 128] = jnp.where(low_half, c2[:SEG], c2[SEG:]).astype(BF)

    def norm_to(h, gain, shift, xh_out, rs_index):
        center = h - jnp.mean(h, axis=-1, keepdims=True)
        rs = lax.rsqrt(jnp.mean(center * center, axis=-1, keepdims=True) + EPS)
        xh = center * rs
        xh_out[0] = xh
        rs_out[0, rs_index] = jnp.broadcast_to(rs, (ROWS, 128))
        return xh * gain + shift

    h1 = x_ref[...] + (dot(c_out[0], wo[layer]) + bias[layer, 2:3, :])
    y = norm_to(h1, norm[layer, 0:1, :], norm[layer, 1:2, :], xh1_out, 0)
    y_ref[...] = y
    y_out[0] = y.astype(BF)

    acc_ref[...] = jnp.zeros_like(acc_ref)
    ff = wup.shape[-1]

    def ffn_step(j, carry):
        cols = pl.ds(pl.multiple_of(j * FT, FT), FT)
        u = dot(y_out[0], wup[layer, :, cols]) + ubias[layer, :, cols]
        cdf = 0.5 * (1.0 + lax.erf(u * RSQRT2))
        g = (u * cdf).astype(BF)
        g_out[0, :, cols] = g
        gp_out[0, :, cols] = (cdf + u * (jnp.exp(-0.5 * (u * u)) * RSQRT2PI)).astype(BF)
        acc_ref[...] += dot(g, wdn[layer, cols, :])
        return carry

    lax.fori_loop(0, ff // FT, ffn_step, 0)
    h2 = y_ref[...] + (acc_ref[...] + bias[layer, 3:4, :])
    x_ref[...] = norm_to(h2, norm[layer, 2:3, :], norm[layer, 3:4, :], xh2_out, 1)

    @pl.when(layer == LAYERS - 1)
    def _():
        for i in range(MB):
            vr = valid_rows(seg, counts[i], lens[i])
            body = x_ref[i * SEG : i * SEG + TEXT, :]
            text_out[i, 0] = jnp.where(row_ids(body.shape) < vr, body, 0.0).astype(BF)
            tail = x_ref[i * SEG + TAIL : (i + 1) * SEG, :]
            both = jnp.where(row_ids(tail.shape) >= TEXT - TAIL + MEM, tail, pltpu.roll(tail, SEG - TAIL - MEM, axis=0))
            mem_ref[i] = jnp.where(seg < counts[i], both, mem_ref[i])
        mem_out[...] = mem_ref[...]


def whole(shape):
    return pl.BlockSpec(shape, lambda *_: (0,) * len(shape), pipeline_mode=pl.Buffered(1))


def saved(rows, cols):
    return pl.BlockSpec((1, rows, cols), lambda s, l: (l, s, 0))


def forward_local(text, mem, counts, lens, weights):
    wqkv, wo, wup, wdn, bias, ubias, norm = weights
    d, ff = wup.shape[1:]
    mem0 = jnp.concatenate([jnp.zeros((MB, TEXT - TAIL, d), F32), mem.astype(F32), mem.astype(F32)], axis=1)
    total = SEGS * ROWS
    units = MB * HEADS * SEG
    smem = pl.BlockSpec(memory_space=pltpu.SMEM)
    outs = pl.pallas_call(
        fwd_kernel,
        grid=(SEGS, LAYERS),
        in_specs=[
            smem, smem,
            pl.BlockSpec((MB, 1, TEXT, d), lambda s, l: (0, s, 0, 0)),
            whole(mem0.shape), whole(wqkv.shape), whole(wo.shape), whole(wup.shape), whole(wdn.shape),
            whole(bias.shape), whole((LAYERS, 1, ff)), whole(norm.shape),
        ],
        out_specs=[
            pl.BlockSpec((MB, 1, TEXT, d), lambda s, l: (0, s, 0, 0)),
            whole(mem0.shape),
            saved(ROWS, d), saved(ROWS, 3 * d), saved(units, 128), saved(ROWS, d), saved(ROWS, d),
            saved(ROWS, ff), saved(ROWS, ff), saved(ROWS, d), saved(ROWS, d),
            pl.BlockSpec((1, 2, ROWS, 128), lambda s, l: (l, 0, s, 0)),
        ],
        out_shape=[
            jax.ShapeDtypeStruct((MB, SEGS, TEXT, d), BF),
            jax.ShapeDtypeStruct(mem0.shape, F32),
            jax.ShapeDtypeStruct((LAYERS, total, d), BF),
            jax.ShapeDtypeStruct((LAYERS, total, 3 * d), BF),
            jax.ShapeDtypeStruct((LAYERS, SEGS * units, 128), BF),
            jax.ShapeDtypeStruct((LAYERS, total, d), BF),
            jax.ShapeDtypeStruct((LAYERS, total, d), BF),
            jax.ShapeDtypeStruct((LAYERS, total, ff), BF),
            jax.ShapeDtypeStruct((LAYERS, total, ff), BF),
            jax.ShapeDtypeStruct((LAYERS, total, d), F32),
            jax.ShapeDtypeStruct((LAYERS, total, d), F32),
            jax.ShapeDtypeStruct((LAYERS, 2, total, 128), F32),
        ],
        scratch_shapes=[
            pltpu.VMEM((ROWS, d), F32), pltpu.VMEM(mem0.shape, F32),
            pltpu.VMEM((ROWS, d), F32), pltpu.VMEM((ROWS, d), F32),
        ],
        compiler_params=pltpu.CompilerParams(
            dimension_semantics=("arbitrary", "arbitrary"), vmem_limit_bytes=VMEM_LIMIT
        ),
        name="rmt_forward",
    )(counts, lens, text, mem0, wqkv, wo, wup, wdn, bias.astype(F32), ubias.astype(F32)[:, None, :], norm.astype(F32))
    text_out, mem_end = outs[:2]
    return text_out, mem_end[:, TEXT - TAIL + MEM :].astype(BF), outs[2:]


def bwd_kernel(
    counts, lens, cot, gm0, qkv, p_in, gp_in, xh1_in, xh2_in, rs_in, wqkv, wo, wup, wdn, norm,
    tg_out, gm_out, dqkv_out, dao_out, du_out, df_out, gb_out, gub_out, gn_out,
    g_ref, gm_ref, t_ref, acc_ref, dc_ref,
):
    seg = SEGS - 1 - pl.program_id(0)
    step = pl.program_id(1)
    layer = LAYERS - 1 - step
    d = g_ref.shape[-1]

    @pl.when((seg == SEGS - 1) & (step == 0))
    def _():
        gm_ref[...] = gm0[...]
        gb_out[...] = jnp.zeros_like(gb_out)
        gub_out[...] = jnp.zeros_like(gub_out)
        gn_out[...] = jnp.zeros_like(gn_out)

    @pl.when(step == 0)
    def _():
        for i in range(MB):
            vr = valid_rows(seg, counts[i], lens[i])
            ct = cot[i, 0].astype(F32)
            g_ref[i * SEG : i * SEG + TEXT, :] = jnp.where(row_ids(ct.shape) < vr, ct, 0.0)
            tail = slice(i * SEG + TAIL, (i + 1) * SEG)
            now = g_ref[tail, :]
            rows = row_ids(now.shape)
            mem_part = jnp.where((rows >= TEXT - TAIL + MEM) & (seg < counts[i]), gm_ref[i], 0.0)
            g_ref[tail, :] = jnp.where(rows < TEXT - TAIL, now, mem_part)

    def norm_back(gout, xh, rs, gain, slot):
        gn_out[layer, slot] += colsum(gout * xh)
        gn_out[layer, slot + 1] += colsum(gout)
        t = gout * gain
        return rs * (t - jnp.mean(t, axis=-1, keepdims=True) - xh * jnp.mean(t * xh, axis=-1, keepdims=True))

    dh2 = norm_back(g_ref[...], xh2_in[0], rs_in[0, 1][:, :1], norm[layer, 2:3, :], 2)
    t_ref[...] = dh2
    df = dh2.astype(BF)
    df_out[0] = df
    gb_out[layer, 3] += colsum(df.astype(F32))
    acc_ref[...] = jnp.zeros_like(acc_ref)
    ff = wup.shape[-1]

    def ffn_step(j, carry):
        cols = pl.ds(pl.multiple_of(j * FT, FT), FT)
        dg = dot_rt(df_out[0], wdn[layer, cols, :])
        du = (dg * gp_in[0, :, cols].astype(F32)).astype(BF)
        du_out[0, :, cols] = du
        gub_out[layer, :, cols] += colsum(du.astype(F32))
        acc_ref[...] += dot_rt(du, wup[layer, :, cols])
        return carry

    lax.fori_loop(0, ff // FT, ffn_step, 0)
    dh1 = norm_back(t_ref[...] + acc_ref[...], xh1_in[0], rs_in[0, 0][:, :1], norm[layer, 0:1, :], 0)
    t_ref[...] = dh1
    dao = dh1.astype(BF)
    dao_out[0] = dao
    gb_out[layer, 2] += colsum(dao.astype(F32))
    dc_ref[...] = dot_rt(dao, wo[layer]).astype(BF)

    low_half = lane_ids((SEG, 128)) < HD
    scale = HD ** -0.5
    for i in range(MB):
        r0 = i * SEG
        for pair in range(HEADS // 2):
            c0 = pair * 128
            q = qkv[0, r0 : r0 + SEG, c0 : c0 + 128]
            k = qkv[0, r0 : r0 + SEG, d + c0 : d + c0 + 128]
            v = qkv[0, r0 : r0 + SEG, 2 * d + c0 : 2 * d + c0 + 128]
            dc = dc_ref[r0 : r0 + SEG, c0 : c0 + 128]
            zero = jnp.zeros_like(q)
            q2 = jnp.concatenate([jnp.where(low_half, q, zero), jnp.where(low_half, zero, q)], axis=0)
            dc2 = jnp.concatenate([jnp.where(low_half, dc, zero), jnp.where(low_half, zero, dc)], axis=0)
            u0 = (i * (HEADS // 2) + pair) * 2 * SEG
            pb = p_in[0, u0 : u0 + 2 * SEG, :]
            p = pb.astype(F32)
            pdp = p * dot_rt(dc2, v)
            ds = (pdp - p * jnp.sum(pdp, axis=-1, keepdims=True)).astype(BF)
            dq2 = dot(ds, k)
            dq = (jnp.where(low_half, dq2[:SEG], dq2[SEG:]) * scale).astype(BF)
            dk = (dot_lt(ds, q2) * scale).astype(BF)
            dv = dot_lt(pb, dc2).astype(BF)
            dqkv_out[0, r0 : r0 + SEG, c0 : c0 + 128] = dq
            dqkv_out[0, r0 : r0 + SEG, d + c0 : d + c0 + 128] = dk
            dqkv_out[0, r0 : r0 + SEG, 2 * d + c0 : 2 * d + c0 + 128] = dv

    gb_out[layer, 0] += colsum(dqkv_out[0, :, 0:d].astype(F32))
    gb_out[layer, 1] += colsum(dqkv_out[0, :, 2 * d : 3 * d].astype(F32))
    g_ref[...] = (
        t_ref[...]
        + dot_rt(dqkv_out[0, :, 0:d], wqkv[layer, 0])
        + dot_rt(dqkv_out[0, :, d : 2 * d], wqkv[layer, 1])
        + dot_rt(dqkv_out[0, :, 2 * d : 3 * d], wqkv[layer, 2])
    )

    @pl.when(layer == 0)
    def _():
        for i in range(MB):
            tg_out[i, 0] = g_ref[i * SEG : i * SEG + TEXT, :].astype(BF)
            tail = g_ref[i * SEG + TAIL : (i + 1) * SEG, :]
            back = tail + pltpu.roll(tail, MEM, axis=0)
            gm_ref[i] = jnp.where(seg < counts[i], 0.0, gm_ref[i]) + back
        gm_out[...] = gm_ref[...]


def backward_local(cot, cot_mem, counts, lens, kept, weights):
    wqkv, wo, wup, wdn, _, _, norm = weights
    _, qkv, p_all, _, _, _, gp, xh1, xh2, rs = kept
    d, ff = wup.shape[1:]
    gm0 = jnp.concatenate([jnp.zeros((MB, TEXT - TAIL + MEM, d), F32), cot_mem.astype(F32)], axis=1)
    total = SEGS * ROWS
    units = MB * HEADS * SEG
    smem = pl.BlockSpec(memory_space=pltpu.SMEM)

    def kept_spec(rows, cols):
        return pl.BlockSpec((1, rows, cols), lambda s, l: (LAYERS - 1 - l, SEGS - 1 - s, 0))

    outs = pl.pallas_call(
        bwd_kernel,
        grid=(SEGS, LAYERS),
        in_specs=[
            smem, smem,
            pl.BlockSpec((MB, 1, TEXT, d), lambda s, l: (0, SEGS - 1 - s, 0, 0)),
            whole(gm0.shape),
            kept_spec(ROWS, 3 * d), kept_spec(units, 128), kept_spec(ROWS, ff), kept_spec(ROWS, d), kept_spec(ROWS, d),
            pl.BlockSpec((1, 2, ROWS, 128), lambda s, l: (LAYERS - 1 - l, 0, SEGS - 1 - s, 0)),
            whole(wqkv.shape), whole(wo.shape), whole(wup.shape), whole(wdn.shape), whole(norm.shape),
        ],
        out_specs=[
            pl.BlockSpec((MB, 1, TEXT, d), lambda s, l: (0, SEGS - 1 - s, 0, 0)),
            whole(gm0.shape),
            kept_spec(ROWS, 3 * d), kept_spec(ROWS, d), kept_spec(ROWS, ff), kept_spec(ROWS, d),
            whole((LAYERS, 4, 8, d)), whole((LAYERS, 8, ff)), whole((LAYERS, 4, 8, d)),
        ],
        out_shape=[
            jax.ShapeDtypeStruct((MB, SEGS, TEXT, d), BF),
            jax.ShapeDtypeStruct(gm0.shape, F32),
            jax.ShapeDtypeStruct((LAYERS, total, 3 * d), BF),
            jax.ShapeDtypeStruct((LAYERS, total, d), BF),
            jax.ShapeDtypeStruct((LAYERS, total, ff), BF),
            jax.ShapeDtypeStruct((LAYERS, total, d), BF),
            jax.ShapeDtypeStruct((LAYERS, 4, 8, d), F32),
            jax.ShapeDtypeStruct((LAYERS, 8, ff), F32),
            jax.ShapeDtypeStruct((LAYERS, 4, 8, d), F32),
        ],
        scratch_shapes=[
            pltpu.VMEM((ROWS, d), F32), pltpu.VMEM(gm0.shape, F32),
            pltpu.VMEM((ROWS, d), F32), pltpu.VMEM((ROWS, d), F32), pltpu.VMEM((ROWS, d), BF),
        ],
        compiler_params=pltpu.CompilerParams(
            dimension_semantics=("arbitrary", "arbitrary"), vmem_limit_bytes=VMEM_LIMIT
        ),
        name="rmt_backward",
    )(counts, lens, cot, gm0, qkv, p_all, gp, xh1, xh2, rs, wqkv, wo, wup, wdn, norm.astype(F32))
    tg, gm = outs[:2]
    small = (outs[6].sum(axis=2), outs[7].sum(axis=1), outs[8].sum(axis=2))
    return tg, gm[:, TEXT - TAIL + MEM :].astype(BF), outs[2:6], small


def weight_grads(kept, grads):
    a, _, _, c, y, g = kept[:6]
    dqkv, dao, du, df = grads
    d = a.shape[-1]

    def per_layer(lhs, rhs):
        return jnp.stack([dot_lt(lhs[l], rhs[l]).astype(BF) for l in range(LAYERS)])

    gq = jnp.stack([
        jnp.stack([dot_lt(a[l], dqkv[l, :, j * d : (j + 1) * d]).astype(BF) for j in range(3)]) for l in range(LAYERS)
    ])
    return gq, per_layer(c, dao), per_layer(y, du), per_layer(g, df)


def gather_weights(pieces):
    wqkv, wo, wup, wdn, bias, ubias, norm = pieces
    narrow = [(wqkv, 3), (wo, 2), (wup, 2), (wdn, 2), (bias, 1), (norm, 1)]
    wqkv, wo, wup, wdn, bias, norm = (lax.all_gather(w, "narrow", axis=k, tiled=True) for w, k in narrow)
    wide = [(wqkv, 2), (wo, 1), (wup, 1), (wdn, 1), (bias, 2), (norm, 2)]
    wqkv, wo, wup, wdn, bias, norm = (lax.all_gather(w, "wide", axis=k, tiled=True) for w, k in wide)
    ubias = lax.all_gather(ubias, ("wide", "narrow"), axis=1, tiled=True)
    return wqkv, wo, wup, wdn, bias, ubias, norm


def scatter_two(grad, row_axis, col_axis):
    low = lax.psum_scatter(grad.astype(BF), "narrow", scatter_dimension=col_axis, tiled=True)
    return lax.psum_scatter(low.astype(F32), "wide", scatter_dimension=row_axis, tiled=True)


def scatter_grads(big, small):
    gq, go, gup, gdn = big
    gb, gub, gn = small
    big = (scatter_two(gq, 2, 3), scatter_two(go, 1, 2), scatter_two(gup, 1, 2), scatter_two(gdn, 1, 2))
    gub = lax.psum_scatter(gub, ("wide", "narrow"), scatter_dimension=1, tiled=True)

    def small_two(g):
        return lax.psum_scatter(
            lax.psum_scatter(g, "narrow", scatter_dimension=1, tiled=True), "wide", scatter_dimension=2, tiled=True
        )

    return big + (small_two(gb), gub, small_two(gn))


def shards(
    text_in, memory_in, counts, last_len, cot_text, cot_memory,
    qkv_weight, out_weight, up_weight, down_weight, biases, up_bias, norm_params,
):
    text, cot = text_in[:, 0], cot_text[:, 0]
    mem, cot_mem = memory_in[:, 0], cot_memory[:, 0]
    cnt, lens = counts[:, 0], last_len[:, 0]
    weights = gather_weights((qkv_weight, out_weight, up_weight, down_weight, biases, up_bias, norm_params))
    text_out, mem_out, kept = forward_local(text, mem, cnt, lens, weights)
    text_grad, mem_grad, grads, small = backward_local(cot, cot_mem, cnt, lens, kept, weights)
    grads = scatter_grads(weight_grads(kept, grads), small)
    return (text_out[:, None], mem_out[:, None], text_grad[:, None], mem_grad[:, None]) + grads


def solution(mesh):
    items = ("wide", "narrow")
    act5 = P(None, items, None, None, None)
    act4 = P(None, items, None, None)
    ids = P(None, items)
    split = P(None, "wide", "narrow")
    small = P(None, "narrow", "wide")
    params = (P(None, None, "wide", "narrow"), split, split, split, small, ids, small)
    return jax.shard_map(
        shards,
        mesh=mesh,
        in_specs=(act5, act4, ids, ids, act5, act4) + params,
        out_specs=(act5, act4, act5, act4) + params,
        check_vma=False,
    )
```

time: 3150 us -> 2150 us (0.68)
  matrix products: 951 us -> 55.7 us
  local copies, waits for them, and re-layouts: 473 us -> 1050 us
  other arithmetic: 455 us -> 39.9 us
  waiting for transfers between devices: 836 us -> 647 us
  Pallas kernels: 0 us -> 181 us
  blocking collectives: 306 us -> 152 us
  loops' own time: 89 us -> 0 us
    unnamed x120 -> x78, local copies, waits for them, and re-layouts: 73.7 us -> 986 us
    dot_general x400 -> x12, matrix products: 951 us -> 55.7 us  [dot_lt(): lax.dot_general(a, b, (((0,), (0,)), ((), ())), preferred_element_type=F32)]
    reduce_scatter x7 -> x2, waiting for transfers between devices: 474 us -> 37.7 us  [the longest x1 37.7 us: scatter_two(): lax.psum_scatter(low.astype(F32), 'wide', scatter_dimension=row_axis, til...]
    pallas_call x0 -> x2, Pallas kernels: none -> 181 us  [the longest x1 103 us: backward_local(): pl.pallas_call(bwd_kernel, grid=(SEGS, LAYERS), in_specs=[smem, smem, pl....]
    unnamed x23 -> x22, waiting for transfers between devices: 116 us -> 280 us
    add x56 -> x0, other arithmetic: 141 us -> none  [the longest x32 129 us: backward_step(): jax.tree.map(jnp.add, layer_sums[layer_index], layer_grads)]
    all_gather x18 -> x7, blocking collectives: 266 us -> 140 us  [the longest x2 66.2 us: gather_weights(): lax.all_gather(w, 'wide', axis=k, tiled=True)]
    reduce_sum x208 -> x3, other arithmetic: 118 us -> 0.19 us  [backward_local(): small = (outs[6].sum(axis=2), outs[7].sum(axis=1), outs[8].sum(axis=2))]
where the time goes in v1:
time: 2150 us; the launch traced here: 2140 us
  local copies, waits for them, and re-layouts  1050 us (49%)
  waiting for transfers between devices  647 us (30%)
  Pallas kernels  181 us (8%)
  blocking collectives  152 us (7%)
  matrix products  55.7 us (3%)
  other arithmetic  39.9 us (2%)
    unnamed x78, local copies, waits for them, and re-layouts  986 us
    all_gather x4, waiting for transfers between devices, gather_weights(): lax.all_gather(w, 'wide', axis=k, tiled=True)  317 us
    unnamed x22, waiting for transfers between devices  280 us
    pallas_call x1, Pallas kernels, backward_local(): pl.pallas_call(bwd_kernel, grid=(SEGS, LAYERS), in_specs=[smem, smem, pl....  103 us
    pallas_call x1, Pallas kernels, forward_local(): pl.pallas_call(fwd_kernel, grid=(SEGS, LAYERS), in_specs=[smem, smem, pl....  78.2 us
    all_gather x2, blocking collectives, gather_weights(): lax.all_gather(w, 'wide', axis=k, tiled=True)  66.2 us
    dot_general x12, matrix products, dot_lt(): lax.dot_general(a, b, (((0,), (0,)), ((), ())), preferred_element_type=F32)  55.7 us
  transfers between devices with their start and end apart: 15, of which 7 were waited for; matrix products, arithmetic and copies ran while one was open for 49% of the time, Pallas kernels for 0%

profile of v1, /device:TPU:0, one launch (start us, length us, event | category | flops | bytes accessed | tf_op | source)
XLA Modules:
  0.0 2137.6 jit_solution(1766798374525760111)
XLA Ops:
  11.0 8.0 all_gather.41
  21.2 14.3 all_gather.39
  35.5 3.1 copy.96
  39.3 13.2 all-gather.16.cloned.1.call-done
  52.5 4.7 copy.100
  57.3 41.1 %all-gather = bf16[32,96,2]{1,2,0:T(2,128)(2,1)S(1)} all-gather(bf16[1,96,2]{1,2,0:T(2,128)(2,1)S(1)} %bitcast.431), channel_id=1, replica_groups=mesh['wide'=8,'narrow'=4] {'wide','narrow'}, dimensions={0}, use_global_device_ids=true | all-gather | bytes 12672 | tf_op jit(solution)/shard_map/all_gather | solution.py:387
  99.2 5.0 all_gather.50
  104.4 5.1 all_gather.47
  109.6 32.9 %all_gather.48 = bf16[2,4,768]{1,0,2:T(2,128)(2,1)S(1)} all-gather(bf16[2,4,96]{1,0,2:T(2,128)(2,1)S(1)} %copy.101), channel_id=1, replica_groups=mesh['wide'=8,'narrow'=4] {'wide'}, dimensions={2}, use_global_device_ids=true | all-gather | bytes 13824 | tf_op jit(solution)/shard_map/all_gather | solution.py:386
  143.5 33.2 %all_gather.51 = bf16[2,4,768]{1,0,2:T(2,128)(2,1)S(1)} all-gather(bf16[2,4,96]{1,0,2:T(2,128)(2,1)S(1)} %copy.104), channel_id=1, replica_groups=mesh['wide'=8,'narrow'=4] {'wide'}, dimensions={2}, use_global_device_ids=true | all-gather | bytes 13824 | tf_op jit(solution)/shard_map/all_gather | solution.py:386
  181.6 40.5 %all-gather.8.cloned.1.call-done.wqkv = bf16[2,3,768,768]{3,2,1,0:T(8,128)(2,1)} async-done(((bf16[2,3,96,768]{3,2,1,0:T(8,128)(2,1)}), bf16[2,3,768,768]{3,2,1,0:T(8,128)(2,1)}) %all-gather.8.cloned.1.call-update) | async-done | bytes 7077904 | tf_op jit(solution)/shard_map/all_gather | solution.py:386
  222.1 137.9 %all-gather.14.cloned.1.call-done.wup = bf16[2,768,3072]{2,1,0:T(8,128)(2,1)} async-done(((bf16[2,96,3072]{2,1,0:T(8,128)(2,1)}), bf16[2,768,3072]{2,1,0:T(8,128)(2,1)}) %all-gather.14.cloned.1.call-update) | async-done | bytes 9437200 | tf_op jit(solution)/shard_map/all_gather | solution.py:386
  360.0 138.1 %all-gather.18.cloned.1.call-done.wdn = bf16[2,3072,768]{2,1,0:T(8,128)(2,1)} async-done(((bf16[2,384,768]{2,1,0:T(8,128)(2,1)}), bf16[2,3072,768]{2,1,0:T(8,128)(2,1)}) %all-gather.18.cloned.1.call-update) | async-done | bytes 9437200 | tf_op jit(solution)/shard_map/all_gather | solution.py:386
  498.1 78.2 %rmt_forward.1 = (bf16[2,4,108,768]{3,2,1,0:T(8,128)(2,1)}, f32[2,24,768]{2,1,0:T(8,128)}, bf16[2,1024,768]{2,1,0:T(8,128)(2,1)}, bf16[2,1024,2304]{2,1,0:T(8,12...) custom-call(s32[2]{0:T(128)} %bitcast.427, ...), custom_call_target="tpu_custom_call" | custom-call | tf_op jit(solution)/shard_map/rmt_forward/pallas_call | solution.py:165
  576.3 102.9 %rmt_backward.1 = (bf16[2,4,108,768]{3,2,1,0:T(8,128)(2,1)}, f32[2,24,768]{2,1,0:T(8,128)}, bf16[2,1024,2304]{2,1,0:T(8,128)(2,1)}, bf16[2,1024,768]{2,1,0:T(8,1...) custom-call(s32[2]{0:T(128)} %bitcast.428, ...), custom_call_target="tpu_custom_call" | custom-call | tf_op jit(solution)/shard_map/rmt_backward/pallas_call | solution.py:325
  679.3 3.5 fusion.118
  682.8 3.5 fusion.123
  697.7 2.5 fusion.153
  701.3 7.4 fusion.24
  708.7 7.0 fusion.27
  716.0 4.6 copy.109
  720.6 3.1 maximum_bitcast_fusion
  723.6 3.4 pad_maximum_fusion.2
  727.1 18.2 copy.108
  745.3 8.3 pad_maximum_fusion.1
  753.6 24.0 %copy.110 = bf16[2,3072,768]{1,0,2:T(2,128)(2,1)} copy(bf16[2,3072,768]{2,1,0:T(8,128)(2,1)} %pad_maximum_fusion.1) | data formatting | bytes 18874368 | tf_op jit(solution)/shard_map/stack | solution.py:373
  779.4 10.9 fusion.30
  790.3 9.5 fusion.33
  799.8 8.3 pad_maximum_fusion
  809.6 12.8 all-reduce.6
  829.9 268.6 %all-reduce.10.cloned.1.call-done = (bf16[2,3,768,768]{2,0,1,3:T(2,128)(2,1)}, bf16[2,768,768]{1,0,2:T(2,128)(2,1)}, bf16[2,3072,768]{1,0,2:T(2,128)(2,1)}) async-done(((bf16[2,3,768,768]{2,0,1,3:T(2,128)(2,1)}, bf16[2,768,768]{1,0,2:T(2,128)(2,1)}, bf16[2,3072,768]{1,0,2:T(2,128)(2,1)}), (bf16[2,3,768,768]{2,0,1,3:T(2,128)(2,1)}, bf16[2,768,768]{1,0,2:T(2,128)(2,1)}, ...) | async-done | bytes 18874384
  1100.0 37.5 %copy.124 = f32[2,768,192]{0,2,1:T(8,128)} copy(f32[2,768,192]{1,0,2:T(2,128)S(1)} %dynamic-slice_convert_fusion.2) | data formatting | bytes 2359296
  1137.5 52.6 %reshape.33 = f32[768,384]{1,0:T(8,128)} reshape(f32[768,192,2]{2,1,0:T(8,128)} %bitcast.51) | data formatting | bytes 2359296
  1190.4 2.7 dynamic-slice_convert_fusion.1
  1193.1 182.8 %copy.122 = f32[2,3,768,192]{0,1,3,2:T(4,128)} copy(f32[2,3,768,192]{2,0,1,3:T(2,128)S(1)} %dynamic-slice_convert_fusion.1) | data formatting | bytes 7077888
  1375.9 211.2 %reshape.31 = f32[768,1152]{1,0:T(8,128)} reshape(f32[768,192,3,2]{3,2,1,0:T(4,128)} %bitcast.48) | data formatting | bytes 7077888
  1587.1 5.4 dynamic-slice_convert_fusion
  1592.6 141.2 %copy.126 = f32[2,3072,192]{0,2,1:T(8,128)} copy(f32[2,3072,192]{1,0,2:T(2,128)} %dynamic-slice_convert_fusion) | data formatting | bytes 9437184
  1733.7 201.6 %reshape.35 = f32[3072,384]{1,0:T(8,128)} reshape(f32[3072,192,2]{2,1,0:T(8,128)} %bitcast.54) | data formatting | bytes 9437184
  1935.7 4.2 convert_element_type.86
  1952.5 11.7 reshape.34
  1964.2 7.0 copy.120
  1971.2 24.1 %reshape.32 = f32[96,192,3,2]{3,2,1,0:T(4,128)} reshape(f32[96,1152]{1,0:T(8,128)} %reduce-scatter.25.cloned.1.call-done) | data formatting | bytes 884736
  1995.3 26.5 %copy.119 = f32[2,3,96,192]{3,2,1,0:T(8,128)} copy(f32[2,3,96,192]{0,1,3,2:T(4,128)} %bitcast.416) | data formatting | bytes 884736
  2021.8 9.6 reduce-scatter.29.cloned.1.call-done
  2031.4 40.1 %reshape.36 = f32[384,192,2]{2,1,0:T(8,128)} reshape(f32[384,384]{1,0:T(8,128)} %reduce-scatter.29.cloned.1.call-done) | data formatting | bytes 1179648
  2071.5 21.6 %copy.121 = f32[2,384,192]{1,2,0:T(8,128)} copy(f32[2,384,192]{0,2,1:T(8,128)} %bitcast.417) | data formatting | bytes 1179648
  2093.1 37.7 %reduce-scatter.23.cloned.1.call-done = f32[2,96,768]{2,1,0:T(8,128)} async-done(((f32[2,768,768]{2,1,0:T(8,128)}), f32[2,96,768]{2,1,0:T(8,128)}) %reduce-scatter.23.cloned.1.call-update) | async-done | bytes 589840 | tf_op jit(solution)/shard_map/reduce_scatter | solution.py:393
  (135 shorter events, 51.0 us)
Async XLA Ops:
  7.2 31.5 %all-gather.12.cloned.1.call-start = ((), (), s32[]{:S(2)}) async-start(), calls=%async_computation.10 | async-start | bytes 1474560 | tf_op jit(solution)/shard_map/all_gather | solution.py:384
  7.9 44.6 %all-gather.16.cloned.1.call-start = ((), (), s32[]{:S(2)}) async-start(), calls=%async_computation.12 | async-start | bytes 1474560 | tf_op jit(solution)/shard_map/all_gather | solution.py:384
  10.0 171.6 %all-gather.10.cloned.1.call-start = ((), (), s32[]{:S(2)}) async-start(), calls=%async_computation.9 | async-start | bytes 2654208 | tf_op jit(solution)/shard_map/all_gather | solution.py:386
  20.0 202.1 %all-gather.8.cloned.1.call-start = ((), (), s32[]{:S(2)}) async-start(), calls=%async_computation.8 | async-start | bytes 7962624 | tf_op jit(solution)/shard_map/all_gather | solution.py:386
  38.6 18.7 copy-start.9
  38.6 60.6 %copy-start.10 = (bf16[2,1,96]{2,0,1:T(2,128)(2,1)S(1)}, bf16[2,1,96]{2,0,1:T(2,128)(2,1)}, u32[]{:S(2)}) copy-start(bf16[2,1,96]{2,0,1:T(2,128)(2,1)} %param.25) | copy-start | bytes 1156
  38.6 65.7 %copy-start.11 = (bf16[2,1,96]{2,0,1:T(2,128)(2,1)S(1)}, bf16[2,1,96]{2,0,1:T(2,128)(2,1)}, u32[]{:S(2)}) copy-start(bf16[2,1,96]{2,0,1:T(2,128)(2,1)} %param.23) | copy-start | bytes 1156
  38.6 70.9 %copy-start.7 = (bf16[2,1,10,768]{3,0,2,1:T(2,128)(2,1)S(1)}, bf16[2,1,10,768]{3,0,2,1:T(2,128)(2,1)}, u32[]{:S(2)}) copy-start(bf16[2,1,10,768]{3,0,2,1:T(2,128)(2,1)} %param.18) | copy-start | bytes 92164
  38.7 321.4 %all-gather.14.cloned.1.call-start = ((), (), s32[]{:S(2)}) async-start(), calls=%async_computation.11 | async-start | bytes 10616832 | tf_op jit(solution)/shard_map/all_gather | solution.py:386
  38.7 138.9 %copy-start.2 = (bf16[2,1,4,108,768]{4,2,3,1,0:T(4,128)(2,1)S(1)}, bf16[2,1,4,108,768]{4,2,3,1,0:T(4,128)(2,1)}, u32[]{:S(2)}) copy-start(bf16[2,1,4,108,768]{4,2,3,1,0:T(4,128)(2,1)} %param.13) | copy-start | bytes 3981316
  39.2 458.9 %all-gather.18.cloned.1.call-start = ((), (), s32[]{:S(2)}) async-start(), calls=%async_computation.13 | async-start | bytes 10616832 | tf_op jit(solution)/shard_map/all_gather | solution.py:386
  57.2 121.7 %copy-start.3 = (bf16[2,1,4,108,768]{4,2,3,1,0:T(4,128)(2,1)S(1)}, bf16[2,1,4,108,768]{4,2,3,1,0:T(4,128)(2,1)}, u32[]{:S(2)}) copy-start(bf16[2,1,4,108,768]{4,2,3,1,0:T(4,128)(2,1)} %param.17) | copy-start | bytes 3981316
  57.3 1041.3 %all-reduce.10.cloned.1.call-start = ((), (), s32[]{:S(2)}) async-start(), calls=%async_computation.22 | async-start | bytes 37748736
  143.5 37.4 %copy-start.8 = (bf16[2,1,10,768]{3,0,2,1:T(2,128)(2,1)S(1)}, bf16[2,1,10,768]{3,0,2,1:T(2,128)(2,1)}, u32[]{:S(2)}) copy-start(bf16[2,1,10,768]{3,0,2,1:T(2,128)(2,1)} %param.14) | copy-start | bytes 92164
  679.2 7.0 slice-start.3
  679.2 7.0 slice-start.4
  682.7 3.5 slice-start.5
  682.7 3.5 copy-start.13
  692.8 7.5 slice-start
  695.2 5.0 slice-start.1
  697.7 2.5 slice-start.2
  697.7 3.6 copy-start.14
  777.5 1.9 copy-start.12
  777.6 1158.2 %reduce-scatter.21.cloned.1.call-start = ((), (), s32[]{:S(2)}) async-start(), calls=%async_computation.14 | async-start | bytes 11796480 | tf_op jit(solution)/shard_map/reduce_scatter | solution.py:392
  808.1 0.7 copy-start.15
  808.1 1.2 copy-start.6
  808.1 1.3 copy-start.5
  808.2 19.9 copy-start.4
  808.2 1139.6 %reduce-scatter.35.cloned.1.call-start = ((), (), s32[]{:S(2)}) async-start(), calls=%async_computation.21 | async-start | bytes 442368
  825.7 1123.8 %reduce-scatter.31.cloned.1.call-start = ((), (), s32[]{:S(2)}) async-start(), calls=%async_computation.19 | async-start | bytes 442368
  827.4 1123.7 %reduce-scatter.33.cloned.1.call-start = ((), (), s32[]{:S(2)}) async-start(), calls=%async_computation.20 | async-start | bytes 1622016
  829.9 1122.6 %reduce-scatter.27.cloned.1.call-start = ((), (), s32[]{:S(2)}) async-start(), calls=%async_computation.17 | async-start | bytes 1327104
  1190.1 781.1 %reduce-scatter.25.cloned.1.call-start = ((), (), s32[]{:S(2)}) async-start(), calls=%async_computation.16 | async-start | bytes 3981312
  1587.1 444.3 %reduce-scatter.29.cloned.1.call-start = ((), (), s32[]{:S(2)}) async-start(), calls=%async_computation.18 | async-start | bytes 5308416
  1935.4 195.4 %reduce-scatter.23.cloned.1.call-start = ((), (), s32[]{:S(2)}) async-start(), calls=%async_computation.15 | async-start | bytes 5308416 | tf_op jit(solution)/shard_map/reduce_scatter | solution.py:393
  1939.9 1.3 copy-start
  1939.9 4.6 copy-start.1
Sparse Core Ops, SparseCore 0:
  9.5 23.6 all-gather.11
  35.3 17.1 all-gather.15
  55.3 52.3 all-gather.9
  110.3 111.7 all-gather.7
  224.2 135.8 all-gather.13
  362.7 135.4 all-gather.17
  777.7 320.7 all-reduce.9
  1101.1 77.9 reduce-scatter.20
  1183.0 62.2 reduce-scatter.34
  1249.0 61.2 reduce-scatter.30
  1315.5 96.9 reduce-scatter.32
  1415.8 63.7 reduce-scatter.26
  1587.2 79.5 reduce-scatter.24
  1935.5 95.8 reduce-scatter.28
  2035.5 95.3 reduce-scatter.22

commit v2 on v1

--- a/solution.py
+++ b/solution.py
@@ -367,15 +367,348 @@
 def weight_grads(kept, grads):
     a, _, _, c, y, g = kept[:6]
     dqkv, dao, du, df = grads
-    d = a.shape[-1]
-
-    def per_layer(lhs, rhs):
-        return jnp.stack([dot_lt(lhs[l], rhs[l]).astype(BF) for l in range(LAYERS)])
-
-    gq = jnp.stack([
-        jnp.stack([dot_lt(a[l], dqkv[l, :, j * d : (j + 1) * d]).astype(BF) for j in range(3)]) for l in range(LAYERS)
-    ])
-    return gq, per_layer(c, dao), per_layer(y, du), per_layer(g, df)
+
+    def product(lhs, rhs):
+        dims = (((1,), (1,)), ((0,), (0,)))
+        return lax.dot_general(lhs, rhs, dims, preferred_element_type=F32).astype(BF)
+
+    return product(a, dqkv), product(c, dao), product(y, du), product(g, df)
+
+
+MESH = pl.DeviceIdType.MESH
+ZN = 4
+
+
+def multiple(v, k):
+    return v if isinstance(v, int) else pl.multiple_of(v, k)
+
+
+def span(start, size):
+    return pl.ds(multiple(start, size if size % 128 else 128), size)
+
+
+def where_am_i():
+    w, n = lax.axis_index("wide"), lax.axis_index("narrow")
+    z, x = lax.div(w, 2), lax.rem(w, 2)
+    y, c = lax.div(n, 2), lax.rem(n, 2)
+    links = {
+        "p": {"wide": w, "narrow": n + 1 - 2 * c},
+        "x": {"wide": w + 1 - 2 * x, "narrow": n},
+        "y": {"wide": w, "narrow": lax.rem(n + 2, 4)},
+        "up": {"wide": w + 2, "narrow": n},
+        "down": {"wide": w - 2, "narrow": n},
+    }
+    return w, n, z, x, y, c, links
+
+
+def enter(z, links):
+    barrier = pltpu.get_barrier_semaphore()
+    for name in ("p", "x", "y"):
+        pl.semaphore_signal(barrier, inc=1, device_id=links[name], device_id_type=MESH)
+
+    @pl.when(z < ZN - 1)
+    def _():
+        pl.semaphore_signal(barrier, inc=1, device_id=links["up"], device_id_type=MESH)
+
+    @pl.when(z > 0)
+    def _():
+        pl.semaphore_signal(barrier, inc=1, device_id=links["down"], device_id_type=MESH)
+
+    pl.semaphore_wait(barrier, 3 + jnp.minimum(z, 1) + jnp.minimum(ZN - 1 - z, 1))
+
+
+class Net:
+    def __init__(self, ssem, rsem, links):
+        self.ssem, self.rsem, self.links = ssem, rsem, links
+        self.next_send, self.next_recv = 0, 0
+
+    def sends(self, count):
+        base, self.next_send = self.next_send, self.next_send + count
+        return base
+
+    def recvs(self, count):
+        base, self.next_recv = self.next_recv, self.next_recv + count
+        return base
+
+    def copy(self, link, src, dst, s, r):
+        return pltpu.make_async_remote_copy(
+            src_ref=src, dst_ref=dst, send_sem=self.ssem.at[s], recv_sem=self.rsem.at[r],
+            device_id=self.links[link], device_id_type=MESH,
+        )
+
+
+def gather_kernel(
+    q_in, o_in, u_in, d_in, s_in, Q, O, U, D, S,
+    tq, to, tu, td, aq, ao, au, ad, ssem, rsem, lsem,
+):
+    w, n, z, x, y, c, links = where_am_i()
+    mine, other = c, 1 - c
+    net = Net(ssem, rsem, links)
+    rw, cn = aq.shape[1], aq.shape[2]
+    rd, cu = ad.shape[0], au.shape[1]
+    half = cu // 2
+    enter(z, links)
+
+    first = [net.copy("p", src, dst, net.sends(1), net.recvs(1)) for src, dst in (
+        (q_in.at[other], tq), (o_in.at[other], to), (u_in.at[other], tu), (d_in.at[other], td),
+        (s_in, S.at[z, x, y, c]),
+    )]
+    for cp in first:
+        cp.start()
+    own_small = pltpu.make_async_copy(s_in, S.at[z, x, y, c], lsem.at[4])
+    own_small.start()
+
+    def join(own, got):
+        a, b = own.astype(F32), got.astype(F32)
+        lo, hi = jnp.where(c == 0, a, b), jnp.where(c == 0, b, a)
+        return jnp.concatenate([lo, hi], axis=-1).astype(BF)
+
+    outs = (
+        (au, U.at[mine, span(rw * w, rw), span(cu * y, cu)]),
+        (aq, Q.at[mine, :, span(rw * w, rw), span(cn * y, cn)]),
+        (ao, O.at[mine, span(rw * w, rw), span(cn * y, cn)]),
+        (ad, D.at[mine, span(rd * w, rd), span(cn * y, cn)]),
+    )
+    first[2].wait()
+    au[...] = join(u_in[mine], tu[...])
+    first[0].wait()
+    for j in range(3):
+        aq[j] = join(q_in[mine, j], tq[j])
+    first[1].wait()
+    ao[...] = join(o_in[mine], to[...])
+    first[3].wait()
+    ad[...] = join(d_in[mine], td[...])
+    first[4].wait()
+    own_small.wait()
+    local = [pltpu.make_async_copy(src, dst, lsem.at[k]) for k, (src, dst) in enumerate(outs)]
+    for cp in local:
+        cp.start()
+    for cp in local:
+        cp.wait()
+
+    def rows_a(zp):
+        return span(2 * rw * zp, 2 * rw)
+
+    def reg_a(zp, yp, layer):
+        return [Q.at[layer, :, rows_a(zp), span(cn * yp, cn)], O.at[layer, rows_a(zp), span(cn * yp, cn)]]
+
+    def blk_a(wp, yp, layer):
+        rows = span(rw * wp, rw)
+        return [Q.at[layer, :, rows, span(cn * yp, cn)], O.at[layer, rows, span(cn * yp, cn)]]
+
+    def reg_d(zp, xp, layer):
+        return [D.at[layer, span(rd * (2 * zp + xp), rd), :]]
+
+    def blk_d(wp, yp, layer):
+        return [D.at[layer, span(rd * wp, rd), span(cn * yp, cn)]]
+
+    def blk_u(zp, xp, yp, layer):
+        return [U.at[layer, span(rw * (2 * zp + xp), rw), span(cu * yp, cu)]]
+
+    def blk_u1(zp, xp, yp, layer):
+        return [U.at[layer, span(rw * (2 * zp + xp), rw), span(cu * yp, half)]]
+
+    def blk_u2(zp, xp, yp, layer):
+        return [U.at[layer, span(rw * (2 * zp + xp), rw), span(cu * yp + half, half)]]
+
+    def pair_u1(zp, yp, layer):
+        return [U.at[layer, rows_a(zp), span(cu * yp, half)]]
+
+    def pair_u2(zp, xp, layer):
+        return blk_u2(zp, xp, 0, layer) + blk_u2(zp, xp, 1, layer)
+
+    class Lane:
+        def __init__(self, link, sent, got, parts):
+            self.link, self.sent, self.got, self.parts = link, sent, got, parts
+            self.s = [net.sends(ZN) for _ in range(parts)]
+            self.r = [net.recvs(ZN) for _ in range(parts)]
+
+        def send(self, zp):
+            for k, ref in enumerate(self.sent(zp)):
+                net.copy(self.link, ref, ref, self.s[k] + zp, self.r[k] + zp).start()
+
+        def recv(self, zp):
+            for k, ref in enumerate(self.got(zp)):
+                net.copy(self.link, ref, ref, self.s[k] + zp, self.r[k] + zp).wait_recv()
+
+        def drain(self, zp):
+            for k, ref in enumerate(self.sent(zp)):
+                net.copy(self.link, ref, ref, self.s[k] + zp, self.r[k] + zp).wait_send()
+
+    class Line:
+        def __init__(self, region, parts):
+            self.region, self.parts = region, parts
+            self.su = [net.sends(ZN) for _ in range(parts)]
+            self.sd = [net.sends(ZN) for _ in range(parts)]
+            self.r = [net.recvs(ZN) for _ in range(parts)]
+
+        def each(self, link, sems, zp, what):
+            for k, ref in enumerate(self.region(zp)):
+                getattr(net.copy(link, ref, ref, sems[k] + zp, self.r[k] + zp), what)()
+
+        def own(self, what="start"):
+            @pl.when(z < ZN - 1)
+            def _():
+                self.each("up", self.su, z, what)
+
+            @pl.when(z > 0)
+            def _():
+                self.each("down", self.sd, z, what)
+
+        def relay(self, t, what="start"):
+            @pl.when(jnp.minimum(z - t, ZN - 2 - z) >= 0)
+            def _():
+                self.each("up", self.su, z - t, what)
+
+            @pl.when(jnp.minimum(ZN - 1 - t - z, z - 1) >= 0)
+            def _():
+                self.each("down", self.sd, z + t, what)
+
+        def recv(self, zp):
+            self.each("up", self.su, zp, "wait_recv")
+
+    line_a = Line(lambda zp: reg_a(zp, y, mine), 2)
+    line_d = Line(lambda zp: reg_d(zp, x, mine), 1)
+    line_u = Line(lambda zp: blk_u(zp, x, y, mine), 1)
+    x1 = Lane("x", lambda zp: blk_a(w, y, mine), lambda zp: blk_a(w + 1 - 2 * x, y, mine), 2)
+    y1 = Lane("y", lambda zp: blk_d(w, y, mine), lambda zp: blk_d(w, 1 - y, mine), 1)
+    x_u1 = Lane("x", lambda zp: blk_u1(zp, x, y, mine), lambda zp: blk_u1(zp, 1 - x, y, mine), 1)
+    y_u2 = Lane("y", lambda zp: blk_u2(zp, x, y, mine), lambda zp: blk_u2(zp, x, 1 - y, mine), 1)
+    y_a = Lane("y", lambda zp: reg_a(zp, y, mine), lambda zp: reg_a(zp, 1 - y, mine), 2)
+    x_d = Lane("x", lambda zp: reg_d(zp, x, mine), lambda zp: reg_d(zp, 1 - x, mine), 1)
+    y_u1 = Lane("y", lambda zp: pair_u1(zp, y, mine), lambda zp: pair_u1(zp, 1 - y, mine), 1)
+    x_u2 = Lane("x", lambda zp: pair_u2(zp, x, mine), lambda zp: pair_u2(zp, 1 - x, mine), 2)
+
+    def to_partner(make, parts):
+        return Lane("p", lambda zp: make(zp, mine), lambda zp: make(zp, other), parts)
+
+    p_a = to_partner(lambda zp, l: reg_a(zp, y, l), 2)
+    p_a2 = to_partner(lambda zp, l: reg_a(zp, 1 - y, l), 2)
+    p_d = to_partner(lambda zp, l: reg_d(zp, x, l), 1)
+    p_d2 = to_partner(lambda zp, l: reg_d(zp, 1 - x, l), 1)
+    p_u1 = to_partner(lambda zp, l: pair_u1(zp, y, l), 1)
+    p_u1b = to_partner(lambda zp, l: pair_u1(zp, 1 - y, l), 1)
+    p_u2 = to_partner(lambda zp, l: pair_u2(zp, x, l), 2)
+    p_u2b = to_partner(lambda zp, l: pair_u2(zp, 1 - x, l), 2)
+
+    small_x = Lane("x", lambda zp: [S.at[z, x, y]], lambda zp: [S.at[z, 1 - x, y]], 1)
+    small_y = Lane("y", lambda zp: [S.at[z, :, y]], lambda zp: [S.at[z, :, 1 - y]], 1)
+    line_s = Line(lambda zp: [S.at[zp]], 1)
+
+    line_u.own()
+    x1.send(0)
+    y1.send(0)
+    small_x.send(0)
+    x_u1.send(z)
+    y_u2.send(z)
+    small_x.recv(0)
+    small_y.send(0)
+    x1.recv(0)
+    line_a.own()
+    y_a.send(z)
+    p_a.send(z)
+    y1.recv(0)
+    line_d.own()
+    x_d.send(z)
+    p_d.send(z)
+    small_y.recv(0)
+    line_s.own()
+
+    def second(zp):
+        x_u1.recv(zp)
+        y_u1.send(zp)
+        p_u1.send(zp)
+        y_u2.recv(zp)
+        x_u2.send(zp)
+        p_u2.send(zp)
+
+    def third(zp):
+        y_a.recv(zp)
+        p_a2.send(zp)
+        x_d.recv(zp)
+        p_d2.send(zp)
+        y_u1.recv(zp)
+        p_u1b.send(zp)
+        x_u2.recv(zp)
+        p_u2b.send(zp)
+
+    def both_ways(t, make):
+        @pl.when(z >= t)
+        def _():
+            make(z - t)
+
+        @pl.when(z < ZN - t)
+        def _():
+            make(z + t)
+
+    def take(line, t, *lanes):
+        both_ways(t, line.recv)
+        line.relay(t)
+        for lane in lanes:
+            both_ways(t, lane.send)
+
+    second(z)
+    for t in range(1, ZN):
+        take(line_u, t, x_u1, y_u2)
+        take(line_a, t, y_a, p_a)
+        if t == 1:
+            third(z)
+        else:
+            both_ways(t - 1, third)
+        take(line_d, t, x_d, p_d)
+        both_ways(t, second)
+        take(line_s, t)
+    both_ways(ZN - 1, third)
+
+    partner = (p_a, p_a2, p_d, p_d2, p_u1, p_u1b, p_u2, p_u2b)
+    for zp in range(ZN):
+        for lane in partner:
+            lane.recv(zp)
+    for zp in range(ZN):
+        for lane in partner + (x_u1, y_u2, y_a, x_d, y_u1, x_u2):
+            lane.drain(zp)
+    for lane in (x1, y1, small_x, small_y):
+        lane.drain(0)
+    for line in (line_u, line_a, line_d, line_s):
+        line.own("wait_send")
+        for t in range(1, ZN):
+            line.relay(t, "wait_send")
+    assert net.next_send <= ssem.shape[0] and net.next_recv <= rsem.shape[0]
+
+
+def gather_fast(pieces):
+    wqkv, wo, wup, wdn, bias, ubias, norm = pieces
+    _, _, rw, cn = wqkv.shape
+    rd, cu = wdn.shape[1], wup.shape[2]
+    d, ff = rw * 8, rd * 8
+    small = jnp.concatenate([bias[:, 0], norm[:, 0], ubias, jnp.zeros_like(ubias)], axis=0).astype(F32)
+    small = jnp.pad(small, ((0, 0), (0, 128 - rw)))
+    hbm = pl.BlockSpec(memory_space=pl.ANY)
+    vmem = pl.BlockSpec(memory_space=pltpu.VMEM)
+    Q, O, U, D, S = pl.pallas_call(
+        gather_kernel,
+        in_specs=[vmem] * 5,
+        out_specs=[hbm] * 5,
+        out_shape=[
+            jax.ShapeDtypeStruct((LAYERS, 3, d, d), BF),
+            jax.ShapeDtypeStruct((LAYERS, d, d), BF),
+            jax.ShapeDtypeStruct((LAYERS, d, ff), BF),
+            jax.ShapeDtypeStruct((LAYERS, ff, d), BF),
+            jax.ShapeDtypeStruct((ZN, 2, 2, 2, 8, 128), F32),
+        ],
+        scratch_shapes=[
+            pltpu.VMEM((3, rw, cn), BF), pltpu.VMEM((rw, cn), BF), pltpu.VMEM((rw, cu), BF), pltpu.VMEM((rd, cn), BF),
+            pltpu.VMEM((3, rw, 2 * cn), BF), pltpu.VMEM((rw, 2 * cn), BF),
+            pltpu.VMEM((rw, 2 * cu), BF), pltpu.VMEM((rd, 2 * cn), BF),
+            pltpu.SemaphoreType.DMA((160,)), pltpu.SemaphoreType.DMA((160,)), pltpu.SemaphoreType.DMA((5,)),
+        ],
+        compiler_params=pltpu.CompilerParams(collective_id=1, has_side_effects=True),
+        name="weight_gather",
+    )(wqkv, wo, wup, wdn, small)
+    S = S.reshape(8, 4, 8, 128)[..., :rw]
+    rows = jnp.transpose(S, (2, 1, 0, 3)).reshape(8, 4, d)
+    ub = jnp.transpose(S[:, :, 4:6], (2, 0, 1, 3)).reshape(2, ff)
+    return Q, O, U, D, rows[0:2], ub, rows[2:4]
 
 
 def gather_weights(pieces):
@@ -395,6 +728,7 @@
 
 def scatter_grads(big, small):
     gq, go, gup, gdn = big
+    gq = jnp.moveaxis(gq.reshape(gq.shape[:2] + (3, -1)), 2, 1)
     gb, gub, gn = small
     big = (scatter_two(gq, 2, 3), scatter_two(go, 1, 2), scatter_two(gup, 1, 2), scatter_two(gdn, 1, 2))
     gub = lax.psum_scatter(gub, ("wide", "narrow"), scatter_dimension=1, tiled=True)
@@ -408,13 +742,14 @@
 
 
 def shards(
-    text_in, memory_in, counts, last_len, cot_text, cot_memory,
+    near, text_in, memory_in, counts, last_len, cot_text, cot_memory,
     qkv_weight, out_weight, up_weight, down_weight, biases, up_bias, norm_params,
 ):
     text, cot = text_in[:, 0], cot_text[:, 0]
     mem, cot_mem = memory_in[:, 0], cot_memory[:, 0]
     cnt, lens = counts[:, 0], last_len[:, 0]
-    weights = gather_weights((qkv_weight, out_weight, up_weight, down_weight, biases, up_bias, norm_params))
+    gather = gather_fast if near else gather_weights
+    weights = gather((qkv_weight, out_weight, up_weight, down_weight, biases, up_bias, norm_params))
     text_out, mem_out, kept = forward_local(text, mem, cnt, lens, weights)
     text_grad, mem_grad, grads, small = backward_local(cot, cot_mem, cnt, lens, kept, weights)
     grads = scatter_grads(weight_grads(kept, grads), small)
@@ -429,8 +764,9 @@
     split = P(None, "wide", "narrow")
     small = P(None, "narrow", "wide")
     params = (P(None, None, "wide", "narrow"), split, split, split, small, ids, small)
+    near = (mesh.shape["wide"], mesh.shape["narrow"]) == (2 * ZN, 4)
     return jax.shard_map(
-        shards,
+        functools.partial(shards, near),
         mesh=mesh,
         in_specs=(act5, act4, ids, ids, act5, act4) + params,
         out_specs=(act5, act4, act5, act4) + params,

time: 2150 us -> 1190 us (0.55)
  local copies, waits for them, and re-layouts: 1050 us -> 68.4 us
  blocking collectives: 152 us -> 14.3 us
  Pallas kernels: 181 us -> 314 us
  waiting for transfers between devices: 647 us -> 711 us
  other arithmetic: 39.9 us -> 11.6 us
    unnamed x78 -> x58, local copies, waits for them, and re-layouts: 986 us -> 53.2 us
    all_gather x6 -> x0, waiting for transfers between devices: 330 us -> none  [the longest x4 317 us: gather_weights(): lax.all_gather(w, 'wide', axis=k, tiled=True)]
    reduce_scatter x1 -> x2, waiting for transfers between devices: 37.7 us -> 196 us  [scatter_two(): lax.psum_scatter(low.astype(F32), 'wide', scatter_dimension=row_axis, til...]
    reduce_scatter x1 -> x4, waiting for transfers between devices: 0.02 us -> 152 us  [scatter_two(): lax.psum_scatter(grad.astype(BF), 'narrow', scatter_dimension=col_axis, t...]
    all_gather x7 -> x0, blocking collectives: 140 us -> none  [the longest x2 66.2 us: gather_weights(): lax.all_gather(w, 'wide', axis=k, tiled=True)]
    pallas_call x0 -> x1, Pallas kernels: none -> 133 us  [gather_fast(): pl.pallas_call(gather_kernel, in_specs=[vmem] * 5, out_specs=[hbm] * 5, o...]
    unnamed x22 -> x16, waiting for transfers between devices: 280 us -> 363 us
    another operation x3 -> x1, local copies, waits for them, and re-layouts: 46.8 us -> 0.72 us  [forward_local(): ubias.astype(F32)[:, None, :]]
  transfers between devices with their start and end apart: 15 -> 11, of which waited for: 7 -> 10; matrix products, arithmetic and copies ran while one was open for 49% -> 9% of each run, Pallas kernels for 0% -> 0%
where the time goes in v2:
time: 1190 us
  waiting for transfers between devices  711 us (60%)
  Pallas kernels  314 us (26%)
  local copies, waits for them, and re-layouts  68.4 us (6%)
  matrix products  55.1 us (5%)
  blocking collectives  14.3 us (1%)
  between operations  14.1 us (1%)
    unnamed x16, waiting for transfers between devices  363 us
    reduce_scatter x2, waiting for transfers between devices, scatter_two(): lax.psum_scatter(low.astype(F32), 'wide', scatter_dimension=row_axis, til...  196 us
    reduce_scatter x4, waiting for transfers between devices, scatter_two(): lax.psum_scatter(grad.astype(BF), 'narrow', scatter_dimension=col_axis, t...  152 us
    pallas_call x1, Pallas kernels, gather_fast(): pl.pallas_call(gather_kernel, in_specs=[vmem] * 5, out_specs=[hbm] * 5, o...  133 us
    pallas_call x1, Pallas kernels, backward_local(): pl.pallas_call(bwd_kernel, grid=(SEGS, LAYERS), in_specs=[smem, smem, pl....  103 us
    pallas_call x1, Pallas kernels, forward_local(): pl.pallas_call(fwd_kernel, grid=(SEGS, LAYERS), in_specs=[smem, smem, pl....  78.3 us
    dot_general x4, matrix products, product(): lax.dot_general(lhs, rhs, dims, preferred_element_type=F32).astype(BF)  55.1 us
    unnamed x58, local copies, waits for them, and re-layouts  53.2 us
  transfers between devices with their start and end apart: 11, of which 10 were waited for; matrix products, arithmetic and copies ran while one was open for 9% of the time, Pallas kernels for 0%

profile of v2, /device:TPU:0, one launch (start us, length us, event | category | flops | bytes accessed | tf_op | source)
XLA Modules:
  0.0 1189.0 jit_solution(17747676367033862887)
XLA Ops:
  7.3 2.7 copy.328
  9.9 0.8 bitcast_convert_fusion
  10.7 1.9 copy.81.d_in
  13.3 132.9 %weight_gather.1 = (bf16[2,3,768,768]{3,2,1,0:T(8,128)(2,1)}, bf16[2,768,768]{2,1,0:T(8,128)(2,1)}, bf16[2,768,3072]{2,1,0:T(8,128)(2,1)}, bf16[2,3072,768]{2,1,0:T(8,128)(2,1)}, f32[4,2,2,2,8,128]{5,4,3,2,1,0:T(8,128)}) custom-call(bf16[2,3,96,192]{3,2,1,0:T(8,128)(2,1)} %q_in.1, bf16[2,96,192]{2,1,0:T(8,128)(2,1)} %o_in.1, bf16[2,96,768]{2,1,0:T(8,128)(2,1)} %u_in.1, ...), custom_call_target="tpu_custom_call" | custom-call | tf_op jit(solution)/shard_map/weight_gather/pallas_call | solution.py:688
  146.3 0.9 slice.37
  147.2 1.0 copy.329
  150.3 1.3 copy.327
  153.0 78.3 %rmt_forward.1 = (bf16[2,4,108,768]{3,2,1,0:T(8,128)(2,1)}, f32[2,24,768]{2,1,0:T(8,128)}, bf16[2,1024,768]{2,1,0:T(8,128)(2,1)}, bf16[2,1024,2304]{2,1,0:T(8,12...) custom-call(s32[2]{0:T(128)} %bitcast.272, ...), custom_call_target="tpu_custom_call" | custom-call | tf_op jit(solution)/shard_map/rmt_forward/pallas_call | solution.py:165
  231.3 102.7 %rmt_backward.1 = (bf16[2,4,108,768]{3,2,1,0:T(8,128)(2,1)}, f32[2,24,768]{2,1,0:T(8,128)}, bf16[2,1024,2304]{2,1,0:T(8,128)(2,1)}, bf16[2,1024,768]{2,1,0:T(8,1...) custom-call(s32[2]{0:T(128)} %bitcast.273, ...), custom_call_target="tpu_custom_call" | custom-call | tf_op jit(solution)/shard_map/rmt_backward/pallas_call | solution.py:325
  334.0 7.1 convolution_convert_fusion.3
  341.2 13.4 %convolution_convert_fusion = bf16[2,768,2304]{2,1,0:T(8,128)(2,1)} fusion(bf16[2,1024,768]{2,1,0:T(8,128)(2,1)S(1)} %copy-done.12, bf16[2,1024,2304]{2,1,0:T(8,128)(2,1)} %get-tuple-element.53), kind=kOutput, calls=%fused_computation | convolution fusion | flops 7251296256 | bytes 19660800 | tf_op jit(solution)/shard_map/dot_general | solution.py:373
  354.6 10.3 copy.87
  365.0 1.8 copy-done.11
  366.8 17.0 %convolution_convert_fusion.2 = bf16[2,768,3072]{2,1,0:T(8,128)(2,1)} fusion(bf16[2,1024,768]{2,1,0:T(8,128)(2,1)S(1)} %copy-done.11, bf16[2,1024,3072]{2,1,0:T(8,128)(2,1)} %get-tuple-element.57), kind=kOutput, calls=%fused_computation.2 | convolution fusion | flops 9668395008 | bytes 25165824 | tf_op jit(solution)/shard_map/dot_general | solution.py:373
  383.9 1.8 copy-done.10
  385.8 17.6 %convolution_convert_fusion.1 = bf16[2,3072,768]{1,2,0:T(8,128)(2,1)} fusion(bf16[2,1024,3072]{2,1,0:T(8,128)(2,1)} %get-tuple-element.58, bf16[2,1024,768]{2,1,0:T(8,128)(2,1)S(1)} %copy-done.10), kind=kOutput, calls=%fused_computation.1 | convolution fusion | flops 9668395008 | bytes 25165824 | tf_op jit(solution)/shard_map/dot_general | solution.py:373
  403.5 0.8 copy-done.5
  405.1 14.3 %all-reduce.4 = (f32[2,4,768]{2,0,1:T(2,128)S(1)}, f32[2,4,768]{2,0,1:T(2,128)S(1)}) all-reduce(f32[2,4,768]{2,0,1:T(2,128)S(1)} %copy.91, f32[2,4,768]{2,0,1:T(2,128)S(1)} %copy.93), channel_id=10, replica_groups=mesh['wide'=8,'narrow'=4] {'narrow'}, use_global_device_ids=true, to_apply=%region_9.10.clone | all-reduce | flops 12288 | bytes 98304
  420.5 1.6 bitcast_reduce_fusion.1
  422.7 1.6 bitcast_reduce_fusion
  424.5 1.7 copy.111
  426.3 2.5 copy.107
  428.8 2.3 reshape.40
  431.2 9.9 reduce-scatter.22.cloned.1.call-done
  441.0 6.3 copy.105
  447.3 8.5 reshape.38
  455.9 65.6 %reduce-scatter.26.cloned.1.call-done = bf16[2,768,768]{2,1,0:T(8,128)(2,1)} async-done(((bf16[2,768,3072]{2,1,0:T(8,128)(2,1)}), bf16[2,768,768]{2,1,0:T(8,128)(2,1)}) %reduce-scatter.26.cloned.1.call-update) | async-done | bytes 2359312 | tf_op jit(solution)/shard_map/reduce_scatter | solution.py:725
  521.4 4.1 convert_element_type.48
  525.6 76.2 %reduce-scatter.30.cloned.1.call-done = bf16[2,3072,192]{1,2,0:T(8,128)(2,1)} async-done(((bf16[2,3072,768]{1,2,0:T(8,128)(2,1)}), bf16[2,3072,192]{1,2,0:T(8,128)(2,1)}) %reduce-scatter.30.cloned.1.call-update) | async-done | bytes 2359312 | tf_op jit(solution)/shard_map/reduce_scatter | solution.py:725
  601.9 4.4 convert_element_type.50
  606.3 1.3 copy-done
  607.6 1.7 copy.95
  609.3 0.9 fusion
  610.9 1.7 copy.97
  612.6 0.9 fusion.1
  614.2 53.5 %reduce-scatter.38.cloned.1.call-done = f32[96,2]{1,0:T(8,128)} async-done(((f32[768,2]{1,0:T(8,128)}), f32[96,2]{1,0:T(8,128)}) %reduce-scatter.38.cloned.1.call-update) | async-done | bytes 784
  667.7 1.0 reshape_bitcast_fusion.1
  669.3 62.8 %reduce-scatter.42.cloned.1.call-done = f32[96,2]{1,0:T(8,128)} async-done(((f32[768,2]{1,0:T(8,128)}), f32[96,2]{1,0:T(8,128)}) %reduce-scatter.42.cloned.1.call-update) | async-done | bytes 784
  732.1 1.0 reshape_bitcast_fusion
  733.7 100.6 %reduce-scatter.40.cloned.1.call-done = f32[96,2]{1,0:T(8,128)} async-done(((f32[3072,2]{1,0:T(8,128)}), f32[96,2]{1,0:T(8,128)}) %reduce-scatter.40.cloned.1.call-update) | async-done | bytes 784
  834.3 1.4 copy.112
  835.7 65.7 %reduce-scatter.36.cloned.1.call-done = f32[96,384]{1,0:T(8,128)} async-done(((f32[768,384]{1,0:T(8,128)}), f32[96,384]{1,0:T(8,128)}) %reduce-scatter.36.cloned.1.call-update) | async-done | bytes 147472
  901.4 1.1 reshape.41
  903.2 80.3 %reduce-scatter.34.cloned.1.call-done = f32[96,1152]{1,0:T(8,128)} async-done(((f32[768,1152]{1,0:T(8,128)}), f32[96,1152]{1,0:T(8,128)}) %reduce-scatter.34.cloned.1.call-update) | async-done | bytes 442384
  983.5 1.6 reshape.39
  985.1 1.0 copy.99
  986.1 96.8 %reduce-scatter.28.cloned.1.call-done = f32[2,96,768]{2,1,0:T(8,128)} async-done(((f32[2,768,768]{2,1,0:T(8,128)}), f32[2,96,768]{2,1,0:T(8,128)}) %reduce-scatter.28.cloned.1.call-update) | async-done | bytes 589840 | tf_op jit(solution)/shard_map/reduce_scatter | solution.py:726
  1082.9 99.6 %reduce-scatter.32.cloned.1.call-done = f32[2,384,192]{1,2,0:T(8,128)} async-done(((f32[2,3072,192]{1,2,0:T(8,128)}), f32[2,384,192]{1,2,0:T(8,128)}) %reduce-scatter.32.cloned.1.call-update) | async-done | bytes 589840 | tf_op jit(solution)/shard_map/reduce_scatter | solution.py:726
  (75 shorter events, 10.7 us)
Async XLA Ops:
  7.2 5.5 copy-start.7
  7.2 5.5 copy-start.8
  7.2 5.5 copy-start.9
  7.2 143.1 %copy-start.2 = (bf16[2,1,4,108,768]{4,2,3,1,0:T(4,128)(2,1)S(1)}, bf16[2,1,4,108,768]{4,2,3,1,0:T(4,128)(2,1)}, u32[]{:S(2)}) copy-start(bf16[2,1,4,108,768]{4,2,3,1,0:T(4,128)(2,1)} %param.17) | copy-start | bytes 3981316
  7.2 419.1 %reduce-scatter.24.cloned.1.call-start = ((), (), s32[]{:S(2)}) async-start(), calls=%async_computation.12 | async-start | bytes 2949120 | tf_op jit(solution)/shard_map/reduce_scatter | solution.py:725
  9.9 141.7 %copy-start.6 = (bf16[2,1,10,768]{3,0,2,1:T(2,128)(2,1)S(1)}, bf16[2,1,10,768]{3,0,2,1:T(2,128)(2,1)}, u32[]{:S(2)}) copy-start(bf16[2,1,10,768]{3,0,2,1:T(2,128)(2,1)} %param.18) | copy-start | bytes 92164
  334.0 7.2 copy-start.12
  341.2 99.8 %reduce-scatter.22.cloned.1.call-start = ((), (), s32[]{:S(2)}) async-start(), calls=%async_computation.11 | async-start | bytes 8847360 | tf_op jit(solution)/shard_map/reduce_scatter | solution.py:725
  364.9 1.9 copy-start.11
  364.9 156.5 %reduce-scatter.26.cloned.1.call-start = ((), (), s32[]{:S(2)}) async-start(), calls=%async_computation.13 | async-start | bytes 11796480 | tf_op jit(solution)/shard_map/reduce_scatter | solution.py:725
  383.9 1.9 copy-start.10
  383.9 218.0 %reduce-scatter.30.cloned.1.call-start = ((), (), s32[]{:S(2)}) async-start(), calls=%async_computation.15 | async-start | bytes 11796480 | tf_op jit(solution)/shard_map/reduce_scatter | solution.py:725
  403.4 0.9 copy-start.5
  403.4 1.0 copy-start.4
  403.4 1.1 copy-start.13
  403.4 21.0 %copy-start.3 = (f32[2,8,3072]{2,1,0:T(8,128)S(1)}, f32[2,8,3072]{2,1,0:T(8,128)}, u32[]{:S(2)}) copy-start(f32[2,8,3072]{2,1,0:T(8,128)} %get-tuple-element.61) | copy-start | bytes 589828
  403.4 264.3 %reduce-scatter.38.cloned.1.call-start = ((), (), s32[]{:S(2)}) async-start(), calls=%async_computation.19 | async-start | bytes 442368
  422.2 309.9 %reduce-scatter.42.cloned.1.call-start = ((), (), s32[]{:S(2)}) async-start(), calls=%async_computation.21 | async-start | bytes 442368
  424.4 409.9 %reduce-scatter.40.cloned.1.call-start = ((), (), s32[]{:S(2)}) async-start(), calls=%async_computation.20 | async-start | bytes 1622016
  426.2 475.2 %reduce-scatter.36.cloned.1.call-start = ((), (), s32[]{:S(2)}) async-start(), calls=%async_computation.18 | async-start | bytes 1327104
  431.1 552.4 %reduce-scatter.34.cloned.1.call-start = ((), (), s32[]{:S(2)}) async-start(), calls=%async_computation.17 | async-start | bytes 3981312
  455.8 627.1 %reduce-scatter.28.cloned.1.call-start = ((), (), s32[]{:S(2)}) async-start(), calls=%async_computation.14 | async-start | bytes 5308416 | tf_op jit(solution)/shard_map/reduce_scatter | solution.py:726
  525.6 656.9 %reduce-scatter.32.cloned.1.call-start = ((), (), s32[]{:S(2)}) async-start(), calls=%async_computation.16 | async-start | bytes 5308416 | tf_op jit(solution)/shard_map/reduce_scatter | solution.py:726
  606.3 1.3 copy-start
  606.3 4.6 copy-start.1
Sparse Core Ops, SparseCore 0:
  341.3 33.3 reduce-scatter.23
  377.2 63.7 reduce-scatter.21
  443.6 77.7 reduce-scatter.25
  523.9 77.9 reduce-scatter.29
  605.5 62.0 reduce-scatter.37
  670.8 61.2 reduce-scatter.41
  737.3 96.9 reduce-scatter.39
  837.7 63.7 reduce-scatter.35
  905.1 78.3 reduce-scatter.33
  987.6 95.2 reduce-scatter.27
  1087.1 95.3 reduce-scatter.31

commit v3 on v2

--- a/solution.py
+++ b/solution.py
@@ -711,6 +711,360 @@
     return Q, O, U, D, rows[0:2], ub, rows[2:4]
 
 
+def accumulate(dst, src, rows, step=48):
+    def body(i, carry):
+        r = pl.ds(pl.multiple_of(i * step, 16), step)
+        dst[r, :] = dst[r, :] + src[r, :]
+        return carry
+
+    lax.fori_loop(0, rows // step, body, 0)
+
+
+def scatter_kernel(
+    gq, go, gu, gd, sm_in, oq, oo, ou, od, sm_out,
+    AQ, AO, AU, AD, PQ, PO, PU, PD, FA, FO, FD, F1, F2, S1, S2, ZA, ZO, ZD, ZU, TA, TO, TD,
+    hq, ho, hu, hd, s_p, s_x, s_y, s_below, s_above, s_a, s_b, s_sum, s_up, s_down, ssem, rsem, lsem,
+):
+    w, n, z, x, y, c, links = where_am_i()
+    mine, other = c, 1 - c
+    net = Net(ssem, rsem, links)
+    d, ff = AO.shape[1], AU.shape[1]
+    rw, cn = d // 8, d // 2
+    rd, cu = ff // 8, ff // 2
+    half = cu // 2
+    enter(z, links)
+
+    class Hop:
+        def __init__(self, link, pairs, parts):
+            self.link, self.pairs = link, pairs
+            self.s = [net.sends(ZN) for _ in range(parts)]
+            self.r = [net.recvs(ZN) for _ in range(parts)]
+
+        def each(self, zp, what):
+            for k, (src, dst) in enumerate(self.pairs(zp)):
+                getattr(net.copy(self.link, src, dst, self.s[k] + zp, self.r[k] + zp), what)()
+
+        def send(self, zp):
+            self.each(zp, "start")
+
+        def recv(self, zp):
+            self.each(zp, "wait_recv")
+
+        def drain(self, zp):
+            self.each(zp, "wait_send")
+
+    def rows_a(zp):
+        return span(2 * rw * zp, 2 * rw)
+
+    def slab(zp, layer, q, o, u, dn):
+        rows = rows_a(zp)
+        down = span(2 * rd * zp, 2 * rd)
+        return [(gq.at[layer, rows, j * d : (j + 1) * d], q.at[j, rows, :]) for j in range(3)] + [
+            (go.at[layer, rows, :], o.at[rows, :]),
+            (gd.at[layer, down, :], dn.at[down, :]),
+            (gu.at[layer, rows, :], u.at[rows, :]),
+        ]
+
+    def own_loads(zp):
+        return [
+            pltpu.make_async_copy(src, dst, lsem.at[k * ZN + zp])
+            for k, (src, dst) in enumerate(slab(zp, mine, AQ, AO, AU, AD))
+        ]
+
+    swap = Hop("p", lambda zp: slab(zp, other, PQ, PO, PU, PD), 6)
+
+    def cols_a(yp):
+        return span(cn * yp, cn)
+
+    def rows_x(zp, xp):
+        return span(rw * (2 * zp + xp), rw)
+
+    def rows_d(zp, xp):
+        return span(rd * (2 * zp + xp), rd)
+
+    def reg_a(zp, yp):
+        return AQ.at[:, rows_a(zp), cols_a(yp)], AO.at[rows_a(zp), cols_a(yp)]
+
+    def reg_d(zp, xp):
+        return AD.at[rows_d(zp, xp), :]
+
+    def u1(zp, yp):
+        return AU.at[rows_a(zp), span(cu * yp, half)]
+
+    def u1_part(zp, xp, yp):
+        return AU.at[rows_x(zp, xp), span(cu * yp, half)]
+
+    def u2(zp, xp, yp):
+        return AU.at[rows_x(zp, xp), span(cu * yp + half, half)]
+
+    def blk_u(zp):
+        return AU.at[rows_x(zp, x), span(cu * y, cu)]
+
+    y_a = Hop("y", lambda zp: list(zip(reg_a(zp, 1 - y), (FA.at[zp], FO.at[zp]))), 2)
+    x_d = Hop("x", lambda zp: [(reg_d(zp, 1 - x), FD.at[zp])], 1)
+    y_u1 = Hop("y", lambda zp: [(u1(zp, 1 - y), F1.at[zp])], 1)
+    x_u2 = Hop("x", lambda zp: [(u2(zp, 1 - x, yp), F2.at[yp, zp]) for yp in range(2)], 2)
+    x_u1 = Hop("x", lambda zp: [(u1_part(zp, 1 - x, y), S1.at[zp])], 1)
+    y_u2 = Hop("y", lambda zp: [(u2(zp, x, 1 - y), S2.at[zp])], 1)
+    last_a = Hop("x", lambda zp: [
+        (AQ.at[:, rows_x(z, 1 - x), cols_a(y)], TA), (AO.at[rows_x(z, 1 - x), cols_a(y)], TO)
+    ], 2)
+    last_d = Hop("y", lambda zp: [(AD.at[rows_d(z, x), cols_a(1 - y)], TD)], 1)
+
+    class Line:
+        def __init__(self, region, bufs):
+            self.region, self.bufs = region, bufs
+            self.su = [net.sends(ZN) for _ in bufs]
+            self.sd = [net.sends(ZN) for _ in bufs]
+            self.r = [net.recvs(ZN + 1) for _ in bufs]
+
+        def up(self, zp, what):
+            slot = jnp.where(zp == z + 1, ZN, zp)
+
+            @pl.when(zp > z)
+            def _():
+                for k, (src, buf) in enumerate(zip(self.region(zp), self.bufs)):
+                    getattr(net.copy("up", src, buf.at[slot], self.su[k] + zp, self.r[k] + slot), what)()
+
+        def down(self, zp, what):
+            @pl.when(zp < z)
+            def _():
+                for k, (src, buf) in enumerate(zip(self.region(zp), self.bufs)):
+                    getattr(net.copy("down", src, buf.at[zp], self.sd[k] + zp, self.r[k] + zp), what)()
+
+        def take(self, zp, slot):
+            for k, (dst, buf) in enumerate(zip(self.region(zp), self.bufs)):
+                net.copy("up", dst, buf.at[slot], self.su[k] + zp, self.r[k] + slot).wait_recv()
+                self.add(dst, buf.at[slot])
+
+        def add(self, dst, src):
+            if len(src.shape) == 3:
+                for j in range(src.shape[0]):
+                    accumulate(dst.at[j], src.at[j], src.shape[1])
+            else:
+                accumulate(dst, src, src.shape[0])
+
+        def go(self, zp):
+            @pl.when(jnp.minimum(z - zp, ZN - 2 - z) >= 0)
+            def _():
+                self.take(zp, zp)
+
+            @pl.when(jnp.minimum(zp - z, z - 1) >= 0)
+            def _():
+                self.take(zp, jnp.where(zp == z, ZN, zp))
+
+            self.up(zp, "start")
+            self.down(zp, "start")
+
+        def drain(self, zp):
+            self.up(zp, "wait_send")
+            self.down(zp, "wait_send")
+
+    line_a = Line(lambda zp: reg_a(zp, y), (ZA, ZO))
+    line_d = Line(lambda zp: (reg_d(zp, x),), (ZD,))
+    line_u = Line(lambda zp: (blk_u(zp),), (ZU,))
+
+    table = ((3, 3, 0, 0), (2, 0, 3, 1), (1, 2, 1, 2), (0, 1, 2, 3))
+    order = [jnp.where(z == 0, t[0], jnp.where(z == 1, t[1], jnp.where(z == 2, t[2], t[3]))) for t in table]
+
+    small = [
+        net.copy(link, src, dst, net.sends(1), net.recvs(1))
+        for link, src, dst in (("p", sm_in, s_p), ("x", s_a, s_x), ("y", s_b, s_y))
+    ]
+    small_up = net.copy("up", s_up, s_below, net.sends(1), net.recvs(1))
+    small_down = net.copy("down", s_down, s_above, net.sends(1), net.recvs(1))
+
+    small[0].start()
+    for zp in order:
+        for cp in own_loads(zp):
+            cp.start()
+        swap.send(zp)
+
+    def open_slab(zp):
+        for cp in own_loads(zp):
+            cp.wait()
+        swap.recv(zp)
+        rows = rows_a(zp)
+        for j in range(3):
+            accumulate(AQ.at[j, rows, :], PQ.at[j, rows, :], 2 * rw)
+        accumulate(AO.at[rows, :], PO.at[rows, :], 2 * rw)
+        y_a.send(zp)
+        down = span(2 * rd * zp, 2 * rd)
+        accumulate(AD.at[down, :], PD.at[down, :], 2 * rd)
+        x_d.send(zp)
+        accumulate(AU.at[rows, :], PU.at[rows, :], 2 * rw, 16)
+        y_u1.send(zp)
+        x_u2.send(zp)
+
+    def middle(zp):
+        y_a.recv(zp)
+        qa, oa = reg_a(zp, y)
+        for j in range(3):
+            accumulate(qa.at[j], FA.at[zp, j], 2 * rw)
+        accumulate(oa, FO.at[zp], 2 * rw)
+        line_a.go(zp)
+        x_d.recv(zp)
+        accumulate(reg_d(zp, x), FD.at[zp], rd)
+        line_d.go(zp)
+        y_u1.recv(zp)
+        accumulate(u1(zp, y), F1.at[zp], 2 * rw)
+        x_u1.send(zp)
+        x_u2.recv(zp)
+        for yp in range(2):
+            accumulate(u2(zp, x, yp), F2.at[yp, zp], rw)
+        y_u2.send(zp)
+
+    def close(zp):
+        x_u1.recv(zp)
+        accumulate(u1_part(zp, x, y), S1.at[zp], rw)
+        y_u2.recv(zp)
+        accumulate(u2(zp, x, y), S2.at[zp], rw)
+        line_u.go(zp)
+
+    open_slab(order[0])
+    small[0].wait()
+    s_a[...] = sm_in[...] + s_p[...]
+    small[1].start()
+    open_slab(order[1])
+    middle(order[0])
+    small[1].wait()
+    s_b[...] = s_a[...] + s_x[...]
+    small[2].start()
+    open_slab(order[2])
+    close(order[0])
+    middle(order[1])
+    small[2].wait()
+    s_sum[...] = s_b[...] + s_y[...]
+    open_slab(order[3])
+    close(order[1])
+    middle(order[2])
+
+    @pl.when(z > 0)
+    def _():
+        small_up.wait_recv()
+
+    @pl.when(z == 0)
+    def _():
+        s_below[...] = jnp.zeros_like(s_below)
+
+    @pl.when(z < ZN - 1)
+    def _():
+        s_up[...] = s_sum[...] + s_below[...]
+        small_up.start()
+
+    close(order[2])
+    middle(order[3])
+    last_a.send(0)
+    last_d.send(0)
+
+    @pl.when(z < ZN - 1)
+    def _():
+        small_down.wait_recv()
+
+    @pl.when(z == ZN - 1)
+    def _():
+        s_above[...] = jnp.zeros_like(s_above)
+
+    @pl.when(z > 0)
+    def _():
+        s_down[...] = s_sum[...] + s_above[...]
+        small_down.start()
+
+    sm_out[...] = s_sum[...] + s_below[...] + s_above[...]
+    close(order[3])
+
+    def pick(v, k):
+        lo, hi = v[..., :k], v[..., k:]
+        return jnp.where(c == 0, lo, hi), jnp.where(c == 0, hi, lo)
+
+    out = [
+        net.copy("p", src, dst.at[mine], net.sends(1), net.recvs(1))
+        for src, dst in ((hu, ou), (hq, oq), (ho, oo), (hd, od))
+    ]
+    rows = rows_x(z, x)
+    ou[mine] = AU[rows, span(cu * y + half * c, half)].astype(F32)
+    hu[...] = AU[rows, span(cu * y + half * (1 - c), half)].astype(F32)
+    out[0].start()
+    last_a.recv(0)
+    for j in range(3):
+        keep, give = pick(AQ[j, rows, cols_a(y)].astype(F32) + TA[j].astype(F32), cn // 2)
+        oq[mine, j] = keep
+        hq[j] = give
+    out[1].start()
+    keep, give = pick(AO[rows, cols_a(y)].astype(F32) + TO[...].astype(F32), cn // 2)
+    oo[mine] = keep
+    ho[...] = give
+    out[2].start()
+    last_d.recv(0)
+    for k in range(rd // rw):
+        part = pl.ds(k * rw, rw)
+        here = span(rd * w + k * rw, rw)
+        keep, give = pick(AD[here, cols_a(y)].astype(F32) + TD[part, :].astype(F32), cn // 2)
+        od[mine, part, :] = keep
+        hd[part, :] = give
+    out[3].start()
+
+    for zp in range(ZN):
+        for hop in (swap, y_a, x_d, y_u1, x_u2, x_u1, y_u2):
+            hop.drain(zp)
+        for line in (line_a, line_d, line_u):
+            line.drain(zp)
+    last_a.drain(0)
+    last_d.drain(0)
+
+    @pl.when(z < ZN - 1)
+    def _():
+        small_up.wait_send()
+
+    @pl.when(z > 0)
+    def _():
+        small_down.wait_send()
+
+    for cp in out:
+        cp.wait()
+    assert net.next_send <= ssem.shape[0] and net.next_recv <= rsem.shape[0]
+
+
+def scatter_fast(big, small):
+    gq, go, gup, gdn = big
+    gb, gub, gn = small
+    d, ff = gup.shape[1:]
+    rw, cn, rd, cu = d // 8, d // 2, ff // 8, ff // 2
+    pack = jnp.concatenate([gb.reshape(-1, d), gub.reshape(-1, d), gn.reshape(-1, d)], axis=0)
+    hbm = pl.BlockSpec(memory_space=pl.ANY)
+    vmem = pl.BlockSpec(memory_space=pltpu.VMEM)
+
+    def buf(*shape):
+        return pltpu.VMEM(shape, BF)
+
+    def wide(*shape):
+        return pltpu.VMEM(shape, F32)
+
+    outs = [(3, rw, cn // 2), (rw, cn // 2), (rw, cu // 2), (rd, cn // 2)]
+    full = [buf(3, d, d), buf(d, d), buf(d, ff), buf(ff, d)]
+    oq, oo, ou, od, total = pl.pallas_call(
+        scatter_kernel,
+        in_specs=[hbm] * 4 + [vmem],
+        out_specs=[vmem] * 5,
+        out_shape=[jax.ShapeDtypeStruct((LAYERS,) + s, F32) for s in outs] + [jax.ShapeDtypeStruct(pack.shape, F32)],
+        scratch_shapes=full + full + [
+            buf(ZN, 3, 2 * rw, cn), buf(ZN, 2 * rw, cn), buf(ZN, rd, d), buf(ZN, 2 * rw, cu // 2),
+            buf(2, ZN, rw, cu // 2), buf(ZN, rw, cu // 2), buf(ZN, rw, cu // 2),
+            buf(ZN + 1, 3, 2 * rw, cn), buf(ZN + 1, 2 * rw, cn), buf(ZN + 1, rd, d), buf(ZN + 1, rw, cu),
+            buf(3, rw, cn), buf(rw, cn), buf(rd, cn),
+        ] + [wide(*s) for s in outs] + [wide(*pack.shape)] * 10 + [
+            pltpu.SemaphoreType.DMA((140,)), pltpu.SemaphoreType.DMA((120,)), pltpu.SemaphoreType.DMA((6 * ZN,)),
+        ],
+        compiler_params=pltpu.CompilerParams(collective_id=2, has_side_effects=True, vmem_limit_bytes=VMEM_LIMIT),
+        name="gradient_scatter",
+    )(gq, go, gup, gdn, pack)
+    w, n = lax.axis_index("wide"), lax.axis_index("narrow")
+    gb = lax.dynamic_slice(total[0:8].reshape(2, 4, d), (0, n, w * rw), (2, 1, rw))
+    gn = lax.dynamic_slice(total[16:24].reshape(2, 4, d), (0, n, w * rw), (2, 1, rw))
+    gub = lax.dynamic_slice(total[8:16].reshape(2, ff), (0, (4 * w + n) * rw), (2, rw))
+    return oq, oo, ou, od, gb, gub, gn
+
+
 def gather_weights(pieces):
     wqkv, wo, wup, wdn, bias, ubias, norm = pieces
     narrow = [(wqkv, 3), (wo, 2), (wup, 2), (wdn, 2), (bias, 1), (norm, 1)]
@@ -752,7 +1106,8 @@
     weights = gather((qkv_weight, out_weight, up_weight, down_weight, biases, up_bias, norm_params))
     text_out, mem_out, kept = forward_local(text, mem, cnt, lens, weights)
     text_grad, mem_grad, grads, small = backward_local(cot, cot_mem, cnt, lens, kept, weights)
-    grads = scatter_grads(weight_grads(kept, grads), small)
+    scatter = scatter_fast if near else scatter_grads
+    grads = scatter(weight_grads(kept, grads), small)
     return (text_out[:, None], mem_out[:, None], text_grad[:, None], mem_grad[:, None]) + grads
 
 

time: 1190 us -> 543 us (0.46)
  waiting for transfers between devices: 711 us -> 0 us
  Pallas kernels: 314 us -> 463 us
  local copies, waits for them, and re-layouts: 68.4 us -> 27.2 us
  blocking collectives: 14.3 us -> 0 us
  between operations: 14.1 us -> 0.87 us
    unnamed x16 -> x0, waiting for transfers between devices: 363 us -> none
    reduce_scatter x6 -> x0, waiting for transfers between devices: 348 us -> none  [the longest x2 196 us: scatter_two(): lax.psum_scatter(low.astype(F32), 'wide', scatter_dimension=row_axis, til...]
    pallas_call x0 -> x1, Pallas kernels: none -> 149 us  [scatter_fast(): pl.pallas_call(scatter_kernel, in_specs=[hbm] * 4 + [vmem], out_specs=[vm...]
    unnamed x58 -> x46, local copies, waits for them, and re-layouts: 53.2 us -> 20.2 us
    unnamed x1 -> x0, blocking collectives: 14.3 us -> none
  transfers between devices with their start and end apart: 11 -> 0, of which waited for: 10 -> 0; matrix products, arithmetic and copies ran while one was open for 9% -> 0% of each run, Pallas kernels for 0% -> 0%
where the time goes in v3:
time: 543 us
  Pallas kernels  463 us (85%)
  matrix products  47.7 us (9%)
  local copies, waits for them, and re-layouts  27.2 us (5%)
    pallas_call x1, Pallas kernels, scatter_fast(): pl.pallas_call(scatter_kernel, in_specs=[hbm] * 4 + [vmem], out_specs=[vm...  149 us
    pallas_call x1, Pallas kernels, gather_fast(): pl.pallas_call(gather_kernel, in_specs=[vmem] * 5, out_specs=[hbm] * 5, o...  133 us
    pallas_call x1, Pallas kernels, backward_local(): pl.pallas_call(bwd_kernel, grid=(SEGS, LAYERS), in_specs=[smem, smem, pl....  103 us
    pallas_call x1, Pallas kernels, forward_local(): pl.pallas_call(fwd_kernel, grid=(SEGS, LAYERS), in_specs=[smem, smem, pl....  78.3 us
    dot_general x4, matrix products, product(): lax.dot_general(lhs, rhs, dims, preferred_element_type=F32).astype(BF)  47.7 us
    unnamed x46, local copies, waits for them, and re-layouts  20.2 us

profile of v3, /device:TPU:0, one launch (start us, length us, event | category | flops | bytes accessed | tf_op | source)
XLA Modules:
  0.0 542.9 jit_solution(2269812872549319016)
XLA Ops:
  0.6 0.0 copy-start.2
  0.7 0.0 copy-start.7
  0.7 0.0 copy-start.8
  0.7 2.6 copy.53
  3.3 0.8 bitcast_convert_fusion
  4.1 0.7 pad_maximum_fusion.mem0
  4.8 0.9 copy.26.d_in
  5.7 0.1 pad.16.clone
  5.8 0.0 copy-done.7
  5.8 0.1 maximum_maximum_fusion
  5.9 0.6 pad_convert_fusion.1.s_in
  6.5 133.1 %weight_gather.1 = (bf16[2,3,768,768]{3,2,1,0:T(8,128)(2,1)}, bf16[2,768,768]{2,1,0:T(8,128)(2,1)}, bf16[2,768,3072]{2,1,0:T(8,128)(2,1)}, bf16[2,3072,768]{2,1,0:T(8,128)(2,1)}, f32[4,2,2,2,8,128]{5,4,3,2,1,0:T(8,128)}) custom-call(bf16[2,3,96,192]{3,2,1,0:T(8,128)(2,1)} %q_in.1, bf16[2,96,192]{2,1,0:T(8,128)(2,1)} %o_in.1, bf16[2,96,768]{2,1,0:T(8,128)(2,1)} %u_in.1, ...), custom_call_target="tpu_custom_call" | custom-call | tf_op jit(solution)/shard_map/weight_gather/pallas_call | solution.py:688
  139.6 1.0 copy.54
  140.6 0.7 slice.38.bias
  141.3 0.9 slice.49
  142.3 0.7 broadcast_in_dim_reshape.3.ubias
  143.0 0.7 slice.41.norm
  143.7 78.3 %rmt_forward.1 = (bf16[2,4,108,768]{3,2,1,0:T(8,128)(2,1)}, f32[2,24,768]{2,1,0:T(8,128)}, bf16[2,1024,768]{2,1,0:T(8,128)(2,1)}, bf16[2,1024,2304]{2,1,0:T(8,12...) custom-call(s32[2]{0:T(128)} %bitcast.51, ...), custom_call_target="tpu_custom_call" | custom-call | tf_op jit(solution)/shard_map/rmt_forward/pallas_call | solution.py:165
  221.9 0.0 copy-start
  221.9 0.0 copy-start.6
  222.0 3.2 copy.35
  225.1 0.9 fusion
  226.1 0.6 copy.36
  226.7 1.2 copy.52
  227.9 0.7 pad_convert_fusion.gm0
  228.6 102.7 %rmt_backward.1 = (bf16[2,4,108,768]{3,2,1,0:T(8,128)(2,1)}, f32[2,24,768]{2,1,0:T(8,128)}, bf16[2,1024,2304]{2,1,0:T(8,128)(2,1)}, bf16[2,1024,768]{2,1,0:T(8,1...) custom-call(s32[2]{0:T(128)} %bitcast.52, ...), custom_call_target="tpu_custom_call" | custom-call | tf_op jit(solution)/shard_map/rmt_backward/pallas_call | solution.py:325
  331.3 0.0 slice-start
  331.3 3.2 copy.37
  334.5 0.9 fusion.1
  335.5 0.6 copy.38
  336.1 14.1 %convolution_convert_fusion.gq = bf16[2,768,2304]{2,1,0:T(8,128)(2,1)} fusion(bf16[2,1024,768]{2,1,0:T(8,128)(2,1)} %get-tuple-element.57, bf16[2,1024,2304]{2,1,0:T(8,128)(2,1)} %get-tuple-element.58), kind=kOutput, calls=%fused_computation | convolution fusion | flops 7251296256 | bytes 19660800 | tf_op jit(solution)/shard_map/dot_general | solution.py:373
  350.2 0.0 copy-done.12
  350.2 4.0 convolution_convert_fusion.3.go
  354.2 0.0 copy-done.10
  354.3 13.0 %convolution_convert_fusion.2.gu = bf16[2,768,3072]{2,1,0:T(8,128)(2,1)} fusion(bf16[2,1024,768]{2,1,0:T(8,128)(2,1)S(1)} %copy-done.10, bf16[2,1024,3072]{2,1,0:T(8,128)(2,1)S(1)} %bitcast.58), kind=kOutput, calls=%fused_computation.2 | convolution fusion | flops 9668395008 | bytes 25165824 | tf_op jit(solution)/shard_map/dot_general | solution.py:373
  367.2 16.6 %convolution_convert_fusion.1.gd = bf16[2,3072,768]{2,1,0:T(8,128)(2,1)} fusion(bf16[2,1024,3072]{2,1,0:T(8,128)(2,1)} %get-tuple-element.63, bf16[2,1024,768]{2,1,0:T(8,128)(2,1)} %get-tuple-element.64), kind=kOutput, calls=%fused_computation.1 | convolution fusion | flops 9668395008 | bytes 25165824 | tf_op jit(solution)/shard_map/dot_general | solution.py:373
  383.8 0.1 reduce_sum.29
  383.9 0.1 reduce_sum.28
  384.0 0.1 reduce_sum.27
  384.1 0.6 pad_maximum_fusion.1.sm_in
  384.7 149.4 %gradient_scatter.1 = (f32[2,3,96,192]{3,2,1,0:T(8,128)}, f32[2,96,192]{2,1,0:T(8,128)}, f32[2,96,768]{2,1,0:T(8,128)}, f32[2,384,192]{2,1,0:T(8,128)}, f32[24,768]{1,0:T(8,128)}) custom-call(bf16[2,768,2304]{2,1,0:T(8,128)(2,1)} %convolution_convert_fusion.gq, bf16[2,768,768]{2,1,0:T(8,128)(2,1)} %convolution_convert_fusion.3.go, ...), custom_call_target="tpu_custom_call" | custom-call | tf_op jit(solution)/shard_map/gradient_scatter/pallas_call | solution.py:1045
  534.1 2.3 copy.39
  536.4 0.8 fusion.3
  537.2 0.6 constant_dynamic-slice_fusion
  537.9 0.6 constant_dynamic-slice_fusion.1
  538.5 1.9 copy.60
  540.4 1.6 copy.61
  542.1 0.8 copy.62
  (36 shorter events, 0.2 us)
Async XLA Ops:
  0.6 4.2 copy-start.2
  0.7 5.2 copy-start.7
  0.7 5.2 copy-start.8
  0.7 5.2 copy-start.9
  221.9 4.8 copy-start
  221.9 6.0 %copy-start.6 = (bf16[2,1,10,768]{3,0,2,1:T(2,128)(2,1)S(1)}, bf16[2,1,10,768]{3,0,2,1:T(2,128)(2,1)}, u32[]{:S(2)}) copy-start(bf16[2,1,10,768]{3,0,2,1:T(2,128)(2,1)} %param.18) | copy-start | bytes 92164
  331.3 22.9 %slice-start = ((s8[12582912]{0:T(1024)(128)(4,1)}), s8[4194304]{0:T(1024)(128)(4,1)S(1)}, s32[]{:S(2)}) async-start(s8[12582912]{0:T(1024)(128)(4,1)} %bitcast.57), calls=%async_computation | async-start | bytes 8388608
  336.1 14.1 %copy-start.11 = (bf16[2,1024,768]{2,1,0:T(8,128)(2,1)S(1)}, bf16[2,1024,768]{2,1,0:T(8,128)(2,1)}, u32[]{:S(2)}) copy-start(bf16[2,1024,768]{2,1,0:T(8,128)(2,1)} %get-tuple-element.59) | copy-start | bytes 9437188
  336.1 14.1 %copy-start.12 = (bf16[2,1024,768]{2,1,0:T(8,128)(2,1)S(1)}, bf16[2,1024,768]{2,1,0:T(8,128)(2,1)}, u32[]{:S(2)}) copy-start(bf16[2,1024,768]{2,1,0:T(8,128)(2,1)} %get-tuple-element.60) | copy-start | bytes 9437188
  336.1 18.1 %slice-start.1 = ((s8[12582912]{0:T(1024)(128)(4,1)}), s8[4194304]{0:T(1024)(128)(4,1)S(1)}, s32[]{:S(2)}) async-start(s8[12582912]{0:T(1024)(128)(4,1)} %bitcast.57), calls=%async_computation.1 | async-start | bytes 8388608
  336.1 18.1 %slice-start.2 = ((s8[12582912]{0:T(1024)(128)(4,1)}), s8[4194304]{0:T(1024)(128)(4,1)S(1)}, s32[]{:S(2)}) async-start(s8[12582912]{0:T(1024)(128)(4,1)} %bitcast.57), calls=%async_computation.2 | async-start | bytes 8388608
  350.2 4.1 copy-start.10
  367.2 16.6 %copy-start.5 = (f32[2,4,8,768]{3,2,1,0:T(8,128)S(1)}, f32[2,4,8,768]{3,2,1,0:T(8,128)}, u32[]{:S(2)}) copy-start(f32[2,4,8,768]{3,2,1,0:T(8,128)} %get-tuple-element.67) | copy-start | bytes 589828
  367.2 16.7 %copy-start.4 = (f32[2,8,3072]{2,1,0:T(8,128)S(1)}, f32[2,8,3072]{2,1,0:T(8,128)}, u32[]{:S(2)}) copy-start(f32[2,8,3072]{2,1,0:T(8,128)} %get-tuple-element.66) | copy-start | bytes 589828
  367.2 16.8 %copy-start.3 = (f32[2,4,8,768]{3,2,1,0:T(8,128)S(1)}, f32[2,4,8,768]{3,2,1,0:T(8,128)}, u32[]{:S(2)}) copy-start(f32[2,4,8,768]{3,2,1,0:T(8,128)} %get-tuple-element.65) | copy-start | bytes 589828
  534.1 8.0 %copy-start.1 = (f32[2,96,768]{2,1,0:T(8,128)S(1)}, f32[2,96,768]{2,1,0:T(8,128)}, u32[]{:S(2)}) copy-start(f32[2,96,768]{2,1,0:T(8,128)} %get-tuple-element.108) | copy-start | bytes 1769476

commit v4 on v3

--- a/solution.py
+++ b/solution.py
@@ -24,7 +24,9 @@
 RSQRT2 = 0.7071067811865476
 RSQRT2PI = 0.3989422804014327
 VMEM_LIMIT = 66_000_000
-FT = 512
+CHUNK = 32
+GROUP_F = 6
+GROUP_B = 6
 
 
 def dot(a, b):
@@ -56,17 +58,41 @@
     return jnp.sum(v.reshape(rows // 8, 8, cols), axis=0)
 
 
+class Loads:
+    def __init__(self, pairs, sems, first, order):
+        self.pairs, self.sems, self.first, self.order = pairs, sems, first, order
+
+    def each(self, layer, what):
+        for k, (src, dst) in enumerate(self.pairs):
+            getattr(pltpu.make_async_copy(src.at[layer], dst.at[layer], self.sems.at[layer, k]), what)()
+
+    def start(self):
+        self.each(self.order[0], "start")
+
+    def need(self, step):
+        @pl.when(self.first & (step == 0))
+        def _():
+            self.each(self.order[0], "wait")
+            self.each(self.order[1], "start")
+
+        @pl.when(self.first & (step == 1))
+        def _():
+            self.each(self.order[1], "wait")
+
+
 def fwd_kernel(
-    counts, lens, text, mem0, wqkv, wo, wup, wdn, bias, ubias, norm,
+    counts, lens, text, mem0, wqkv_hbm, wo_hbm, wup_hbm, wdn_hbm, bias, ubias, norm,
     text_out, mem_out, a_out, qkv_out, p_out, c_out, y_out, g_out, gp_out, xh1_out, xh2_out, rs_out,
-    x_ref, mem_ref, y_ref, acc_ref,
+    x_ref, mem_ref, y_ref, acc_ref, wqkv, wo, wup, wdn, wsem,
 ):
     seg = pl.program_id(0)
     layer = pl.program_id(1)
     d = x_ref.shape[-1]
+    loads = Loads(((wqkv_hbm, wqkv), (wo_hbm, wo), (wup_hbm, wup), (wdn_hbm, wdn)), wsem, seg == 0, (0, 1))
 
     @pl.when((seg == 0) & (layer == 0))
     def _():
+        loads.start()
         mem_ref[...] = mem0[...]
 
     @pl.when(layer == 0)
@@ -77,6 +103,7 @@
             now = x_ref[tail, :]
             x_ref[tail, :] = jnp.where(row_ids(now.shape) < TEXT - TAIL, now, mem_ref[i])
 
+    loads.need(layer)
     xb = x_ref[...].astype(BF)
     a_out[0] = xb
     qkv_out[0, :, 0:d] = (dot(xb, wqkv[layer, 0]) + bias[layer, 0:1, :]).astype(BF)
@@ -85,55 +112,60 @@
 
     low_half = lane_ids((SEG, 128)) < HD
     lanes = lane_ids((1, SEG))
+
+    def heads_of(v):
+        zero = jnp.zeros_like(v)
+        return jnp.concatenate([jnp.where(low_half, v, zero), jnp.where(low_half, zero, v)], axis=0)
+
     for i in range(MB):
         vr = valid_rows(seg, counts[i], lens[i])
         keep = (lanes < vr) | (lanes >= TEXT)
         r0 = i * SEG
-        for pair in range(HEADS // 2):
-            c0 = pair * 128
-            q = qkv_out[0, r0 : r0 + SEG, c0 : c0 + 128]
-            k = qkv_out[0, r0 : r0 + SEG, d + c0 : d + c0 + 128]
-            v = qkv_out[0, r0 : r0 + SEG, 2 * d + c0 : 2 * d + c0 + 128]
-            zero = jnp.zeros_like(q)
-            q2 = jnp.concatenate([jnp.where(low_half, q, zero), jnp.where(low_half, zero, q)], axis=0)
-            s = dot_rt(q2, k) * (HD ** -0.5)
-            s = jnp.where(keep, s, NEG)
-            e = jnp.exp(s - jnp.max(s, axis=-1, keepdims=True))
-            p = (e / jnp.sum(e, axis=-1, keepdims=True)).astype(BF)
-            u0 = (i * (HEADS // 2) + pair) * 2 * SEG
-            p_out[0, u0 : u0 + 2 * SEG, :] = p
-            c2 = dot(p, v)
-            c_out[0, r0 : r0 + SEG, c0 : c0 + 128] = jnp.where(low_half, c2[:SEG], c2[SEG:]).astype(BF)
-
-    def norm_to(h, gain, shift, xh_out, rs_index):
-        center = h - jnp.mean(h, axis=-1, keepdims=True)
-        rs = lax.rsqrt(jnp.mean(center * center, axis=-1, keepdims=True) + EPS)
-        xh = center * rs
-        xh_out[0] = xh
-        rs_out[0, rs_index] = jnp.broadcast_to(rs, (ROWS, 128))
-        return xh * gain + shift
-
-    h1 = x_ref[...] + (dot(c_out[0], wo[layer]) + bias[layer, 2:3, :])
-    y = norm_to(h1, norm[layer, 0:1, :], norm[layer, 1:2, :], xh1_out, 0)
-    y_ref[...] = y
-    y_out[0] = y.astype(BF)
-
-    acc_ref[...] = jnp.zeros_like(acc_ref)
+        for g0 in range(0, HEADS // 2, GROUP_F):
+            pairs = range(g0, g0 + GROUP_F)
+
+            def part(j, pair):
+                return qkv_out[0, r0 : r0 + SEG, j * d + pair * 128 : j * d + pair * 128 + 128]
+
+            s_all = [dot_rt(heads_of(part(0, p) * (HD ** -0.5)), part(1, p)) for p in pairs]
+            s_all = [jnp.where(keep, s, NEG) for s in s_all]
+            e_all = [jnp.exp(s - jnp.max(s, axis=-1, keepdims=True)) for s in s_all]
+            p_all = [(e * (1.0 / jnp.sum(e, axis=-1, keepdims=True))).astype(BF) for e in e_all]
+            c_all = [dot(pv, part(2, p)) for pv, p in zip(p_all, pairs)]
+            for p, pv, c2 in zip(pairs, p_all, c_all):
+                u0 = (i * (HEADS // 2) + p) * 2 * SEG
+                p_out[0, u0 : u0 + 2 * SEG, :] = pv
+                c_out[0, r0 : r0 + SEG, p * 128 : p * 128 + 128] = jnp.where(low_half, c2[:SEG], c2[SEG:]).astype(BF)
+
+    def norm_to(base_ref, gain, shift, add, xh_out, rs_index, to_ref, low_out):
+        for k in range(0, ROWS, CHUNK):
+            rows = slice(k, k + CHUNK)
+            h = base_ref[rows, :] + (acc_ref[rows, :] + add)
+            center = h - jnp.mean(h, axis=-1, keepdims=True)
+            rs = lax.rsqrt(jnp.mean(center * center, axis=-1, keepdims=True) + EPS)
+            xh = center * rs
+            xh_out[0, rows, :] = xh
+            rs_out[0, rs_index, rows, :] = jnp.broadcast_to(rs, (CHUNK, 128))
+            out = xh * gain + shift
+            to_ref[rows, :] = out
+            if low_out is not None:
+                low_out[0, rows, :] = out.astype(BF)
+
+    acc_ref[...] = dot(c_out[0], wo[layer])
+    norm_to(x_ref, norm[layer, 0:1, :], norm[layer, 1:2, :], bias[layer, 2:3, :], xh1_out, 0, y_ref, y_out)
+
     ff = wup.shape[-1]
 
-    def ffn_step(j, carry):
-        cols = pl.ds(pl.multiple_of(j * FT, FT), FT)
+    def ffn_step():
+        cols = slice(0, ff)
         u = dot(y_out[0], wup[layer, :, cols]) + ubias[layer, :, cols]
         cdf = 0.5 * (1.0 + lax.erf(u * RSQRT2))
-        g = (u * cdf).astype(BF)
-        g_out[0, :, cols] = g
+        g_out[0, :, cols] = (u * cdf).astype(BF)
         gp_out[0, :, cols] = (cdf + u * (jnp.exp(-0.5 * (u * u)) * RSQRT2PI)).astype(BF)
-        acc_ref[...] += dot(g, wdn[layer, cols, :])
-        return carry
-
-    lax.fori_loop(0, ff // FT, ffn_step, 0)
-    h2 = y_ref[...] + (acc_ref[...] + bias[layer, 3:4, :])
-    x_ref[...] = norm_to(h2, norm[layer, 2:3, :], norm[layer, 3:4, :], xh2_out, 1)
+
+    ffn_step()
+    acc_ref[...] = dot(g_out[0], wdn[layer])
+    norm_to(y_ref, norm[layer, 2:3, :], norm[layer, 3:4, :], bias[layer, 3:4, :], xh2_out, 1, x_ref, None)
 
     @pl.when(layer == LAYERS - 1)
     def _():
@@ -162,13 +194,14 @@
     total = SEGS * ROWS
     units = MB * HEADS * SEG
     smem = pl.BlockSpec(memory_space=pltpu.SMEM)
+    hbm = pl.BlockSpec(memory_space=pl.ANY)
     outs = pl.pallas_call(
         fwd_kernel,
         grid=(SEGS, LAYERS),
         in_specs=[
             smem, smem,
             pl.BlockSpec((MB, 1, TEXT, d), lambda s, l: (0, s, 0, 0)),
-            whole(mem0.shape), whole(wqkv.shape), whole(wo.shape), whole(wup.shape), whole(wdn.shape),
+            whole(mem0.shape), hbm, hbm, hbm, hbm,
             whole(bias.shape), whole((LAYERS, 1, ff)), whole(norm.shape),
         ],
         out_specs=[
@@ -195,6 +228,8 @@
         scratch_shapes=[
             pltpu.VMEM((ROWS, d), F32), pltpu.VMEM(mem0.shape, F32),
             pltpu.VMEM((ROWS, d), F32), pltpu.VMEM((ROWS, d), F32),
+            pltpu.VMEM(wqkv.shape, BF), pltpu.VMEM(wo.shape, BF), pltpu.VMEM(wup.shape, BF), pltpu.VMEM(wdn.shape, BF),
+            pltpu.SemaphoreType.DMA((LAYERS, 4)),
         ],
         compiler_params=pltpu.CompilerParams(
             dimension_semantics=("arbitrary", "arbitrary"), vmem_limit_bytes=VMEM_LIMIT
@@ -206,17 +241,19 @@
 
 
 def bwd_kernel(
-    counts, lens, cot, gm0, qkv, p_in, gp_in, xh1_in, xh2_in, rs_in, wqkv, wo, wup, wdn, norm,
+    counts, lens, cot, gm0, qkv, p_in, gp_in, xh1_in, xh2_in, rs_in, wqkv_hbm, wo_hbm, wup_hbm, wdn_hbm, norm,
     tg_out, gm_out, dqkv_out, dao_out, du_out, df_out, gb_out, gub_out, gn_out,
-    g_ref, gm_ref, t_ref, acc_ref, dc_ref,
+    g_ref, gm_ref, t_ref, acc_ref, dc_ref, wqkv, wo, wup, wdn, wsem,
 ):
     seg = SEGS - 1 - pl.program_id(0)
     step = pl.program_id(1)
     layer = LAYERS - 1 - step
+    loads = Loads(((wqkv_hbm, wqkv), (wo_hbm, wo), (wup_hbm, wup), (wdn_hbm, wdn)), wsem, seg == SEGS - 1, (1, 0))
     d = g_ref.shape[-1]
 
     @pl.when((seg == SEGS - 1) & (step == 0))
     def _():
+        loads.start()
         gm_ref[...] = gm0[...]
         gb_out[...] = jnp.zeros_like(gb_out)
         gub_out[...] = jnp.zeros_like(gub_out)
@@ -234,62 +271,78 @@
             mem_part = jnp.where((rows >= TEXT - TAIL + MEM) & (seg < counts[i]), gm_ref[i], 0.0)
             g_ref[tail, :] = jnp.where(rows < TEXT - TAIL, now, mem_part)
 
-    def norm_back(gout, xh, rs, gain, slot):
-        gn_out[layer, slot] += colsum(gout * xh)
-        gn_out[layer, slot + 1] += colsum(gout)
-        t = gout * gain
-        return rs * (t - jnp.mean(t, axis=-1, keepdims=True) - xh * jnp.mean(t * xh, axis=-1, keepdims=True))
-
-    dh2 = norm_back(g_ref[...], xh2_in[0], rs_in[0, 1][:, :1], norm[layer, 2:3, :], 2)
-    t_ref[...] = dh2
-    df = dh2.astype(BF)
-    df_out[0] = df
-    gb_out[layer, 3] += colsum(df.astype(F32))
-    acc_ref[...] = jnp.zeros_like(acc_ref)
+    loads.need(step)
+
+    def norm_back(base_ref, add_ref, xh_in, rs_slot, gain, slot, low_out, low_slot):
+        sums = [jnp.zeros((8, d), F32) for _ in range(3)]
+        for k in range(0, ROWS, CHUNK):
+            rows = slice(k, k + CHUNK)
+            gout = base_ref[rows, :]
+            if add_ref is not None:
+                gout = gout + add_ref[rows, :]
+            xh = xh_in[0, rows, :]
+            gx = gout * xh
+            t = gout * gain
+            inner = jnp.mean(gx * gain, axis=-1, keepdims=True)
+            dh = rs_in[0, rs_slot, rows, :][:, :1] * (t - jnp.mean(t, axis=-1, keepdims=True) - xh * inner)
+            t_ref[rows, :] = dh
+            low = dh.astype(BF)
+            low_out[0, rows, :] = low
+            sums = [v + colsum(w) for v, w in zip(sums, (gx, gout, low.astype(F32)))]
+        gn_out[layer, slot] += sums[0]
+        gn_out[layer, slot + 1] += sums[1]
+        gb_out[layer, low_slot] += sums[2]
+
+    norm_back(g_ref, None, xh2_in, 1, norm[layer, 2:3, :], 2, df_out, 3)
     ff = wup.shape[-1]
 
-    def ffn_step(j, carry):
-        cols = pl.ds(pl.multiple_of(j * FT, FT), FT)
+    def ffn_step():
+        cols = slice(0, ff)
         dg = dot_rt(df_out[0], wdn[layer, cols, :])
         du = (dg * gp_in[0, :, cols].astype(F32)).astype(BF)
         du_out[0, :, cols] = du
         gub_out[layer, :, cols] += colsum(du.astype(F32))
-        acc_ref[...] += dot_rt(du, wup[layer, :, cols])
-        return carry
-
-    lax.fori_loop(0, ff // FT, ffn_step, 0)
-    dh1 = norm_back(t_ref[...] + acc_ref[...], xh1_in[0], rs_in[0, 0][:, :1], norm[layer, 0:1, :], 0)
-    t_ref[...] = dh1
-    dao = dh1.astype(BF)
-    dao_out[0] = dao
-    gb_out[layer, 2] += colsum(dao.astype(F32))
-    dc_ref[...] = dot_rt(dao, wo[layer]).astype(BF)
+
+    ffn_step()
+    acc_ref[...] = dot_rt(du_out[0], wup[layer])
+    norm_back(t_ref, acc_ref, xh1_in, 0, norm[layer, 0:1, :], 0, dao_out, 2)
+    dc_ref[...] = dot_rt(dao_out[0], wo[layer]).astype(BF)
 
     low_half = lane_ids((SEG, 128)) < HD
     scale = HD ** -0.5
+
+    def heads_of(v):
+        zero = jnp.zeros_like(v)
+        return jnp.concatenate([jnp.where(low_half, v, zero), jnp.where(low_half, zero, v)], axis=0)
+
     for i in range(MB):
         r0 = i * SEG
-        for pair in range(HEADS // 2):
-            c0 = pair * 128
-            q = qkv[0, r0 : r0 + SEG, c0 : c0 + 128]
-            k = qkv[0, r0 : r0 + SEG, d + c0 : d + c0 + 128]
-            v = qkv[0, r0 : r0 + SEG, 2 * d + c0 : 2 * d + c0 + 128]
-            dc = dc_ref[r0 : r0 + SEG, c0 : c0 + 128]
-            zero = jnp.zeros_like(q)
-            q2 = jnp.concatenate([jnp.where(low_half, q, zero), jnp.where(low_half, zero, q)], axis=0)
-            dc2 = jnp.concatenate([jnp.where(low_half, dc, zero), jnp.where(low_half, zero, dc)], axis=0)
-            u0 = (i * (HEADS // 2) + pair) * 2 * SEG
-            pb = p_in[0, u0 : u0 + 2 * SEG, :]
-            p = pb.astype(F32)
-            pdp = p * dot_rt(dc2, v)
-            ds = (pdp - p * jnp.sum(pdp, axis=-1, keepdims=True)).astype(BF)
-            dq2 = dot(ds, k)
-            dq = (jnp.where(low_half, dq2[:SEG], dq2[SEG:]) * scale).astype(BF)
-            dk = (dot_lt(ds, q2) * scale).astype(BF)
-            dv = dot_lt(pb, dc2).astype(BF)
-            dqkv_out[0, r0 : r0 + SEG, c0 : c0 + 128] = dq
-            dqkv_out[0, r0 : r0 + SEG, d + c0 : d + c0 + 128] = dk
-            dqkv_out[0, r0 : r0 + SEG, 2 * d + c0 : 2 * d + c0 + 128] = dv
+        for g0 in range(0, HEADS // 2, GROUP_B):
+            pairs = range(g0, g0 + GROUP_B)
+
+            def part(j, pair):
+                return qkv[0, r0 : r0 + SEG, j * d + pair * 128 : j * d + pair * 128 + 128]
+
+            def probs(pair):
+                u0 = (i * (HEADS // 2) + pair) * 2 * SEG
+                return p_in[0, u0 : u0 + 2 * SEG, :]
+
+            def out(j, pair, v):
+                dqkv_out[0, r0 : r0 + SEG, j * d + pair * 128 : j * d + pair * 128 + 128] = v.astype(BF)
+
+            dc2 = [heads_of(dc_ref[r0 : r0 + SEG, p * 128 : p * 128 + 128]) for p in pairs]
+            dp = [dot_rt(v, part(2, p)) for v, p in zip(dc2, pairs)]
+            for p, v in zip(pairs, dc2):
+                out(2, p, dot_lt(probs(p), v))
+            pdp = [probs(p).astype(F32) * v for p, v in zip(pairs, dp)]
+            ds = [
+                (v - probs(p).astype(F32) * jnp.sum(v, axis=-1, keepdims=True)).astype(BF) for p, v in zip(pairs, pdp)
+            ]
+            dq2 = [dot(v, part(1, p)) for v, p in zip(ds, pairs)]
+            dk = [dot_lt(v, heads_of(part(0, p))) for v, p in zip(ds, pairs)]
+            for p, a, b in zip(pairs, dq2, dk):
+                out(0, p, jnp.where(low_half, a[:SEG], a[SEG:]) * scale)
+                out(1, p, b * scale)
 
     gb_out[layer, 0] += colsum(dqkv_out[0, :, 0:d].astype(F32))
     gb_out[layer, 1] += colsum(dqkv_out[0, :, 2 * d : 3 * d].astype(F32))
@@ -318,6 +371,7 @@
     total = SEGS * ROWS
     units = MB * HEADS * SEG
     smem = pl.BlockSpec(memory_space=pltpu.SMEM)
+    hbm = pl.BlockSpec(memory_space=pl.ANY)
 
     def kept_spec(rows, cols):
         return pl.BlockSpec((1, rows, cols), lambda s, l: (LAYERS - 1 - l, SEGS - 1 - s, 0))
@@ -331,7 +385,7 @@
             whole(gm0.shape),
             kept_spec(ROWS, 3 * d), kept_spec(units, 128), kept_spec(ROWS, ff), kept_spec(ROWS, d), kept_spec(ROWS, d),
             pl.BlockSpec((1, 2, ROWS, 128), lambda s, l: (LAYERS - 1 - l, 0, SEGS - 1 - s, 0)),
-            whole(wqkv.shape), whole(wo.shape), whole(wup.shape), whole(wdn.shape), whole(norm.shape),
+            hbm, hbm, hbm, hbm, whole(norm.shape),
         ],
         out_specs=[
             pl.BlockSpec((MB, 1, TEXT, d), lambda s, l: (0, SEGS - 1 - s, 0, 0)),
@@ -353,6 +407,8 @@
         scratch_shapes=[
             pltpu.VMEM((ROWS, d), F32), pltpu.VMEM(gm0.shape, F32),
             pltpu.VMEM((ROWS, d), F32), pltpu.VMEM((ROWS, d), F32), pltpu.VMEM((ROWS, d), BF),
+            pltpu.VMEM(wqkv.shape, BF), pltpu.VMEM(wo.shape, BF), pltpu.VMEM(wup.shape, BF), pltpu.VMEM(wdn.shape, BF),
+            pltpu.SemaphoreType.DMA((LAYERS, 4)),
         ],
         compiler_params=pltpu.CompilerParams(
             dimension_semantics=("arbitrary", "arbitrary"), vmem_limit_bytes=VMEM_LIMIT

time: 543 us -> 502 us (0.924); the launches traced: 543 us -> 494 us
  Pallas kernels: 463 us -> 414 us
    pallas_call x1, Pallas kernels: 103 us -> 64.1 us  [backward_local(): pl.pallas_call(bwd_kernel, grid=(SEGS, LAYERS), in_specs=[smem, smem, pl....]
    pallas_call x1, Pallas kernels: 78.3 us -> 67.3 us  [forward_local(): pl.pallas_call(fwd_kernel, grid=(SEGS, LAYERS), in_specs=[smem, smem, pl....]
where the time goes in v4:
time: 502 us; the launch traced here: 494 us
  Pallas kernels  414 us (82%)
  matrix products  47.4 us (9%)
  local copies, waits for them, and re-layouts  27.2 us (5%)
    pallas_call x1, Pallas kernels, scatter_fast(): pl.pallas_call(scatter_kernel, in_specs=[hbm] * 4 + [vmem], out_specs=[vm...  149 us
    pallas_call x1, Pallas kernels, gather_fast(): pl.pallas_call(gather_kernel, in_specs=[vmem] * 5, out_specs=[hbm] * 5, o...  133 us
    pallas_call x1, Pallas kernels, forward_local(): pl.pallas_call(fwd_kernel, grid=(SEGS, LAYERS), in_specs=[smem, smem, pl....  67.3 us
    pallas_call x1, Pallas kernels, backward_local(): pl.pallas_call(bwd_kernel, grid=(SEGS, LAYERS), in_specs=[smem, smem, pl....  64.1 us
    dot_general x4, matrix products, product(): lax.dot_general(lhs, rhs, dims, preferred_element_type=F32).astype(BF)  47.4 us
    unnamed x46, local copies, waits for them, and re-layouts  20.2 us

profile of v4, /device:TPU:0, one launch (start us, length us, event | category | flops | bytes accessed | tf_op | source)
XLA Modules:
  0.0 493.6 jit_solution(15349331397820256390)
XLA Ops:
  0.7 2.6 copy.53
  3.3 0.8 bitcast_convert_fusion
  4.1 0.7 pad_maximum_fusion.mem0
  4.8 0.9 copy.26.d_in
  5.7 0.1 pad.16.clone
  5.8 0.1 maximum_maximum_fusion
  5.9 0.6 pad_convert_fusion.1.s_in
  6.5 133.1 %weight_gather.1 = (bf16[2,3,768,768]{3,2,1,0:T(8,128)(2,1)}, bf16[2,768,768]{2,1,0:T(8,128)(2,1)}, bf16[2,768,3072]{2,1,0:T(8,128)(2,1)}, bf16[2,3072,768]{2,1,0:T(8,128)(2,1)}, f32[4,2,2,2,8,128]{5,4,3,2,1,0:T(8,128)}) custom-call(bf16[2,3,96,192]{3,2,1,0:T(8,128)(2,1)} %q_in.1, bf16[2,96,192]{2,1,0:T(8,128)(2,1)} %o_in.1, bf16[2,96,768]{2,1,0:T(8,128)(2,1)} %u_in.1, ...), custom_call_target="tpu_custom_call" | custom-call | tf_op jit(solution)/shard_map/weight_gather/pallas_call | solution.py:744
  139.6 1.0 copy.54
  140.6 0.7 slice.38.bias
  141.3 0.9 slice.49
  142.3 0.7 broadcast_in_dim_reshape.3.ubias
  143.0 0.7 slice.41.norm
  143.7 67.3 %rmt_forward.1 = (bf16[2,4,108,768]{3,2,1,0:T(8,128)(2,1)}, f32[2,24,768]{2,1,0:T(8,128)}, bf16[2,1024,768]{2,1,0:T(8,128)(2,1)}, bf16[2,1024,2304]{2,1,0:T(8,12...) custom-call(s32[2]{0:T(128)} %bitcast.51, ...), custom_call_target="tpu_custom_call" | custom-call | tf_op jit(solution)/shard_map/rmt_forward/pallas_call | solution.py:198
  211.0 0.0 copy-start
  211.0 0.0 copy-start.6
  211.0 3.2 copy.35
  214.2 0.9 fusion
  215.1 0.6 copy.36
  215.7 1.2 copy.52
  216.9 0.0 copy-done.6
  217.0 0.7 pad_convert_fusion.gm0
  217.6 64.1 %rmt_backward.1 = (bf16[2,4,108,768]{3,2,1,0:T(8,128)(2,1)}, f32[2,24,768]{2,1,0:T(8,128)}, bf16[2,1024,2304]{2,1,0:T(8,128)(2,1)}, bf16[2,1024,768]{2,1,0:T(8,1...) custom-call(s32[2]{0:T(128)} %bitcast.52, ...), custom_call_target="tpu_custom_call" | custom-call | tf_op jit(solution)/shard_map/rmt_backward/pallas_call | solution.py:379
  281.8 0.0 slice-start
  281.8 3.2 copy.37
  285.0 0.9 fusion.1
  285.9 0.6 copy.38
  286.6 13.9 %convolution_convert_fusion.gq = bf16[2,768,2304]{2,1,0:T(8,128)(2,1)} fusion(bf16[2,1024,768]{2,1,0:T(8,128)(2,1)} %get-tuple-element.57, bf16[2,1024,2304]{2,1,0:T(8,128)(2,1)} %get-tuple-element.58), kind=kOutput, calls=%fused_computation | convolution fusion | flops 7251296256 | bytes 19660800 | tf_op jit(solution)/shard_map/dot_general | solution.py:429
  300.4 0.0 copy-done.12
  300.4 4.3 convolution_convert_fusion.3.go
  304.7 0.0 slice-done
  304.7 13.0 %convolution_convert_fusion.2.gu = bf16[2,768,3072]{2,1,0:T(8,128)(2,1)} fusion(bf16[2,1024,768]{2,1,0:T(8,128)(2,1)S(1)} %copy-done.10, bf16[2,1024,3072]{2,1,0:T(8,128)(2,1)S(1)} %bitcast.58), kind=kOutput, calls=%fused_computation.2 | convolution fusion | flops 9668395008 | bytes 25165824 | tf_op jit(solution)/shard_map/dot_general | solution.py:429
  317.7 16.3 %convolution_convert_fusion.1.gd = bf16[2,3072,768]{2,1,0:T(8,128)(2,1)} fusion(bf16[2,1024,3072]{2,1,0:T(8,128)(2,1)} %get-tuple-element.63, bf16[2,1024,768]{2,1,0:T(8,128)(2,1)} %get-tuple-element.64), kind=kOutput, calls=%fused_computation.1 | convolution fusion | flops 9668395008 | bytes 25165824 | tf_op jit(solution)/shard_map/dot_general | solution.py:429
  334.0 0.0 copy-done.5
  334.0 0.1 reduce_sum.29
  334.1 0.0 copy-done.4
  334.1 0.1 reduce_sum.28
  334.2 0.1 reduce_sum.27
  334.3 0.6 pad_maximum_fusion.1.sm_in
  335.0 149.4 %gradient_scatter.1 = (f32[2,3,96,192]{3,2,1,0:T(8,128)}, f32[2,96,192]{2,1,0:T(8,128)}, f32[2,96,768]{2,1,0:T(8,128)}, f32[2,384,192]{2,1,0:T(8,128)}, f32[24,768]{1,0:T(8,128)}) custom-call(bf16[2,768,2304]{2,1,0:T(8,128)(2,1)} %convolution_convert_fusion.gq, bf16[2,768,768]{2,1,0:T(8,128)(2,1)} %convolution_convert_fusion.3.go, ...), custom_call_target="tpu_custom_call" | custom-call | tf_op jit(solution)/shard_map/gradient_scatter/pallas_call | solution.py:1101
  484.3 0.0 copy-start.1
  484.4 2.3 copy.39
  486.6 0.8 fusion.3
  487.4 0.6 constant_dynamic-slice_fusion
  488.1 0.6 constant_dynamic-slice_fusion.1
  488.7 1.9 copy.60
  490.7 1.6 copy.61
  492.3 0.8 copy.62
  (36 shorter events, 0.2 us)
Async XLA Ops:
  0.6 4.2 copy-start.2
  0.7 5.2 %copy-start.7 = (bf16[2,96]{1,0:T(2,128)(2,1)S(1)}, bf16[2,96]{1,0:T(2,128)(2,1)}, u32[]{:S(2)}) copy-start(bf16[2,96]{1,0:T(2,128)(2,1)} %param.24) | copy-start | bytes 1156
  0.7 5.2 %copy-start.8 = (bf16[2,1,96]{2,0,1:T(2,128)(2,1)S(1)}, bf16[2,1,96]{2,0,1:T(2,128)(2,1)}, u32[]{:S(2)}) copy-start(bf16[2,1,96]{2,0,1:T(2,128)(2,1)} %param.25) | copy-start | bytes 1156
  0.7 5.2 %copy-start.9 = (bf16[2,1,96]{2,0,1:T(2,128)(2,1)S(1)}, bf16[2,1,96]{2,0,1:T(2,128)(2,1)}, u32[]{:S(2)}) copy-start(bf16[2,1,96]{2,0,1:T(2,128)(2,1)} %param.23) | copy-start | bytes 1156
  211.0 4.8 copy-start
  211.0 6.0 %copy-start.6 = (bf16[2,1,10,768]{3,0,2,1:T(2,128)(2,1)S(1)}, bf16[2,1,10,768]{3,0,2,1:T(2,128)(2,1)}, u32[]{:S(2)}) copy-start(bf16[2,1,10,768]{3,0,2,1:T(2,128)(2,1)} %param.18) | copy-start | bytes 92164
  281.8 22.9 %slice-start = ((s8[12582912]{0:T(1024)(128)(4,1)}), s8[4194304]{0:T(1024)(128)(4,1)S(1)}, s32[]{:S(2)}) async-start(s8[12582912]{0:T(1024)(128)(4,1)} %bitcast.57), calls=%async_computation | async-start | bytes 8388608
  286.5 13.9 %copy-start.11 = (bf16[2,1024,768]{2,1,0:T(8,128)(2,1)S(1)}, bf16[2,1024,768]{2,1,0:T(8,128)(2,1)}, u32[]{:S(2)}) copy-start(bf16[2,1024,768]{2,1,0:T(8,128)(2,1)} %get-tuple-element.59) | copy-start | bytes 9437188
  286.6 13.9 %copy-start.12 = (bf16[2,1024,768]{2,1,0:T(8,128)(2,1)S(1)}, bf16[2,1024,768]{2,1,0:T(8,128)(2,1)}, u32[]{:S(2)}) copy-start(bf16[2,1024,768]{2,1,0:T(8,128)(2,1)} %get-tuple-element.60) | copy-start | bytes 9437188
  286.6 18.1 %slice-start.1 = ((s8[12582912]{0:T(1024)(128)(4,1)}), s8[4194304]{0:T(1024)(128)(4,1)S(1)}, s32[]{:S(2)}) async-start(s8[12582912]{0:T(1024)(128)(4,1)} %bitcast.57), calls=%async_computation.1 | async-start | bytes 8388608
  286.6 18.1 %slice-start.2 = ((s8[12582912]{0:T(1024)(128)(4,1)}), s8[4194304]{0:T(1024)(128)(4,1)S(1)}, s32[]{:S(2)}) async-start(s8[12582912]{0:T(1024)(128)(4,1)} %bitcast.57), calls=%async_computation.2 | async-start | bytes 8388608
  300.4 4.3 copy-start.10
  317.7 16.3 %copy-start.5 = (f32[2,4,8,768]{3,2,1,0:T(8,128)S(1)}, f32[2,4,8,768]{3,2,1,0:T(8,128)}, u32[]{:S(2)}) copy-start(f32[2,4,8,768]{3,2,1,0:T(8,128)} %get-tuple-element.67) | copy-start | bytes 589828
  317.7 16.4 %copy-start.4 = (f32[2,8,3072]{2,1,0:T(8,128)S(1)}, f32[2,8,3072]{2,1,0:T(8,128)}, u32[]{:S(2)}) copy-start(f32[2,8,3072]{2,1,0:T(8,128)} %get-tuple-element.66) | copy-start | bytes 589828
  317.7 16.5 %copy-start.3 = (f32[2,4,8,768]{3,2,1,0:T(8,128)S(1)}, f32[2,4,8,768]{3,2,1,0:T(8,128)}, u32[]{:S(2)}) copy-start(f32[2,4,8,768]{3,2,1,0:T(8,128)} %get-tuple-element.65) | copy-start | bytes 589828
  484.3 8.0 %copy-start.1 = (f32[2,96,768]{2,1,0:T(8,128)S(1)}, f32[2,96,768]{2,1,0:T(8,128)}, u32[]{:S(2)}) copy-start(f32[2,96,768]{2,1,0:T(8,128)} %get-tuple-element.108) | copy-start | bytes 1769476

commit v5 on v4

--- a/solution.py
+++ b/solution.py
@@ -82,12 +82,14 @@
 
 def fwd_kernel(
     counts, lens, text, mem0, wqkv_hbm, wo_hbm, wup_hbm, wdn_hbm, bias, ubias, norm,
-    text_out, mem_out, a_out, qkv_out, p_out, c_out, y_out, g_out, gp_out, xh1_out, xh2_out, rs_out,
+    text_out, mem_out, lhs_out, qkv_out, p_out, gp_out, xh1_out, xh2_out, rs_out,
     x_ref, mem_ref, y_ref, acc_ref, wqkv, wo, wup, wdn, wsem,
 ):
     seg = pl.program_id(0)
     layer = pl.program_id(1)
     d = x_ref.shape[-1]
+    a_out, c_out, y_out = (lhs_out.at[:, :, j * d : (j + 1) * d] for j in range(3))
+    g_out = lhs_out.at[:, :, 3 * d :]
     loads = Loads(((wqkv_hbm, wqkv), (wo_hbm, wo), (wup_hbm, wup), (wdn_hbm, wdn)), wsem, seg == 0, (0, 1))
 
     @pl.when((seg == 0) & (layer == 0))
@@ -207,19 +209,16 @@
         out_specs=[
             pl.BlockSpec((MB, 1, TEXT, d), lambda s, l: (0, s, 0, 0)),
             whole(mem0.shape),
-            saved(ROWS, d), saved(ROWS, 3 * d), saved(units, 128), saved(ROWS, d), saved(ROWS, d),
-            saved(ROWS, ff), saved(ROWS, ff), saved(ROWS, d), saved(ROWS, d),
+            saved(ROWS, 3 * d + ff), saved(ROWS, 3 * d), saved(units, 128),
+            saved(ROWS, ff), saved(ROWS, d), saved(ROWS, d),
             pl.BlockSpec((1, 2, ROWS, 128), lambda s, l: (l, 0, s, 0)),
         ],
         out_shape=[
             jax.ShapeDtypeStruct((MB, SEGS, TEXT, d), BF),
             jax.ShapeDtypeStruct(mem0.shape, F32),
-            jax.ShapeDtypeStruct((LAYERS, total, d), BF),
+            jax.ShapeDtypeStruct((LAYERS, total, 3 * d + ff), BF),
             jax.ShapeDtypeStruct((LAYERS, total, 3 * d), BF),
             jax.ShapeDtypeStruct((LAYERS, SEGS * units, 128), BF),
-            jax.ShapeDtypeStruct((LAYERS, total, d), BF),
-            jax.ShapeDtypeStruct((LAYERS, total, d), BF),
-            jax.ShapeDtypeStruct((LAYERS, total, ff), BF),
             jax.ShapeDtypeStruct((LAYERS, total, ff), BF),
             jax.ShapeDtypeStruct((LAYERS, total, d), F32),
             jax.ShapeDtypeStruct((LAYERS, total, d), F32),
@@ -242,14 +241,17 @@
 
 def bwd_kernel(
     counts, lens, cot, gm0, qkv, p_in, gp_in, xh1_in, xh2_in, rs_in, wqkv_hbm, wo_hbm, wup_hbm, wdn_hbm, norm,
-    tg_out, gm_out, dqkv_out, dao_out, du_out, df_out, gb_out, gub_out, gn_out,
-    g_ref, gm_ref, t_ref, acc_ref, dc_ref, wqkv, wo, wup, wdn, wsem,
+    tg_out, gm_out, rhs_out, small_out,
+    g_ref, gm_ref, t_ref, acc_ref, dc_ref, wqkv, wo, wup, wdn, wsem, gb_out, gub_out, gn_out,
 ):
     seg = SEGS - 1 - pl.program_id(0)
     step = pl.program_id(1)
     layer = LAYERS - 1 - step
     loads = Loads(((wqkv_hbm, wqkv), (wo_hbm, wo), (wup_hbm, wup), (wdn_hbm, wdn)), wsem, seg == SEGS - 1, (1, 0))
     d = g_ref.shape[-1]
+    ff = wup.shape[-1]
+    dqkv_out, dao_out = rhs_out.at[:, :, 0 : 3 * d], rhs_out.at[:, :, 3 * d : 4 * d]
+    du_out, df_out = rhs_out.at[:, :, 4 * d : 4 * d + ff], rhs_out.at[:, :, 4 * d + ff :]
 
     @pl.when((seg == SEGS - 1) & (step == 0))
     def _():
@@ -294,7 +296,6 @@
         gb_out[layer, low_slot] += sums[2]
 
     norm_back(g_ref, None, xh2_in, 1, norm[layer, 2:3, :], 2, df_out, 3)
-    ff = wup.shape[-1]
 
     def ffn_step():
         cols = slice(0, ff)
@@ -362,10 +363,19 @@
             gm_ref[i] = jnp.where(seg < counts[i], 0.0, gm_ref[i]) + back
         gm_out[...] = gm_ref[...]
 
+    @pl.when((seg == 0) & (layer == 0))
+    def _():
+        for l in range(LAYERS):
+            for k in range(4):
+                parts = (gb_out[l, k], gub_out[l, :, k * d : (k + 1) * d], gn_out[l, k])
+                for base, part in zip((0, 8, 16), parts):
+                    row = base + 4 * l + k
+                    small_out[row : row + 1, :] = jnp.sum(part, axis=0, keepdims=True)
+
 
 def backward_local(cot, cot_mem, counts, lens, kept, weights):
     wqkv, wo, wup, wdn, _, _, norm = weights
-    _, qkv, p_all, _, _, _, gp, xh1, xh2, rs = kept
+    _, qkv, p_all, gp, xh1, xh2, rs = kept
     d, ff = wup.shape[1:]
     gm0 = jnp.concatenate([jnp.zeros((MB, TEXT - TAIL + MEM, d), F32), cot_mem.astype(F32)], axis=1)
     total = SEGS * ROWS
@@ -390,25 +400,20 @@
         out_specs=[
             pl.BlockSpec((MB, 1, TEXT, d), lambda s, l: (0, SEGS - 1 - s, 0, 0)),
             whole(gm0.shape),
-            kept_spec(ROWS, 3 * d), kept_spec(ROWS, d), kept_spec(ROWS, ff), kept_spec(ROWS, d),
-            whole((LAYERS, 4, 8, d)), whole((LAYERS, 8, ff)), whole((LAYERS, 4, 8, d)),
+            kept_spec(ROWS, 5 * d + ff), whole((24, d)),
         ],
         out_shape=[
             jax.ShapeDtypeStruct((MB, SEGS, TEXT, d), BF),
             jax.ShapeDtypeStruct(gm0.shape, F32),
-            jax.ShapeDtypeStruct((LAYERS, total, 3 * d), BF),
-            jax.ShapeDtypeStruct((LAYERS, total, d), BF),
-            jax.ShapeDtypeStruct((LAYERS, total, ff), BF),
-            jax.ShapeDtypeStruct((LAYERS, total, d), BF),
-            jax.ShapeDtypeStruct((LAYERS, 4, 8, d), F32),
-            jax.ShapeDtypeStruct((LAYERS, 8, ff), F32),
-            jax.ShapeDtypeStruct((LAYERS, 4, 8, d), F32),
+            jax.ShapeDtypeStruct((LAYERS, total, 5 * d + ff), BF),
+            jax.ShapeDtypeStruct((24, d), F32),
         ],
         scratch_shapes=[
             pltpu.VMEM((ROWS, d), F32), pltpu.VMEM(gm0.shape, F32),
             pltpu.VMEM((ROWS, d), F32), pltpu.VMEM((ROWS, d), F32), pltpu.VMEM((ROWS, d), BF),
             pltpu.VMEM(wqkv.shape, BF), pltpu.VMEM(wo.shape, BF), pltpu.VMEM(wup.shape, BF), pltpu.VMEM(wdn.shape, BF),
             pltpu.SemaphoreType.DMA((LAYERS, 4)),
+            pltpu.VMEM((LAYERS, 4, 8, d), F32), pltpu.VMEM((LAYERS, 8, ff), F32), pltpu.VMEM((LAYERS, 4, 8, d), F32),
         ],
         compiler_params=pltpu.CompilerParams(
             dimension_semantics=("arbitrary", "arbitrary"), vmem_limit_bytes=VMEM_LIMIT
@@ -416,19 +421,37 @@
         name="rmt_backward",
     )(counts, lens, cot, gm0, qkv, p_all, gp, xh1, xh2, rs, wqkv, wo, wup, wdn, norm.astype(F32))
     tg, gm = outs[:2]
-    small = (outs[6].sum(axis=2), outs[7].sum(axis=1), outs[8].sum(axis=2))
-    return tg, gm[:, TEXT - TAIL + MEM :].astype(BF), outs[2:6], small
-
-
-def weight_grads(kept, grads):
-    a, _, _, c, y, g = kept[:6]
-    dqkv, dao, du, df = grads
-
-    def product(lhs, rhs):
-        dims = (((1,), (1,)), ((0,), (0,)))
-        return lax.dot_general(lhs, rhs, dims, preferred_element_type=F32).astype(BF)
-
-    return product(a, dqkv), product(c, dao), product(y, du), product(g, df)
+    return tg, gm[:, TEXT - TAIL + MEM :].astype(BF), outs[2], outs[3]
+
+
+TILES = 12
+
+
+def product_kernel(lhs, rhs, out):
+    out[0, 0] = dot_lt(lhs[0], rhs[0]).astype(BF)
+
+
+def weight_grads(lhs, rhs):
+    d = rhs.shape[-1] // 9
+    total = lhs.shape[1]
+
+    def left(l, t):
+        return (l, 0, jnp.where(t < 3, 0, jnp.where(t < 4, 1, jnp.where(t < 8, 2, t - 5))))
+
+    return pl.pallas_call(
+        product_kernel,
+        grid=(LAYERS, TILES),
+        in_specs=[
+            pl.BlockSpec((1, total, d), left),
+            pl.BlockSpec((1, total, d), lambda l, t: (l, 0, jnp.minimum(t, 8))),
+        ],
+        out_specs=pl.BlockSpec((1, 1, d, d), lambda l, t: (l, t, 0, 0)),
+        out_shape=jax.ShapeDtypeStruct((LAYERS, TILES, d, d), BF),
+        compiler_params=pltpu.CompilerParams(
+            dimension_semantics=("arbitrary", "arbitrary"), vmem_limit_bytes=VMEM_LIMIT
+        ),
+        name="weight_products",
+    )(lhs, rhs)
 
 
 MESH = pl.DeviceIdType.MESH
@@ -542,36 +565,55 @@
     for cp in local:
         cp.wait()
 
+    main = rd - rw
+
     def rows_a(zp):
         return span(2 * rw * zp, 2 * rw)
 
+    def rows_x(zp, xp):
+        return span(rw * (2 * zp + xp), rw)
+
+    def rows_d(zp, xp):
+        return pl.ds(pl.multiple_of(rd * (2 * zp + xp), rw), main)
+
+    def rows_v(zp, xp):
+        return pl.ds(pl.multiple_of(rd * (2 * zp + xp) + main, rw), rw)
+
+    def cols(yp):
+        return span(cn * yp, cn)
+
+    def blk_a(zp, xp, yp):
+        return [Q.at[mine, :, rows_x(zp, xp), cols(yp)]]
+
+    def blk_d(zp, xp, yp):
+        return [D.at[mine, rows_d(zp, xp), cols(yp)]]
+
     def reg_a(zp, yp, layer):
-        return [Q.at[layer, :, rows_a(zp), span(cn * yp, cn)], O.at[layer, rows_a(zp), span(cn * yp, cn)]]
-
-    def blk_a(wp, yp, layer):
-        rows = span(rw * wp, rw)
-        return [Q.at[layer, :, rows, span(cn * yp, cn)], O.at[layer, rows, span(cn * yp, cn)]]
+        return [Q.at[layer, :, rows_a(zp), cols(yp)]]
 
     def reg_d(zp, xp, layer):
-        return [D.at[layer, span(rd * (2 * zp + xp), rd), :]]
-
-    def blk_d(wp, yp, layer):
-        return [D.at[layer, span(rd * wp, rd), span(cn * yp, cn)]]
-
-    def blk_u(zp, xp, yp, layer):
-        return [U.at[layer, span(rw * (2 * zp + xp), rw), span(cu * yp, cu)]]
-
-    def blk_u1(zp, xp, yp, layer):
-        return [U.at[layer, span(rw * (2 * zp + xp), rw), span(cu * yp, half)]]
-
-    def blk_u2(zp, xp, yp, layer):
-        return [U.at[layer, span(rw * (2 * zp + xp), rw), span(cu * yp + half, half)]]
+        return [D.at[layer, rows_d(zp, xp), :]]
+
+    def u_cols(zp, xp, start, size):
+        return U.at[mine, rows_x(zp, xp), span(start, size)]
+
+    def blk_u(zp, xp, yp):
+        return [
+            u_cols(zp, xp, cu * yp, cu), O.at[mine, rows_x(zp, xp), cols(yp)], D.at[mine, rows_v(zp, xp), cols(yp)]
+        ]
+
+    def blk_u1(zp, xp, yp):
+        return [u_cols(zp, xp, cu * yp, half), O.at[mine, rows_x(zp, xp), cols(yp)]]
+
+    def blk_u2(zp, xp, yp):
+        return [u_cols(zp, xp, cu * yp + half, half), D.at[mine, rows_v(zp, xp), cols(yp)]]
 
     def pair_u1(zp, yp, layer):
-        return [U.at[layer, rows_a(zp), span(cu * yp, half)]]
+        return [U.at[layer, rows_a(zp), span(cu * yp, half)], O.at[layer, rows_a(zp), cols(yp)]]
 
     def pair_u2(zp, xp, layer):
-        return blk_u2(zp, xp, 0, layer) + blk_u2(zp, xp, 1, layer)
+        rows = rows_x(zp, xp)
+        return [U.at[layer, rows, span(cu * yp + half, half)] for yp in range(2)] + [D.at[layer, rows_v(zp, xp), :]]
 
     class Lane:
         def __init__(self, link, sent, got, parts):
@@ -623,49 +665,57 @@
         def recv(self, zp):
             self.each("up", self.su, zp, "wait_recv")
 
-    line_a = Line(lambda zp: reg_a(zp, y, mine), 2)
-    line_d = Line(lambda zp: reg_d(zp, x, mine), 1)
-    line_u = Line(lambda zp: blk_u(zp, x, y, mine), 1)
-    x1 = Lane("x", lambda zp: blk_a(w, y, mine), lambda zp: blk_a(w + 1 - 2 * x, y, mine), 2)
-    y1 = Lane("y", lambda zp: blk_d(w, y, mine), lambda zp: blk_d(w, 1 - y, mine), 1)
-    x_u1 = Lane("x", lambda zp: blk_u1(zp, x, y, mine), lambda zp: blk_u1(zp, 1 - x, y, mine), 1)
-    y_u2 = Lane("y", lambda zp: blk_u2(zp, x, y, mine), lambda zp: blk_u2(zp, x, 1 - y, mine), 1)
-    y_a = Lane("y", lambda zp: reg_a(zp, y, mine), lambda zp: reg_a(zp, 1 - y, mine), 2)
-    x_d = Lane("x", lambda zp: reg_d(zp, x, mine), lambda zp: reg_d(zp, 1 - x, mine), 1)
-    y_u1 = Lane("y", lambda zp: pair_u1(zp, y, mine), lambda zp: pair_u1(zp, 1 - y, mine), 1)
-    x_u2 = Lane("x", lambda zp: pair_u2(zp, x, mine), lambda zp: pair_u2(zp, 1 - x, mine), 2)
+    line_a = [Line(lambda zp, xp=xp: blk_a(zp, xp, y), 1) for xp in (x, 1 - x)]
+    line_d = [Line(lambda zp, yp=yp: blk_d(zp, x, yp), 1) for yp in (y, 1 - y)]
+    line_u = Line(lambda zp: blk_u(zp, x, y), 3)
+    x1 = Lane("x", lambda zp: blk_a(z, x, y), lambda zp: blk_a(z, 1 - x, y), 1)
+    y1 = Lane("y", lambda zp: blk_d(z, x, y), lambda zp: blk_d(z, x, 1 - y), 1)
+    x_u1 = Lane("x", lambda zp: blk_u1(zp, x, y), lambda zp: blk_u1(zp, 1 - x, y), 2)
+    y_u2 = Lane("y", lambda zp: blk_u2(zp, x, y), lambda zp: blk_u2(zp, x, 1 - y), 2)
+    y_a = [
+        Lane("y", lambda zp, xp=xp: blk_a(zp, xp, y), lambda zp, xp=xp: blk_a(zp, xp, 1 - y), 1) for xp in (x, 1 - x)
+    ]
+    x_d = [
+        Lane("x", lambda zp, yp=yp: blk_d(zp, x, yp), lambda zp, yp=yp: blk_d(zp, 1 - x, yp), 1) for yp in (y, 1 - y)
+    ]
+    y_u1 = Lane("y", lambda zp: pair_u1(zp, y, mine), lambda zp: pair_u1(zp, 1 - y, mine), 2)
+    x_u2 = Lane("x", lambda zp: pair_u2(zp, x, mine), lambda zp: pair_u2(zp, 1 - x, mine), 3)
 
     def to_partner(make, parts):
         return Lane("p", lambda zp: make(zp, mine), lambda zp: make(zp, other), parts)
 
-    p_a = to_partner(lambda zp, l: reg_a(zp, y, l), 2)
-    p_a2 = to_partner(lambda zp, l: reg_a(zp, 1 - y, l), 2)
+    p_a = to_partner(lambda zp, l: reg_a(zp, y, l), 1)
+    p_a2 = to_partner(lambda zp, l: reg_a(zp, 1 - y, l), 1)
     p_d = to_partner(lambda zp, l: reg_d(zp, x, l), 1)
     p_d2 = to_partner(lambda zp, l: reg_d(zp, 1 - x, l), 1)
-    p_u1 = to_partner(lambda zp, l: pair_u1(zp, y, l), 1)
-    p_u1b = to_partner(lambda zp, l: pair_u1(zp, 1 - y, l), 1)
-    p_u2 = to_partner(lambda zp, l: pair_u2(zp, x, l), 2)
-    p_u2b = to_partner(lambda zp, l: pair_u2(zp, 1 - x, l), 2)
+    p_u1 = to_partner(lambda zp, l: pair_u1(zp, y, l), 2)
+    p_u1b = to_partner(lambda zp, l: pair_u1(zp, 1 - y, l), 2)
+    p_u2 = to_partner(lambda zp, l: pair_u2(zp, x, l), 3)
+    p_u2b = to_partner(lambda zp, l: pair_u2(zp, 1 - x, l), 3)
 
     small_x = Lane("x", lambda zp: [S.at[z, x, y]], lambda zp: [S.at[z, 1 - x, y]], 1)
     small_y = Lane("y", lambda zp: [S.at[z, :, y]], lambda zp: [S.at[z, :, 1 - y]], 1)
     line_s = Line(lambda zp: [S.at[zp]], 1)
 
-    line_u.own()
+    small_x.send(0)
     x1.send(0)
     y1.send(0)
-    small_x.send(0)
     x_u1.send(z)
     y_u2.send(z)
+    line_a[0].own()
+    line_d[0].own()
+    line_u.own()
+    y_a[0].send(z)
+    x_d[0].send(z)
     small_x.recv(0)
     small_y.send(0)
     x1.recv(0)
-    line_a.own()
-    y_a.send(z)
+    line_a[1].own()
+    y_a[1].send(z)
     p_a.send(z)
     y1.recv(0)
-    line_d.own()
-    x_d.send(z)
+    line_d[1].own()
+    x_d[1].send(z)
     p_d.send(z)
     small_y.recv(0)
     line_s.own()
@@ -679,9 +729,11 @@
         p_u2.send(zp)
 
     def third(zp):
-        y_a.recv(zp)
+        for lane in y_a:
+            lane.recv(zp)
         p_a2.send(zp)
-        x_d.recv(zp)
+        for lane in x_d:
+            lane.recv(zp)
         p_d2.send(zp)
         y_u1.recv(zp)
         p_u1b.send(zp)
@@ -705,13 +757,15 @@
 
     second(z)
     for t in range(1, ZN):
+        take(line_a[0], t, y_a[0])
+        take(line_d[0], t, x_d[0])
         take(line_u, t, x_u1, y_u2)
-        take(line_a, t, y_a, p_a)
+        take(line_a[1], t, y_a[1], p_a)
         if t == 1:
             third(z)
         else:
             both_ways(t - 1, third)
-        take(line_d, t, x_d, p_d)
+        take(line_d[1], t, x_d[1], p_d)
         both_ways(t, second)
         take(line_s, t)
     both_ways(ZN - 1, third)
@@ -721,11 +775,11 @@
         for lane in partner:
             lane.recv(zp)
     for zp in range(ZN):
-        for lane in partner + (x_u1, y_u2, y_a, x_d, y_u1, x_u2):
+        for lane in partner + (x_u1, y_u2, *y_a, *x_d, y_u1, x_u2):
             lane.drain(zp)
     for lane in (x1, y1, small_x, small_y):
         lane.drain(0)
-    for line in (line_u, line_a, line_d, line_s):
+    for line in (line_u, *line_a, *line_d, line_s):
         line.own("wait_send")
         for t in range(1, ZN):
             line.relay(t, "wait_send")
@@ -756,7 +810,7 @@
             pltpu.VMEM((3, rw, cn), BF), pltpu.VMEM((rw, cn), BF), pltpu.VMEM((rw, cu), BF), pltpu.VMEM((rd, cn), BF),
             pltpu.VMEM((3, rw, 2 * cn), BF), pltpu.VMEM((rw, 2 * cn), BF),
             pltpu.VMEM((rw, 2 * cu), BF), pltpu.VMEM((rd, 2 * cn), BF),
-            pltpu.SemaphoreType.DMA((160,)), pltpu.SemaphoreType.DMA((160,)), pltpu.SemaphoreType.DMA((5,)),
+            pltpu.SemaphoreType.DMA((200,)), pltpu.SemaphoreType.DMA((200,)), pltpu.SemaphoreType.DMA((5,)),
         ],
         compiler_params=pltpu.CompilerParams(collective_id=1, has_side_effects=True),
         name="weight_gather",
@@ -777,8 +831,8 @@
 
 
 def scatter_kernel(
-    gq, go, gu, gd, sm_in, oq, oo, ou, od, sm_out,
-    AQ, AO, AU, AD, PQ, PO, PU, PD, FA, FO, FD, F1, F2, S1, S2, ZA, ZO, ZD, ZU, TA, TO, TD,
+    gw, sm_in, oq, oo, ou, od, sm_out,
+    AQ, AO, AU, AD, PQ, PO, PU, PD, FA, FD, F1, FO, F2, FV, S1, SO, S2, SV, ZA, ZD, ZU, ZO, ZV, TA, TD,
     hq, ho, hu, hd, s_p, s_x, s_y, s_below, s_above, s_a, s_b, s_sum, s_up, s_down, ssem, rsem, lsem,
 ):
     w, n, z, x, y, c, links = where_am_i()
@@ -812,22 +866,25 @@
     def rows_a(zp):
         return span(2 * rw * zp, 2 * rw)
 
+    main = rd - rw
+
     def slab(zp, layer, q, o, u, dn):
         rows = rows_a(zp)
         down = span(2 * rd * zp, 2 * rd)
-        return [(gq.at[layer, rows, j * d : (j + 1) * d], q.at[j, rows, :]) for j in range(3)] + [
-            (go.at[layer, rows, :], o.at[rows, :]),
-            (gd.at[layer, down, :], dn.at[down, :]),
-            (gu.at[layer, rows, :], u.at[rows, :]),
+        return [
+            [(gw.at[layer, j, rows, :], q.at[j, rows, :]) for j in range(3)],
+            [(gw.at[layer, 8 + zp], dn.at[down, :])],
+            [(gw.at[layer, 3, rows, :], o.at[rows, :])]
+            + [(gw.at[layer, 4 + j, rows, :], u.at[rows, j * d : (j + 1) * d]) for j in range(4)],
         ]
 
-    def own_loads(zp):
+    def own_loads(zp, part):
         return [
-            pltpu.make_async_copy(src, dst, lsem.at[k * ZN + zp])
-            for k, (src, dst) in enumerate(slab(zp, mine, AQ, AO, AU, AD))
+            pltpu.make_async_copy(src, dst, lsem.at[((0, 3, 4)[part] + k) * ZN + zp])
+            for k, (src, dst) in enumerate(slab(zp, mine, AQ, AO, AU, AD)[part])
         ]
 
-    swap = Hop("p", lambda zp: slab(zp, other, PQ, PO, PU, PD), 6)
+    swap = [Hop("p", lambda zp, p=p: slab(zp, other, PQ, PO, PU, PD)[p], (3, 1, 5)[p]) for p in range(3)]
 
     def cols_a(yp):
         return span(cn * yp, cn)
@@ -836,36 +893,58 @@
         return span(rw * (2 * zp + xp), rw)
 
     def rows_d(zp, xp):
-        return span(rd * (2 * zp + xp), rd)
+        return pl.ds(pl.multiple_of(rd * (2 * zp + xp), rw), main)
+
+    def rows_v(zp, xp):
+        return pl.ds(pl.multiple_of(rd * (2 * zp + xp) + main, rw), rw)
 
     def reg_a(zp, yp):
-        return AQ.at[:, rows_a(zp), cols_a(yp)], AO.at[rows_a(zp), cols_a(yp)]
+        return AQ.at[:, rows_a(zp), cols_a(yp)]
 
     def reg_d(zp, xp):
         return AD.at[rows_d(zp, xp), :]
 
     def u1(zp, yp):
-        return AU.at[rows_a(zp), span(cu * yp, half)]
+        return [AU.at[rows_a(zp), span(cu * yp, half)], AO.at[rows_a(zp), cols_a(yp)]]
 
     def u1_part(zp, xp, yp):
-        return AU.at[rows_x(zp, xp), span(cu * yp, half)]
-
-    def u2(zp, xp, yp):
-        return AU.at[rows_x(zp, xp), span(cu * yp + half, half)]
+        return [AU.at[rows_x(zp, xp), span(cu * yp, half)], AO.at[rows_x(zp, xp), cols_a(yp)]]
+
+    def u2(zp, xp):
+        rows = rows_x(zp, xp)
+        return [AU.at[rows, span(cu * yp + half, half)] for yp in range(2)] + [AD.at[rows_v(zp, xp), :]]
+
+    def u2_part(zp, xp, yp):
+        return [AU.at[rows_x(zp, xp), span(cu * yp + half, half)], AD.at[rows_v(zp, xp), cols_a(yp)]]
 
     def blk_u(zp):
-        return AU.at[rows_x(zp, x), span(cu * y, cu)]
-
-    y_a = Hop("y", lambda zp: list(zip(reg_a(zp, 1 - y), (FA.at[zp], FO.at[zp]))), 2)
+        rows = rows_x(zp, x)
+        return [AU.at[rows, span(cu * y, cu)], AO.at[rows, cols_a(y)], AD.at[rows_v(zp, x), cols_a(y)]]
+
+    def bufs_u1(zp):
+        return [F1.at[zp], FO.at[zp]]
+
+    def bufs_u2(zp):
+        return [F2.at[0, zp], F2.at[1, zp], FV.at[zp]]
+
+    def bufs_s1(zp):
+        return [S1.at[zp], SO.at[zp]]
+
+    def bufs_s2(zp):
+        return [S2.at[zp], SV.at[zp]]
+
+    y_a = Hop("y", lambda zp: [(reg_a(zp, 1 - y), FA.at[zp])], 1)
     x_d = Hop("x", lambda zp: [(reg_d(zp, 1 - x), FD.at[zp])], 1)
-    y_u1 = Hop("y", lambda zp: [(u1(zp, 1 - y), F1.at[zp])], 1)
-    x_u2 = Hop("x", lambda zp: [(u2(zp, 1 - x, yp), F2.at[yp, zp]) for yp in range(2)], 2)
-    x_u1 = Hop("x", lambda zp: [(u1_part(zp, 1 - x, y), S1.at[zp])], 1)
-    y_u2 = Hop("y", lambda zp: [(u2(zp, x, 1 - y), S2.at[zp])], 1)
-    last_a = Hop("x", lambda zp: [
-        (AQ.at[:, rows_x(z, 1 - x), cols_a(y)], TA), (AO.at[rows_x(z, 1 - x), cols_a(y)], TO)
-    ], 2)
+    y_u1 = Hop("y", lambda zp: list(zip(u1(zp, 1 - y), bufs_u1(zp))), 2)
+    x_u2 = Hop("x", lambda zp: list(zip(u2(zp, 1 - x), bufs_u2(zp))), 3)
+    x_u1 = Hop("x", lambda zp: list(zip(u1_part(zp, 1 - x, y), bufs_s1(zp))), 2)
+    y_u2 = Hop("y", lambda zp: list(zip(u2_part(zp, x, 1 - y), bufs_s2(zp))), 2)
+    last_a = Hop("x", lambda zp: [(AQ.at[:, rows_x(z, 1 - x), cols_a(y)], TA)], 1)
     last_d = Hop("y", lambda zp: [(AD.at[rows_d(z, x), cols_a(1 - y)], TD)], 1)
+
+    def add_all(dsts, srcs):
+        for dst, src in zip(dsts, srcs):
+            accumulate(dst, src, src.shape[0])
 
     class Line:
         def __init__(self, region, bufs):
@@ -916,9 +995,9 @@
             self.up(zp, "wait_send")
             self.down(zp, "wait_send")
 
-    line_a = Line(lambda zp: reg_a(zp, y), (ZA, ZO))
+    line_a = Line(lambda zp: (reg_a(zp, y),), (ZA,))
     line_d = Line(lambda zp: (reg_d(zp, x),), (ZD,))
-    line_u = Line(lambda zp: (blk_u(zp),), (ZU,))
+    line_u = Line(blk_u, (ZU, ZO, ZV))
 
     table = ((3, 3, 0, 0), (2, 0, 3, 1), (1, 2, 1, 2), (0, 1, 2, 3))
     order = [jnp.where(z == 0, t[0], jnp.where(z == 1, t[1], jnp.where(z == 2, t[2], t[3]))) for t in table]
@@ -932,68 +1011,81 @@
 
     small[0].start()
     for zp in order:
-        for cp in own_loads(zp):
-            cp.start()
-        swap.send(zp)
+        for part in range(3):
+            for cp in own_loads(zp, part):
+                cp.start()
+            swap[part].send(zp)
+
+    def arrive(zp, part):
+        for cp in own_loads(zp, part):
+            cp.wait()
+        swap[part].recv(zp)
 
     def open_slab(zp):
-        for cp in own_loads(zp):
-            cp.wait()
-        swap.recv(zp)
         rows = rows_a(zp)
+        arrive(zp, 0)
         for j in range(3):
             accumulate(AQ.at[j, rows, :], PQ.at[j, rows, :], 2 * rw)
-        accumulate(AO.at[rows, :], PO.at[rows, :], 2 * rw)
         y_a.send(zp)
         down = span(2 * rd * zp, 2 * rd)
+        arrive(zp, 1)
         accumulate(AD.at[down, :], PD.at[down, :], 2 * rd)
         x_d.send(zp)
+        arrive(zp, 2)
+        accumulate(AO.at[rows, :], PO.at[rows, :], 2 * rw)
         accumulate(AU.at[rows, :], PU.at[rows, :], 2 * rw, 16)
         y_u1.send(zp)
         x_u2.send(zp)
 
-    def middle(zp):
+    def mid_a(zp):
         y_a.recv(zp)
-        qa, oa = reg_a(zp, y)
         for j in range(3):
-            accumulate(qa.at[j], FA.at[zp, j], 2 * rw)
-        accumulate(oa, FO.at[zp], 2 * rw)
+            accumulate(reg_a(zp, y).at[j], FA.at[zp, j], 2 * rw)
         line_a.go(zp)
+
+    def mid_d(zp):
         x_d.recv(zp)
-        accumulate(reg_d(zp, x), FD.at[zp], rd)
+        accumulate(reg_d(zp, x), FD.at[zp], main)
         line_d.go(zp)
+
+    def mid_u(zp):
         y_u1.recv(zp)
-        accumulate(u1(zp, y), F1.at[zp], 2 * rw)
+        add_all(u1(zp, y), bufs_u1(zp))
         x_u1.send(zp)
         x_u2.recv(zp)
-        for yp in range(2):
-            accumulate(u2(zp, x, yp), F2.at[yp, zp], rw)
+        add_all(u2(zp, x), bufs_u2(zp))
         y_u2.send(zp)
 
     def close(zp):
         x_u1.recv(zp)
-        accumulate(u1_part(zp, x, y), S1.at[zp], rw)
+        add_all(u1_part(zp, x, y), bufs_s1(zp))
         y_u2.recv(zp)
-        accumulate(u2(zp, x, y), S2.at[zp], rw)
+        add_all(u2_part(zp, x, y), bufs_s2(zp))
         line_u.go(zp)
 
     open_slab(order[0])
+    mid_a(order[0])
     small[0].wait()
     s_a[...] = sm_in[...] + s_p[...]
     small[1].start()
     open_slab(order[1])
-    middle(order[0])
+    mid_d(order[0])
+    mid_u(order[0])
     small[1].wait()
     s_b[...] = s_a[...] + s_x[...]
     small[2].start()
     open_slab(order[2])
+    mid_a(order[1])
     close(order[0])
-    middle(order[1])
+    mid_d(order[1])
+    mid_u(order[1])
     small[2].wait()
     s_sum[...] = s_b[...] + s_y[...]
     open_slab(order[3])
+    mid_a(order[2])
     close(order[1])
-    middle(order[2])
+    mid_d(order[2])
+    mid_u(order[2])
 
     @pl.when(z > 0)
     def _():
@@ -1008,10 +1100,12 @@
         s_up[...] = s_sum[...] + s_below[...]
         small_up.start()
 
+    mid_a(order[3])
+    last_a.send(0)
     close(order[2])
-    middle(order[3])
-    last_a.send(0)
+    mid_d(order[3])
     last_d.send(0)
+    mid_u(order[3])
 
     @pl.when(z < ZN - 1)
     def _():
@@ -1041,27 +1135,30 @@
     ou[mine] = AU[rows, span(cu * y + half * c, half)].astype(F32)
     hu[...] = AU[rows, span(cu * y + half * (1 - c), half)].astype(F32)
     out[0].start()
+    keep, give = pick(AO[rows, cols_a(y)].astype(F32), cn // 2)
+    oo[mine] = keep
+    ho[...] = give
+    out[2].start()
     last_a.recv(0)
     for j in range(3):
         keep, give = pick(AQ[j, rows, cols_a(y)].astype(F32) + TA[j].astype(F32), cn // 2)
         oq[mine, j] = keep
         hq[j] = give
     out[1].start()
-    keep, give = pick(AO[rows, cols_a(y)].astype(F32) + TO[...].astype(F32), cn // 2)
-    oo[mine] = keep
-    ho[...] = give
-    out[2].start()
     last_d.recv(0)
     for k in range(rd // rw):
-        part = pl.ds(k * rw, rw)
+        part = slice(k * rw, (k + 1) * rw)
         here = span(rd * w + k * rw, rw)
-        keep, give = pick(AD[here, cols_a(y)].astype(F32) + TD[part, :].astype(F32), cn // 2)
+        total = AD[here, cols_a(y)].astype(F32)
+        if k * rw < main:
+            total = total + TD[part, :].astype(F32)
+        keep, give = pick(total, cn // 2)
         od[mine, part, :] = keep
         hd[part, :] = give
     out[3].start()
 
     for zp in range(ZN):
-        for hop in (swap, y_a, x_d, y_u1, x_u2, x_u1, y_u2):
+        for hop in (*swap, y_a, x_d, y_u1, x_u2, x_u1, y_u2):
             hop.drain(zp)
         for line in (line_a, line_d, line_u):
             line.drain(zp)
@@ -1081,12 +1178,10 @@
     assert net.next_send <= ssem.shape[0] and net.next_recv <= rsem.shape[0]
 
 
-def scatter_fast(big, small):
-    gq, go, gup, gdn = big
-    gb, gub, gn = small
-    d, ff = gup.shape[1:]
+def scatter_fast(gw, pack):
+    d = gw.shape[-1]
+    ff = 4 * d
     rw, cn, rd, cu = d // 8, d // 2, ff // 8, ff // 2
-    pack = jnp.concatenate([gb.reshape(-1, d), gub.reshape(-1, d), gn.reshape(-1, d)], axis=0)
     hbm = pl.BlockSpec(memory_space=pl.ANY)
     vmem = pl.BlockSpec(memory_space=pltpu.VMEM)
 
@@ -1100,20 +1195,20 @@
     full = [buf(3, d, d), buf(d, d), buf(d, ff), buf(ff, d)]
     oq, oo, ou, od, total = pl.pallas_call(
         scatter_kernel,
-        in_specs=[hbm] * 4 + [vmem],
+        in_specs=[hbm, vmem],
         out_specs=[vmem] * 5,
         out_shape=[jax.ShapeDtypeStruct((LAYERS,) + s, F32) for s in outs] + [jax.ShapeDtypeStruct(pack.shape, F32)],
         scratch_shapes=full + full + [
-            buf(ZN, 3, 2 * rw, cn), buf(ZN, 2 * rw, cn), buf(ZN, rd, d), buf(ZN, 2 * rw, cu // 2),
-            buf(2, ZN, rw, cu // 2), buf(ZN, rw, cu // 2), buf(ZN, rw, cu // 2),
-            buf(ZN + 1, 3, 2 * rw, cn), buf(ZN + 1, 2 * rw, cn), buf(ZN + 1, rd, d), buf(ZN + 1, rw, cu),
-            buf(3, rw, cn), buf(rw, cn), buf(rd, cn),
+            buf(ZN, 3, 2 * rw, cn), buf(ZN, rd - rw, d), buf(ZN, 2 * rw, cu // 2), buf(ZN, 2 * rw, cn),
+            buf(2, ZN, rw, cu // 2), buf(ZN, rw, d), buf(ZN, rw, cu // 2), buf(ZN, rw, cn),
+            buf(ZN, rw, cu // 2), buf(ZN, rw, cn), buf(ZN + 1, 3, 2 * rw, cn), buf(ZN + 1, rd - rw, d),
+            buf(ZN + 1, rw, cu), buf(ZN + 1, rw, cn), buf(ZN + 1, rw, cn), buf(3, rw, cn), buf(rd - rw, cn),
         ] + [wide(*s) for s in outs] + [wide(*pack.shape)] * 10 + [
-            pltpu.SemaphoreType.DMA((140,)), pltpu.SemaphoreType.DMA((120,)), pltpu.SemaphoreType.DMA((6 * ZN,)),
+            pltpu.SemaphoreType.DMA((180,)), pltpu.SemaphoreType.DMA((160,)), pltpu.SemaphoreType.DMA((9 * ZN,)),
         ],
         compiler_params=pltpu.CompilerParams(collective_id=2, has_side_effects=True, vmem_limit_bytes=VMEM_LIMIT),
         name="gradient_scatter",
-    )(gq, go, gup, gdn, pack)
+    )(gw, pack)
     w, n = lax.axis_index("wide"), lax.axis_index("narrow")
     gb = lax.dynamic_slice(total[0:8].reshape(2, 4, d), (0, n, w * rw), (2, 1, rw))
     gn = lax.dynamic_slice(total[16:24].reshape(2, 4, d), (0, n, w * rw), (2, 1, rw))
@@ -1136,10 +1231,11 @@
     return lax.psum_scatter(low.astype(F32), "wide", scatter_dimension=row_axis, tiled=True)
 
 
-def scatter_grads(big, small):
-    gq, go, gup, gdn = big
-    gq = jnp.moveaxis(gq.reshape(gq.shape[:2] + (3, -1)), 2, 1)
-    gb, gub, gn = small
+def scatter_grads(gw, pack):
+    d = gw.shape[-1]
+    gq, go, gdn = gw[:, 0:3], gw[:, 3], gw[:, 8:].reshape(LAYERS, -1, d)
+    gup = jnp.moveaxis(gw[:, 4:8], 1, 2).reshape(LAYERS, d, -1)
+    gb, gub, gn = pack[0:8].reshape(LAYERS, 4, d), pack[8:16].reshape(LAYERS, -1), pack[16:24].reshape(LAYERS, 4, d)
     big = (scatter_two(gq, 2, 3), scatter_two(go, 1, 2), scatter_two(gup, 1, 2), scatter_two(gdn, 1, 2))
     gub = lax.psum_scatter(gub, ("wide", "narrow"), scatter_dimension=1, tiled=True)
 
@@ -1161,9 +1257,9 @@
     gather = gather_fast if near else gather_weights
     weights = gather((qkv_weight, out_weight, up_weight, down_weight, biases, up_bias, norm_params))
     text_out, mem_out, kept = forward_local(text, mem, cnt, lens, weights)
-    text_grad, mem_grad, grads, small = backward_local(cot, cot_mem, cnt, lens, kept, weights)
+    text_grad, mem_grad, rhs, small = backward_local(cot, cot_mem, cnt, lens, kept, weights)
     scatter = scatter_fast if near else scatter_grads
-    grads = scatter(weight_grads(kept, grads), small)
+    grads = scatter(weight_grads(kept[0], rhs), small)
     return (text_out[:, None], mem_out[:, None], text_grad[:, None], mem_grad[:, None]) + grads
 
 

time: 502 us -> 465 us (0.926); the launches traced: 494 us -> 464 us
  matrix products: 47.4 us -> 0 us
  Pallas kernels: 414 us -> 430 us
    dot_general x4 -> x0, matrix products: 47.4 us -> none  [product(): lax.dot_general(lhs, rhs, dims, preferred_element_type=F32).astype(BF)]
    pallas_call x1 -> x2, Pallas kernels: 149 us -> 180 us  [the longest x1 135 us: scatter_fast(): pl.pallas_call(scatter_kernel, in_specs=[hbm, vmem], out_specs=[vmem] * 5...]
    pallas_call x1, Pallas kernels: 133 us -> 119 us  [gather_fast(): pl.pallas_call(gather_kernel, in_specs=[vmem] * 5, out_specs=[hbm] * 5, o...]
    unnamed x46 -> x16, local copies, waits for them, and re-layouts: 20.2 us -> 23.2 us
where the time goes in v5:
time: 465 us; the launch traced here: 464 us
  Pallas kernels  430 us (92%)
  local copies, waits for them, and re-layouts  30.2 us (6%)
    pallas_call x1, Pallas kernels, scatter_fast(): pl.pallas_call(scatter_kernel, in_specs=[hbm, vmem], out_specs=[vmem] * 5...  135 us
    pallas_call x1, Pallas kernels, gather_fast(): pl.pallas_call(gather_kernel, in_specs=[vmem] * 5, out_specs=[hbm] * 5, o...  119 us
    pallas_call x1, Pallas kernels, forward_local(): pl.pallas_call(fwd_kernel, grid=(SEGS, LAYERS), in_specs=[smem, smem, pl....  67.2 us
    pallas_call x1, Pallas kernels, backward_local(): pl.pallas_call(bwd_kernel, grid=(SEGS, LAYERS), in_specs=[smem, smem, pl....  64 us
    pallas_call x1, Pallas kernels, weight_grads(): pl.pallas_call(product_kernel, grid=(LAYERS, TILES), in_specs=[pl.BlockSp...  44.8 us
    unnamed x16, local copies, waits for them, and re-layouts  23.2 us

profile of v5, /device:TPU:0, one launch (start us, length us, event | category | flops | bytes accessed | tf_op | source)
XLA Modules:
  0.0 464.2 jit_solution(7758790111914838691)
XLA Ops:
  0.6 2.6 copy.45
  3.2 0.8 bitcast_convert_fusion
  4.0 0.7 pad_maximum_fusion.mem0
  4.8 1.9 copy.26.d_in
  6.7 0.1 pad.13.clone
  6.7 0.8 maximum_maximum_fusion
  7.5 0.6 pad_convert_fusion.1.s_in
  8.1 119.0 %weight_gather.1 = (bf16[2,3,768,768]{3,2,1,0:T(8,128)(2,1)}, bf16[2,768,768]{2,1,0:T(8,128)(2,1)}, bf16[2,768,3072]{2,1,0:T(8,128)(2,1)}, bf16[2,3072,768]{2,1,0:T(8,128)(2,1)}, f32[4,2,2,2,8,128]{5,4,3,2,1,0:T(8,128)}) custom-call(bf16[2,3,96,192]{3,2,1,0:T(8,128)(2,1)} %q_in.1, bf16[2,96,192]{2,1,0:T(8,128)(2,1)} %o_in.1, bf16[2,96,768]{2,1,0:T(8,128)(2,1)} %u_in.1, ...), custom_call_target="tpu_custom_call" | custom-call | tf_op jit(solution)/shard_map/weight_gather/pallas_call | solution.py:798
  127.1 1.0 copy.46
  128.1 0.7 slice.38.bias
  128.8 0.9 slice.49
  129.8 0.7 broadcast_in_dim_reshape.3.ubias
  130.5 0.7 slice.41.norm
  131.2 0.0 copy-start
  131.2 67.2 %rmt_forward.1 = (bf16[2,4,108,768]{3,2,1,0:T(8,128)(2,1)}, f32[2,24,768]{2,1,0:T(8,128)}, bf16[2,1024,5376]{2,1,0:T(8,128)(2,1)}, bf16[2,1024,2304]{2,1,0:T(8,1...) custom-call(s32[2]{0:T(128)} %bitcast.43, ...), custom_call_target="tpu_custom_call" | custom-call | tf_op jit(solution)/shard_map/rmt_forward/pallas_call | solution.py:200
  198.3 3.1 copy.31
  201.4 0.9 fusion
  202.3 0.6 copy.32
  203.0 2.6 copy.44
  205.6 0.0 copy-done
  205.6 0.7 pad_convert_fusion.gm0
  206.3 64.0 %rmt_backward.1 = (bf16[2,4,108,768]{3,2,1,0:T(8,128)(2,1)}, f32[2,24,768]{2,1,0:T(8,128)}, bf16[2,1024,6912]{2,1,0:T(8,128)(2,1)}, f32[24,768]{1,0:T(8,128)}) custom-call(s32[2]{0:T(128)} %bitcast.44, s32[2]{0:T(128)} %bitcast.46, bf16[2,4,108,768]{3,2,1,0:T(8,128)(2,1)} %bitcast.35, f32[2,24,768]{2,1,0:T(8,128)} %pad_convert_fusion.gm0, ...), custom_call_target="tpu_custom_call" | custom-call | tf_op jit(solution)/shard_map/rmt_backward/pallas_call | solution.py:389
  270.3 3.1 copy.33
  273.4 0.9 fusion.1
  274.3 0.6 copy.34
  274.9 44.8 %weight_products.1.gw = bf16[2,12,768,768]{3,2,1,0:T(8,128)(2,1)} custom-call(bf16[2,1024,5376]{2,1,0:T(8,128)(2,1)} %get-tuple-element.49.lhs, bf16[2,1024,6912]{2,1,0:T(8,128)(2,1)} %get-tuple-element.50.rhs), custom_call_target="tpu_custom_call" | custom-call | tf_op jit(solution)/shard_map/weight_products/pallas_call | solution.py:441
  319.7 134.7 %gradient_scatter.1 = (f32[2,3,96,192]{3,2,1,0:T(8,128)}, f32[2,96,192]{2,1,0:T(8,128)}, f32[2,96,768]{2,1,0:T(8,128)}, f32[2,384,192]{2,1,0:T(8,128)}, f32[24,768]{1,0:T(8,128)}) custom-call(bf16[2,12,768,768]{3,2,1,0:T(8,128)(2,1)} %weight_products.1.gw, f32[24,768]{1,0:T(8,128)} %get-tuple-element.51.sm_in), custom_call_target="tpu_custom_call" | custom-call | tf_op jit(solution)/shard_map/gradient_scatter/pallas_call | solution.py:1196
  454.4 2.2 copy.35
  456.6 0.8 fusion.3
  457.5 0.6 constant_dynamic-slice_fusion
  458.1 0.6 constant_dynamic-slice_fusion.1
  458.8 1.9 copy.52
  460.7 1.6 copy.53
  462.3 1.9 copy.54
  (9 shorter events, 0.1 us)
Async XLA Ops:
  131.2 74.4 %copy-start = (bf16[2,1,10,768]{3,0,2,1:T(2,128)(2,1)S(1)}, bf16[2,1,10,768]{3,0,2,1:T(2,128)(2,1)}, u32[]{:S(2)}) copy-start(bf16[2,1,10,768]{3,0,2,1:T(2,128)(2,1)} %param.18) | copy-start | bytes 92164

commit v6 on v5

--- a/solution.py
+++ b/solution.py
@@ -427,31 +427,35 @@
 TILES = 12
 
 
-def product_kernel(lhs, rhs, out):
+def product_kernel(ids, lhs, rhs, out):
     out[0, 0] = dot_lt(lhs[0], rhs[0]).astype(BF)
 
 
-def weight_grads(lhs, rhs):
+def weight_grads(lhs, rhs, layers):
     d = rhs.shape[-1] // 9
     total = lhs.shape[1]
-
-    def left(l, t):
-        return (l, 0, jnp.where(t < 3, 0, jnp.where(t < 4, 1, jnp.where(t < 8, 2, t - 5))))
+    count = layers.shape[0]
+
+    def left(l, t, ids):
+        return (ids[l], 0, jnp.where(t < 3, 0, jnp.where(t < 4, 1, jnp.where(t < 8, 2, t - 5))))
 
     return pl.pallas_call(
         product_kernel,
-        grid=(LAYERS, TILES),
-        in_specs=[
-            pl.BlockSpec((1, total, d), left),
-            pl.BlockSpec((1, total, d), lambda l, t: (l, 0, jnp.minimum(t, 8))),
-        ],
-        out_specs=pl.BlockSpec((1, 1, d, d), lambda l, t: (l, t, 0, 0)),
-        out_shape=jax.ShapeDtypeStruct((LAYERS, TILES, d, d), BF),
+        grid_spec=pltpu.PrefetchScalarGridSpec(
+            num_scalar_prefetch=1,
+            grid=(count, TILES),
+            in_specs=[
+                pl.BlockSpec((1, total, d), left),
+                pl.BlockSpec((1, total, d), lambda l, t, ids: (ids[l], 0, jnp.minimum(t, 8))),
+            ],
+            out_specs=pl.BlockSpec((1, 1, d, d), lambda l, t, ids: (l, t, 0, 0)),
+        ),
+        out_shape=jax.ShapeDtypeStruct((count, TILES, d, d), BF),
         compiler_params=pltpu.CompilerParams(
             dimension_semantics=("arbitrary", "arbitrary"), vmem_limit_bytes=VMEM_LIMIT
         ),
         name="weight_products",
-    )(lhs, rhs)
+    )(layers, lhs, rhs)
 
 
 MESH = pl.DeviceIdType.MESH
@@ -831,14 +835,14 @@
 
 
 def scatter_kernel(
-    gw, sm_in, oq, oo, ou, od, sm_out,
-    AQ, AO, AU, AD, PQ, PO, PU, PD, FA, FD, F1, FO, F2, FV, S1, SO, S2, SV, ZA, ZD, ZU, ZO, ZV, TA, TD,
+    gw, lhs, rhs, sm_in, oq, oo, ou, od, sm_out,
+    AT, AD, RH, LT, LB, FA, FD, F1, FO, F2, FV, S1, SO, S2, SV, ZA, ZD, ZU, ZO, ZV, TA, TD,
     hq, ho, hu, hd, s_p, s_x, s_y, s_below, s_above, s_a, s_b, s_sum, s_up, s_down, ssem, rsem, lsem,
 ):
     w, n, z, x, y, c, links = where_am_i()
     mine, other = c, 1 - c
     net = Net(ssem, rsem, links)
-    d, ff = AO.shape[1], AU.shape[1]
+    d, ff = AT.shape[2], AD.shape[0]
     rw, cn = d // 8, d // 2
     rd, cu = ff // 8, ff // 2
     half = cu // 2
@@ -868,23 +872,54 @@
 
     main = rd - rw
 
-    def slab(zp, layer, q, o, u, dn):
+    def down(zp):
+        return span(d * zp, d)
+
+    swap = [
+        Hop("p", lambda zp: [(gw.at[0, 0:3, rows_a(zp), :], AT.at[0:3, rows_a(zp), :])], 1),
+        Hop("p", lambda zp: [(gw.at[0, 8 + zp], AD.at[down(zp), :])], 1),
+        Hop("p", lambda zp: [(gw.at[0, 3:8, rows_a(zp), :], AT.at[3:8, rows_a(zp), :])], 1),
+    ]
+
+    def right(t):
+        return pltpu.make_async_copy(rhs.at[mine, :, t * d : (t + 1) * d], RH.at[t], lsem.at[t])
+
+    def left(j):
+        return pltpu.make_async_copy(lhs.at[mine, :, j * d : (j + 1) * d], LB.at[j], lsem.at[9 + j])
+
+    def left_g(v, zp):
+        slot = (v + 3) % 4
+        return pltpu.make_async_copy(lhs.at[mine, :, span(d * (3 + zp), d)], LB.at[slot], lsem.at[12 + v])
+
+    def turn(j):
+        step = 256
+
+        def body(k, carry):
+            part = pl.ds(pl.multiple_of(k * step, step), step)
+            LT[j, :, part] = LB[j, part, :].T
+            return carry
+
+        lax.fori_loop(0, LB.shape[1] // step, body, 0)
+
+    def products(first, last, zp):
         rows = rows_a(zp)
-        down = span(2 * rd * zp, 2 * rd)
-        return [
-            [(gw.at[layer, j, rows, :], q.at[j, rows, :]) for j in range(3)],
-            [(gw.at[layer, 8 + zp], dn.at[down, :])],
-            [(gw.at[layer, 3, rows, :], o.at[rows, :])]
-            + [(gw.at[layer, 4 + j, rows, :], u.at[rows, j * d : (j + 1) * d]) for j in range(4)],
-        ]
-
-    def own_loads(zp, part):
-        return [
-            pltpu.make_async_copy(src, dst, lsem.at[((0, 3, 4)[part] + k) * ZN + zp])
-            for k, (src, dst) in enumerate(slab(zp, mine, AQ, AO, AU, AD)[part])
-        ]
-
-    swap = [Hop("p", lambda zp, p=p: slab(zp, other, PQ, PO, PU, PD)[p], (3, 1, 5)[p]) for p in range(3)]
+
+        def body(t, carry):
+            j = jnp.where(t < 3, 0, jnp.where(t < 4, 1, 2))
+            AT[t, rows, :] = (AT[t, rows, :].astype(F32) + dot(LT[j, rows, :], RH[t])).astype(BF)
+            return carry
+
+        lax.fori_loop(first, last, body, 0)
+
+    def products_down(v, zp):
+        rows = down(zp)
+
+        def body(k, carry):
+            cols = pl.ds(pl.multiple_of(k * cn, cn), cn)
+            AD[rows, cols] = (AD[rows, cols].astype(F32) + dot_lt(LB[(v + 3) % 4], RH[8, :, cols])).astype(BF)
+            return carry
+
+        lax.fori_loop(0, 2, body, 0)
 
     def cols_a(yp):
         return span(cn * yp, cn)
@@ -899,27 +934,27 @@
         return pl.ds(pl.multiple_of(rd * (2 * zp + xp) + main, rw), rw)
 
     def reg_a(zp, yp):
-        return AQ.at[:, rows_a(zp), cols_a(yp)]
+        return AT.at[0:3, rows_a(zp), cols_a(yp)]
 
     def reg_d(zp, xp):
         return AD.at[rows_d(zp, xp), :]
 
     def u1(zp, yp):
-        return [AU.at[rows_a(zp), span(cu * yp, half)], AO.at[rows_a(zp), cols_a(yp)]]
+        return [AT.at[4 + 2 * yp, rows_a(zp), :], AT.at[3, rows_a(zp), cols_a(yp)]]
 
     def u1_part(zp, xp, yp):
-        return [AU.at[rows_x(zp, xp), span(cu * yp, half)], AO.at[rows_x(zp, xp), cols_a(yp)]]
+        return [AT.at[4 + 2 * yp, rows_x(zp, xp), :], AT.at[3, rows_x(zp, xp), cols_a(yp)]]
 
     def u2(zp, xp):
         rows = rows_x(zp, xp)
-        return [AU.at[rows, span(cu * yp + half, half)] for yp in range(2)] + [AD.at[rows_v(zp, xp), :]]
+        return [AT.at[5 + 2 * yp, rows, :] for yp in range(2)] + [AD.at[rows_v(zp, xp), :]]
 
     def u2_part(zp, xp, yp):
-        return [AU.at[rows_x(zp, xp), span(cu * yp + half, half)], AD.at[rows_v(zp, xp), cols_a(yp)]]
+        return [AT.at[5 + 2 * yp, rows_x(zp, xp), :], AD.at[rows_v(zp, xp), cols_a(yp)]]
 
     def blk_u(zp):
         rows = rows_x(zp, x)
-        return [AU.at[rows, span(cu * y, cu)], AO.at[rows, cols_a(y)], AD.at[rows_v(zp, x), cols_a(y)]]
+        return [AT.at[pl.ds(4 + 2 * y, 2), rows, :], AT.at[3, rows, cols_a(y)], AD.at[rows_v(zp, x), cols_a(y)]]
 
     def bufs_u1(zp):
         return [F1.at[zp], FO.at[zp]]
@@ -939,7 +974,7 @@
     x_u2 = Hop("x", lambda zp: list(zip(u2(zp, 1 - x), bufs_u2(zp))), 3)
     x_u1 = Hop("x", lambda zp: list(zip(u1_part(zp, 1 - x, y), bufs_s1(zp))), 2)
     y_u2 = Hop("y", lambda zp: list(zip(u2_part(zp, x, 1 - y), bufs_s2(zp))), 2)
-    last_a = Hop("x", lambda zp: [(AQ.at[:, rows_x(z, 1 - x), cols_a(y)], TA)], 1)
+    last_a = Hop("x", lambda zp: [(AT.at[0:3, rows_x(z, 1 - x), cols_a(y)], TA)], 1)
     last_d = Hop("y", lambda zp: [(AD.at[rows_d(z, x), cols_a(1 - y)], TD)], 1)
 
     def add_all(dsts, srcs):
@@ -1010,30 +1045,45 @@
     small_down = net.copy("down", s_down, s_above, net.sends(1), net.recvs(1))
 
     small[0].start()
+    left(0).start()
+    for t in range(3):
+        right(t).start()
+    left_g(0, order[0]).start()
+    right(8).start()
+    for j in (1, 2):
+        left(j).start()
+    for t in range(3, 8):
+        right(t).start()
     for zp in order:
-        for part in range(3):
-            for cp in own_loads(zp, part):
-                cp.start()
-            swap[part].send(zp)
-
-    def arrive(zp, part):
-        for cp in own_loads(zp, part):
-            cp.wait()
-        swap[part].recv(zp)
-
-    def open_slab(zp):
-        rows = rows_a(zp)
-        arrive(zp, 0)
-        for j in range(3):
-            accumulate(AQ.at[j, rows, :], PQ.at[j, rows, :], 2 * rw)
+        for part in swap:
+            part.send(zp)
+
+    def open_slab(v):
+        zp = order[v]
+        if v == 0:
+            left(0).wait()
+            turn(0)
+            for t in range(3):
+                right(t).wait()
+        swap[0].recv(zp)
+        products(0, 3, zp)
         y_a.send(zp)
-        down = span(2 * rd * zp, 2 * rd)
-        arrive(zp, 1)
-        accumulate(AD.at[down, :], PD.at[down, :], 2 * rd)
+        left_g(v, zp).wait()
+        if v == 0:
+            right(8).wait()
+        swap[1].recv(zp)
+        products_down(v, zp)
         x_d.send(zp)
-        arrive(zp, 2)
-        accumulate(AO.at[rows, :], PO.at[rows, :], 2 * rw)
-        accumulate(AU.at[rows, :], PU.at[rows, :], 2 * rw, 16)
+        if v == 0:
+            left_g(1, order[1]).start()
+            for j in (1, 2):
+                left(j).wait()
+                turn(j)
+                left_g(j + 1, order[j + 1]).start()
+            for t in range(3, 8):
+                right(t).wait()
+        swap[2].recv(zp)
+        products(3, 8, zp)
         y_u1.send(zp)
         x_u2.send(zp)
 
@@ -1063,25 +1113,25 @@
         add_all(u2_part(zp, x, y), bufs_s2(zp))
         line_u.go(zp)
 
-    open_slab(order[0])
+    open_slab(0)
     mid_a(order[0])
     small[0].wait()
     s_a[...] = sm_in[...] + s_p[...]
     small[1].start()
-    open_slab(order[1])
+    open_slab(1)
     mid_d(order[0])
     mid_u(order[0])
     small[1].wait()
     s_b[...] = s_a[...] + s_x[...]
     small[2].start()
-    open_slab(order[2])
+    open_slab(2)
     mid_a(order[1])
     close(order[0])
     mid_d(order[1])
     mid_u(order[1])
     small[2].wait()
     s_sum[...] = s_b[...] + s_y[...]
-    open_slab(order[3])
+    open_slab(3)
     mid_a(order[2])
     close(order[1])
     mid_d(order[2])
@@ -1132,16 +1182,16 @@
         for src, dst in ((hu, ou), (hq, oq), (ho, oo), (hd, od))
     ]
     rows = rows_x(z, x)
-    ou[mine] = AU[rows, span(cu * y + half * c, half)].astype(F32)
-    hu[...] = AU[rows, span(cu * y + half * (1 - c), half)].astype(F32)
+    ou[mine] = AT[4 + 2 * y + c, rows, :].astype(F32)
+    hu[...] = AT[5 + 2 * y - c, rows, :].astype(F32)
     out[0].start()
-    keep, give = pick(AO[rows, cols_a(y)].astype(F32), cn // 2)
+    keep, give = pick(AT[3, rows, cols_a(y)].astype(F32), cn // 2)
     oo[mine] = keep
     ho[...] = give
     out[2].start()
     last_a.recv(0)
     for j in range(3):
-        keep, give = pick(AQ[j, rows, cols_a(y)].astype(F32) + TA[j].astype(F32), cn // 2)
+        keep, give = pick(AT[j, rows, cols_a(y)].astype(F32) + TA[j].astype(F32), cn // 2)
         oq[mine, j] = keep
         hq[j] = give
     out[1].start()
@@ -1178,7 +1228,7 @@
     assert net.next_send <= ssem.shape[0] and net.next_recv <= rsem.shape[0]
 
 
-def scatter_fast(gw, pack):
+def scatter_fast(gw, lhs, rhs, pack):
     d = gw.shape[-1]
     ff = 4 * d
     rw, cn, rd, cu = d // 8, d // 2, ff // 8, ff // 2
@@ -1192,27 +1242,28 @@
         return pltpu.VMEM(shape, F32)
 
     outs = [(3, rw, cn // 2), (rw, cn // 2), (rw, cu // 2), (rd, cn // 2)]
-    full = [buf(3, d, d), buf(d, d), buf(d, ff), buf(ff, d)]
-    oq, oo, ou, od, total = pl.pallas_call(
+    total = lhs.shape[1]
+    full = [buf(8, d, d), buf(ff, d), buf(9, total, d), buf(3, d, total), buf(4, total, d)]
+    oq, oo, ou, od, summed = pl.pallas_call(
         scatter_kernel,
-        in_specs=[hbm, vmem],
+        in_specs=[hbm, hbm, hbm, vmem],
         out_specs=[vmem] * 5,
         out_shape=[jax.ShapeDtypeStruct((LAYERS,) + s, F32) for s in outs] + [jax.ShapeDtypeStruct(pack.shape, F32)],
-        scratch_shapes=full + full + [
+        scratch_shapes=full + [
             buf(ZN, 3, 2 * rw, cn), buf(ZN, rd - rw, d), buf(ZN, 2 * rw, cu // 2), buf(ZN, 2 * rw, cn),
             buf(2, ZN, rw, cu // 2), buf(ZN, rw, d), buf(ZN, rw, cu // 2), buf(ZN, rw, cn),
             buf(ZN, rw, cu // 2), buf(ZN, rw, cn), buf(ZN + 1, 3, 2 * rw, cn), buf(ZN + 1, rd - rw, d),
-            buf(ZN + 1, rw, cu), buf(ZN + 1, rw, cn), buf(ZN + 1, rw, cn), buf(3, rw, cn), buf(rd - rw, cn),
+            buf(ZN + 1, 2, rw, cu // 2), buf(ZN + 1, rw, cn), buf(ZN + 1, rw, cn), buf(3, rw, cn), buf(rd - rw, cn),
         ] + [wide(*s) for s in outs] + [wide(*pack.shape)] * 10 + [
-            pltpu.SemaphoreType.DMA((180,)), pltpu.SemaphoreType.DMA((160,)), pltpu.SemaphoreType.DMA((9 * ZN,)),
+            pltpu.SemaphoreType.DMA((180,)), pltpu.SemaphoreType.DMA((160,)), pltpu.SemaphoreType.DMA((16,)),
         ],
         compiler_params=pltpu.CompilerParams(collective_id=2, has_side_effects=True, vmem_limit_bytes=VMEM_LIMIT),
         name="gradient_scatter",
-    )(gw, pack)
+    )(gw, lhs, rhs, pack)
     w, n = lax.axis_index("wide"), lax.axis_index("narrow")
-    gb = lax.dynamic_slice(total[0:8].reshape(2, 4, d), (0, n, w * rw), (2, 1, rw))
-    gn = lax.dynamic_slice(total[16:24].reshape(2, 4, d), (0, n, w * rw), (2, 1, rw))
-    gub = lax.dynamic_slice(total[8:16].reshape(2, ff), (0, (4 * w + n) * rw), (2, rw))
+    gb = lax.dynamic_slice(summed[0:8].reshape(2, 4, d), (0, n, w * rw), (2, 1, rw))
+    gn = lax.dynamic_slice(summed[16:24].reshape(2, 4, d), (0, n, w * rw), (2, 1, rw))
+    gub = lax.dynamic_slice(summed[8:16].reshape(2, ff), (0, (4 * w + n) * rw), (2, rw))
     return oq, oo, ou, od, gb, gub, gn
 
 
@@ -1258,8 +1309,11 @@
     weights = gather((qkv_weight, out_weight, up_weight, down_weight, biases, up_bias, norm_params))
     text_out, mem_out, kept = forward_local(text, mem, cnt, lens, weights)
     text_grad, mem_grad, rhs, small = backward_local(cot, cot_mem, cnt, lens, kept, weights)
-    scatter = scatter_fast if near else scatter_grads
-    grads = scatter(weight_grads(kept[0], rhs), small)
+    if near:
+        other = 1 - lax.rem(lax.axis_index("narrow"), 2)
+        grads = scatter_fast(weight_grads(kept[0], rhs, other[None]), kept[0], rhs, small)
+    else:
+        grads = scatter_grads(weight_grads(kept[0], rhs, jnp.arange(LAYERS, dtype=jnp.int32)), small)
     return (text_out[:, None], mem_out[:, None], text_grad[:, None], mem_grad[:, None]) + grads
 
 

time: 465 us -> 446 us (0.959)
  Pallas kernels: 430 us -> 410 us
    pallas_call x2, Pallas kernels: 180 us -> 160 us  [the longest x1 137 us: scatter_fast(): pl.pallas_call(scatter_kernel, in_specs=[hbm, hbm, hbm, vmem], out_specs=...]
where the time goes in v6:
time: 446 us; the launch traced here: 445 us
  Pallas kernels  410 us (92%)
  local copies, waits for them, and re-layouts  30.2 us (7%)
    pallas_call x1, Pallas kernels, scatter_fast(): pl.pallas_call(scatter_kernel, in_specs=[hbm, hbm, hbm, vmem], out_specs=...  137 us
    pallas_call x1, Pallas kernels, gather_fast(): pl.pallas_call(gather_kernel, in_specs=[vmem] * 5, out_specs=[hbm] * 5, o...  119 us
    pallas_call x1, Pallas kernels, forward_local(): pl.pallas_call(fwd_kernel, grid=(SEGS, LAYERS), in_specs=[smem, smem, pl....  67.1 us
    pallas_call x1, Pallas kernels, backward_local(): pl.pallas_call(bwd_kernel, grid=(SEGS, LAYERS), in_specs=[smem, smem, pl....  64 us
    pallas_call x1, Pallas kernels, weight_grads(): pl.pallas_call(product_kernel, grid_spec=pltpu.PrefetchScalarGridSpec(num...  23.5 us
    unnamed x16, local copies, waits for them, and re-layouts  23.2 us

profile of v6, /device:TPU:0, one launch (start us, length us, event | category | flops | bytes accessed | tf_op | source)
XLA Modules:
  0.0 444.8 jit_solution(9169950938993198170)
XLA Ops:
  0.6 2.6 copy.45
  3.2 0.8 bitcast_convert_fusion
  4.0 0.7 pad_maximum_fusion.mem0
  4.8 1.9 copy.26.d_in
  6.7 0.1 pad.13.clone
  6.7 0.8 maximum_maximum_fusion
  7.5 0.6 pad_convert_fusion.1.s_in
  8.1 118.9 %weight_gather.1 = (bf16[2,3,768,768]{3,2,1,0:T(8,128)(2,1)}, bf16[2,768,768]{2,1,0:T(8,128)(2,1)}, bf16[2,768,3072]{2,1,0:T(8,128)(2,1)}, bf16[2,3072,768]{2,1,0:T(8,128)(2,1)}, f32[4,2,2,2,8,128]{5,4,3,2,1,0:T(8,128)}) custom-call(bf16[2,3,96,192]{3,2,1,0:T(8,128)(2,1)} %q_in.1, bf16[2,96,192]{2,1,0:T(8,128)(2,1)} %o_in.1, bf16[2,96,768]{2,1,0:T(8,128)(2,1)} %u_in.1, ...), custom_call_target="tpu_custom_call" | custom-call | tf_op jit(solution)/shard_map/weight_gather/pallas_call | solution.py:802
  127.0 1.0 copy.46
  128.0 0.7 slice.38.bias
  128.7 0.9 slice.49
  129.6 0.7 broadcast_in_dim_reshape.3.ubias
  130.4 0.7 slice.41.norm
  131.1 0.0 copy-start
  131.1 67.1 %rmt_forward.1 = (bf16[2,4,108,768]{3,2,1,0:T(8,128)(2,1)}, f32[2,24,768]{2,1,0:T(8,128)}, bf16[2,1024,5376]{2,1,0:T(8,128)(2,1)}, bf16[2,1024,2304]{2,1,0:T(8,1...) custom-call(s32[2]{0:T(128)} %bitcast.44, ...), custom_call_target="tpu_custom_call" | custom-call | tf_op jit(solution)/shard_map/rmt_forward/pallas_call | solution.py:200
  198.2 3.1 copy.31
  201.3 0.9 fusion
  202.2 0.6 copy.32
  202.8 2.6 copy.44
  205.4 0.0 copy-done
  205.4 0.7 pad_convert_fusion.gm0
  206.1 64.0 %rmt_backward.1 = (bf16[2,4,108,768]{3,2,1,0:T(8,128)(2,1)}, f32[2,24,768]{2,1,0:T(8,128)}, bf16[2,1024,6912]{2,1,0:T(8,128)(2,1)}, f32[24,768]{1,0:T(8,128)}) custom-call(s32[2]{0:T(128)} %bitcast.45, s32[2]{0:T(128)} %bitcast.47, bf16[2,4,108,768]{3,2,1,0:T(8,128)(2,1)} %bitcast.36, f32[2,24,768]{2,1,0:T(8,128)} %pad_convert_fusion.gm0, ...), custom_call_target="tpu_custom_call" | custom-call | tf_op jit(solution)/shard_map/rmt_backward/pallas_call | solution.py:389
  270.1 3.1 copy.33
  273.2 0.9 fusion.1
  274.1 0.6 copy.34
  274.8 23.5 %weight_products.1.gw = bf16[1,12,768,768]{3,2,1,0:T(8,128)(2,1)} custom-call(s32[1]{0:T(128)} %bitcast.15.ids, bf16[2,1024,5376]{2,1,0:T(8,128)(2,1)} %get-tuple-element.49.lhs, bf16[2,1024,6912]{2,1,0:T(8,128)(2,1)} %get-tuple-element.50.rhs), custom_call_target="tpu_custom_call" | custom-call | tf_op jit(solution)/shard_map/weight_products/pallas_call | solution.py:442
  298.3 136.7 %gradient_scatter.1 = (f32[2,3,96,192]{3,2,1,0:T(8,128)}, f32[2,96,192]{2,1,0:T(8,128)}, f32[2,96,768]{2,1,0:T(8,128)}, f32[2,384,192]{2,1,0:T(8,128)}, f32[24,768]{1,0:T(8,128)}) custom-call(bf16[1,12,768,768]{3,2,1,0:T(8,128)(2,1)} %weight_products.1.gw, bf16[2,1024,5376]{2,1,0:T(8,128)(2,1)} %get-tuple-element.49.lhs, ...), custom_call_target="tpu_custom_call" | custom-call | tf_op jit(solution)/shard_map/gradient_scatter/pallas_call | solution.py:1247
  435.0 2.2 copy.35
  437.2 0.8 fusion.3
  438.0 0.6 constant_dynamic-slice_fusion
  438.7 0.6 constant_dynamic-slice_fusion.1
  439.3 1.9 copy.52
  441.2 1.6 copy.53
  442.9 1.9 copy.54
  (9 shorter events, 0.1 us)
Async XLA Ops:
  131.1 74.4 %copy-start = (bf16[2,1,10,768]{3,0,2,1:T(2,128)(2,1)S(1)}, bf16[2,1,10,768]{3,0,2,1:T(2,128)(2,1)}, u32[]{:S(2)}) copy-start(bf16[2,1,10,768]{3,0,2,1:T(2,128)(2,1)} %param.18) | copy-start | bytes 92164

commit v7 on v6

--- a/solution.py
+++ b/solution.py
@@ -533,7 +533,7 @@
     enter(z, links)
 
     first = [net.copy("p", src, dst, net.sends(1), net.recvs(1)) for src, dst in (
-        (q_in.at[other], tq), (o_in.at[other], to), (u_in.at[other], tu), (d_in.at[other], td),
+        (q_in.at[other], tq), (d_in.at[other], td), (u_in.at[other], tu), (o_in.at[other], to),
         (s_in, S.at[z, x, y, c]),
     )]
     for cp in first:
@@ -546,28 +546,19 @@
         lo, hi = jnp.where(c == 0, a, b), jnp.where(c == 0, b, a)
         return jnp.concatenate([lo, hi], axis=-1).astype(BF)
 
-    outs = (
+    places = (
+        (aq, Q.at[mine, :, span(rw * w, rw), span(cn * y, cn)]),
+        (ad, D.at[mine, span(rd * w, rd), span(cn * y, cn)]),
         (au, U.at[mine, span(rw * w, rw), span(cu * y, cu)]),
-        (aq, Q.at[mine, :, span(rw * w, rw), span(cn * y, cn)]),
         (ao, O.at[mine, span(rw * w, rw), span(cn * y, cn)]),
-        (ad, D.at[mine, span(rd * w, rd), span(cn * y, cn)]),
     )
-    first[2].wait()
-    au[...] = join(u_in[mine], tu[...])
-    first[0].wait()
-    for j in range(3):
-        aq[j] = join(q_in[mine, j], tq[j])
-    first[1].wait()
-    ao[...] = join(o_in[mine], to[...])
-    first[3].wait()
-    ad[...] = join(d_in[mine], td[...])
-    first[4].wait()
-    own_small.wait()
-    local = [pltpu.make_async_copy(src, dst, lsem.at[k]) for k, (src, dst) in enumerate(outs)]
-    for cp in local:
-        cp.start()
-    for cp in local:
-        cp.wait()
+
+    def put(*which):
+        local = [pltpu.make_async_copy(*places[k], lsem.at[k]) for k in which]
+        for cp in local:
+            cp.start()
+        for cp in local:
+            cp.wait()
 
     main = rd - rw
 
@@ -701,13 +692,27 @@
     small_y = Lane("y", lambda zp: [S.at[z, :, y]], lambda zp: [S.at[z, :, 1 - y]], 1)
     line_s = Line(lambda zp: [S.at[zp]], 1)
 
+    first[0].wait()
+    for j in range(3):
+        aq[j] = join(q_in[mine, j], tq[j])
+    put(0)
+    x1.send(0)
+    line_a[0].own()
+    first[1].wait()
+    ad[...] = join(d_in[mine], td[...])
+    put(1)
+    y1.send(0)
+    line_d[0].own()
+    first[2].wait()
+    au[...] = join(u_in[mine], tu[...])
+    first[3].wait()
+    ao[...] = join(o_in[mine], to[...])
+    put(2, 3)
+    first[4].wait()
+    own_small.wait()
     small_x.send(0)
-    x1.send(0)
-    y1.send(0)
     x_u1.send(z)
     y_u2.send(z)
-    line_a[0].own()
-    line_d[0].own()
     line_u.own()
     y_a[0].send(z)
     x_d[0].send(z)
@@ -1058,7 +1063,7 @@
         for part in swap:
             part.send(zp)
 
-    def open_slab(v):
+    def open_q(v):
         zp = order[v]
         if v == 0:
             left(0).wait()
@@ -1068,12 +1073,18 @@
         swap[0].recv(zp)
         products(0, 3, zp)
         y_a.send(zp)
+
+    def open_d(v):
+        zp = order[v]
         left_g(v, zp).wait()
         if v == 0:
             right(8).wait()
         swap[1].recv(zp)
         products_down(v, zp)
         x_d.send(zp)
+
+    def open_u(v):
+        zp = order[v]
         if v == 0:
             left_g(1, order[1]).start()
             for j in (1, 2):
@@ -1113,26 +1124,34 @@
         add_all(u2_part(zp, x, y), bufs_s2(zp))
         line_u.go(zp)
 
-    open_slab(0)
+    open_q(0)
+    open_d(0)
+    open_u(0)
     mid_a(order[0])
     small[0].wait()
     s_a[...] = sm_in[...] + s_p[...]
     small[1].start()
-    open_slab(1)
+    open_q(1)
+    open_d(1)
     mid_d(order[0])
+    open_u(1)
     mid_u(order[0])
     small[1].wait()
     s_b[...] = s_a[...] + s_x[...]
     small[2].start()
-    open_slab(2)
+    open_q(2)
+    open_d(2)
     mid_a(order[1])
+    open_u(2)
     close(order[0])
     mid_d(order[1])
     mid_u(order[1])
     small[2].wait()
     s_sum[...] = s_b[...] + s_y[...]
-    open_slab(3)
+    open_q(3)
+    open_d(3)
     mid_a(order[2])
+    open_u(3)
     close(order[1])
     mid_d(order[2])
     mid_u(order[2])

time: 446 us -> 445 us (level)
  no operation moved by 1% of the time
where the time goes in v7:
time: 445 us; the launch traced here: 444 us
  Pallas kernels  409 us (92%)
  local copies, waits for them, and re-layouts  30.2 us (7%)
    pallas_call x1, Pallas kernels, scatter_fast(): pl.pallas_call(scatter_kernel, in_specs=[hbm, hbm, hbm, vmem], out_specs=...  137 us
    pallas_call x1, Pallas kernels, gather_fast(): pl.pallas_call(gather_kernel, in_specs=[vmem] * 5, out_specs=[hbm] * 5, o...  118 us
    pallas_call x1, Pallas kernels, forward_local(): pl.pallas_call(fwd_kernel, grid=(SEGS, LAYERS), in_specs=[smem, smem, pl....  67.1 us
    pallas_call x1, Pallas kernels, backward_local(): pl.pallas_call(bwd_kernel, grid=(SEGS, LAYERS), in_specs=[smem, smem, pl....  64 us
    pallas_call x1, Pallas kernels, weight_grads(): pl.pallas_call(product_kernel, grid_spec=pltpu.PrefetchScalarGridSpec(num...  23.5 us
    unnamed x16, local copies, waits for them, and re-layouts  23.2 us

profile of v7, /device:TPU:0, one launch (start us, length us, event | category | flops | bytes accessed | tf_op | source)
XLA Modules:
  0.0 443.9 jit_solution(11808096427147718111)
XLA Ops:
  0.6 2.6 copy.45
  3.2 0.8 bitcast_convert_fusion
  4.0 0.7 pad_maximum_fusion.mem0
  4.8 1.9 copy.26.d_in
  6.7 0.1 pad.13.clone
  6.7 0.8 maximum_maximum_fusion
  7.5 0.6 pad_convert_fusion.1.s_in
  8.1 118.1 %weight_gather.1 = (bf16[2,3,768,768]{3,2,1,0:T(8,128)(2,1)}, bf16[2,768,768]{2,1,0:T(8,128)(2,1)}, bf16[2,768,3072]{2,1,0:T(8,128)(2,1)}, bf16[2,3072,768]{2,1,0:T(8,128)(2,1)}, f32[4,2,2,2,8,128]{5,4,3,2,1,0:T(8,128)}) custom-call(bf16[2,3,96,192]{3,2,1,0:T(8,128)(2,1)} %q_in.1, bf16[2,96,192]{2,1,0:T(8,128)(2,1)} %o_in.1, bf16[2,96,768]{2,1,0:T(8,128)(2,1)} %u_in.1, ...), custom_call_target="tpu_custom_call" | custom-call | tf_op jit(solution)/shard_map/weight_gather/pallas_call | solution.py:807
  126.2 1.0 copy.46
  127.2 0.7 slice.38.bias
  127.9 0.9 slice.49
  128.9 0.7 broadcast_in_dim_reshape.3.ubias
  129.6 0.7 slice.41.norm
  130.3 0.0 copy-start
  130.3 67.1 %rmt_forward.1 = (bf16[2,4,108,768]{3,2,1,0:T(8,128)(2,1)}, f32[2,24,768]{2,1,0:T(8,128)}, bf16[2,1024,5376]{2,1,0:T(8,128)(2,1)}, bf16[2,1024,2304]{2,1,0:T(8,1...) custom-call(s32[2]{0:T(128)} %bitcast.44, ...), custom_call_target="tpu_custom_call" | custom-call | tf_op jit(solution)/shard_map/rmt_forward/pallas_call | solution.py:200
  197.4 3.1 copy.31
  200.5 0.9 fusion
  201.4 0.6 copy.32
  202.0 2.6 copy.44
  204.6 0.0 copy-done
  204.7 0.7 pad_convert_fusion.gm0
  205.3 64.0 %rmt_backward.1 = (bf16[2,4,108,768]{3,2,1,0:T(8,128)(2,1)}, f32[2,24,768]{2,1,0:T(8,128)}, bf16[2,1024,6912]{2,1,0:T(8,128)(2,1)}, f32[24,768]{1,0:T(8,128)}) custom-call(s32[2]{0:T(128)} %bitcast.45, s32[2]{0:T(128)} %bitcast.47, bf16[2,4,108,768]{3,2,1,0:T(8,128)(2,1)} %bitcast.36, f32[2,24,768]{2,1,0:T(8,128)} %pad_convert_fusion.gm0, ...), custom_call_target="tpu_custom_call" | custom-call | tf_op jit(solution)/shard_map/rmt_backward/pallas_call | solution.py:389
  269.3 3.1 copy.33
  272.4 0.9 fusion.1
  273.3 0.6 copy.34
  274.0 23.5 %weight_products.1.gw = bf16[1,12,768,768]{3,2,1,0:T(8,128)(2,1)} custom-call(s32[1]{0:T(128)} %bitcast.15.ids, bf16[2,1024,5376]{2,1,0:T(8,128)(2,1)} %get-tuple-element.49.lhs, bf16[2,1024,6912]{2,1,0:T(8,128)(2,1)} %get-tuple-element.50.rhs), custom_call_target="tpu_custom_call" | custom-call | tf_op jit(solution)/shard_map/weight_products/pallas_call | solution.py:442
  297.5 136.6 %gradient_scatter.1 = (f32[2,3,96,192]{3,2,1,0:T(8,128)}, f32[2,96,192]{2,1,0:T(8,128)}, f32[2,96,768]{2,1,0:T(8,128)}, f32[2,384,192]{2,1,0:T(8,128)}, f32[24,768]{1,0:T(8,128)}) custom-call(bf16[1,12,768,768]{3,2,1,0:T(8,128)(2,1)} %weight_products.1.gw, bf16[2,1024,5376]{2,1,0:T(8,128)(2,1)} %get-tuple-element.49.lhs, ...), custom_call_target="tpu_custom_call" | custom-call | tf_op jit(solution)/shard_map/gradient_scatter/pallas_call | solution.py:1266
  434.1 2.2 copy.35
  436.3 0.8 fusion.3
  437.1 0.6 constant_dynamic-slice_fusion
  437.8 0.6 constant_dynamic-slice_fusion.1
  438.5 1.9 copy.52
  440.4 1.6 copy.53
  442.0 1.9 copy.54
  (9 shorter events, 0.1 us)
Async XLA Ops:
  130.3 74.4 %copy-start = (bf16[2,1,10,768]{3,0,2,1:T(2,128)(2,1)S(1)}, bf16[2,1,10,768]{3,0,2,1:T(2,128)(2,1)}, u32[]{:S(2)}) copy-start(bf16[2,1,10,768]{3,0,2,1:T(2,128)(2,1)} %param.18) | copy-start | bytes 92164

commit v8 on v7

--- a/solution.py
+++ b/solution.py
@@ -81,7 +81,7 @@
 
 
 def fwd_kernel(
-    counts, lens, text, mem0, wqkv_hbm, wo_hbm, wup_hbm, wdn_hbm, bias, ubias, norm,
+    counts, lens, text, mem0, wqkv_hbm, wo_hbm, wup_hbm, wdn_hbm, par, ubias,
     text_out, mem_out, lhs_out, qkv_out, p_out, gp_out, xh1_out, xh2_out, rs_out,
     x_ref, mem_ref, y_ref, acc_ref, wqkv, wo, wup, wdn, wsem,
 ):
@@ -90,6 +90,7 @@
     d = x_ref.shape[-1]
     a_out, c_out, y_out = (lhs_out.at[:, :, j * d : (j + 1) * d] for j in range(3))
     g_out = lhs_out.at[:, :, 3 * d :]
+    bias, norm = par.at[0:LAYERS], par.at[LAYERS : 2 * LAYERS]
     loads = Loads(((wqkv_hbm, wqkv), (wo_hbm, wo), (wup_hbm, wup), (wdn_hbm, wdn)), wsem, seg == 0, (0, 1))
 
     @pl.when((seg == 0) & (layer == 0))
@@ -190,7 +191,7 @@
 
 
 def forward_local(text, mem, counts, lens, weights):
-    wqkv, wo, wup, wdn, bias, ubias, norm = weights
+    wqkv, wo, wup, wdn, par, ubias = weights
     d, ff = wup.shape[1:]
     mem0 = jnp.concatenate([jnp.zeros((MB, TEXT - TAIL, d), F32), mem.astype(F32), mem.astype(F32)], axis=1)
     total = SEGS * ROWS
@@ -204,7 +205,7 @@
             smem, smem,
             pl.BlockSpec((MB, 1, TEXT, d), lambda s, l: (0, s, 0, 0)),
             whole(mem0.shape), hbm, hbm, hbm, hbm,
-            whole(bias.shape), whole((LAYERS, 1, ff)), whole(norm.shape),
+            whole(par.shape), whole((LAYERS, 1, ff)),
         ],
         out_specs=[
             pl.BlockSpec((MB, 1, TEXT, d), lambda s, l: (0, s, 0, 0)),
@@ -234,13 +235,13 @@
             dimension_semantics=("arbitrary", "arbitrary"), vmem_limit_bytes=VMEM_LIMIT
         ),
         name="rmt_forward",
-    )(counts, lens, text, mem0, wqkv, wo, wup, wdn, bias.astype(F32), ubias.astype(F32)[:, None, :], norm.astype(F32))
+    )(counts, lens, text, mem0, wqkv, wo, wup, wdn, par, ubias.astype(F32)[:, None, :])
     text_out, mem_end = outs[:2]
     return text_out, mem_end[:, TEXT - TAIL + MEM :].astype(BF), outs[2:]
 
 
 def bwd_kernel(
-    counts, lens, cot, gm0, qkv, p_in, gp_in, xh1_in, xh2_in, rs_in, wqkv_hbm, wo_hbm, wup_hbm, wdn_hbm, norm,
+    counts, lens, cot, gm0, qkv, p_in, gp_in, xh1_in, xh2_in, rs_in, wqkv_hbm, wo_hbm, wup_hbm, wdn_hbm, par,
     tg_out, gm_out, rhs_out, small_out,
     g_ref, gm_ref, t_ref, acc_ref, dc_ref, wqkv, wo, wup, wdn, wsem, gb_out, gub_out, gn_out,
 ):
@@ -250,6 +251,7 @@
     loads = Loads(((wqkv_hbm, wqkv), (wo_hbm, wo), (wup_hbm, wup), (wdn_hbm, wdn)), wsem, seg == SEGS - 1, (1, 0))
     d = g_ref.shape[-1]
     ff = wup.shape[-1]
+    norm = par.at[LAYERS : 2 * LAYERS]
     dqkv_out, dao_out = rhs_out.at[:, :, 0 : 3 * d], rhs_out.at[:, :, 3 * d : 4 * d]
     du_out, df_out = rhs_out.at[:, :, 4 * d : 4 * d + ff], rhs_out.at[:, :, 4 * d + ff :]
 
@@ -374,7 +376,7 @@
 
 
 def backward_local(cot, cot_mem, counts, lens, kept, weights):
-    wqkv, wo, wup, wdn, _, _, norm = weights
+    wqkv, wo, wup, wdn, par, _ = weights
     _, qkv, p_all, gp, xh1, xh2, rs = kept
     d, ff = wup.shape[1:]
     gm0 = jnp.concatenate([jnp.zeros((MB, TEXT - TAIL + MEM, d), F32), cot_mem.astype(F32)], axis=1)
@@ -395,7 +397,7 @@
             whole(gm0.shape),
             kept_spec(ROWS, 3 * d), kept_spec(units, 128), kept_spec(ROWS, ff), kept_spec(ROWS, d), kept_spec(ROWS, d),
             pl.BlockSpec((1, 2, ROWS, 128), lambda s, l: (LAYERS - 1 - l, 0, SEGS - 1 - s, 0)),
-            hbm, hbm, hbm, hbm, whole(norm.shape),
+            hbm, hbm, hbm, hbm, whole(par.shape),
         ],
         out_specs=[
             pl.BlockSpec((MB, 1, TEXT, d), lambda s, l: (0, SEGS - 1 - s, 0, 0)),
@@ -419,7 +421,7 @@
             dimension_semantics=("arbitrary", "arbitrary"), vmem_limit_bytes=VMEM_LIMIT
         ),
         name="rmt_backward",
-    )(counts, lens, cot, gm0, qkv, p_all, gp, xh1, xh2, rs, wqkv, wo, wup, wdn, norm.astype(F32))
+    )(counts, lens, cot, gm0, qkv, p_all, gp, xh1, xh2, rs, wqkv, wo, wup, wdn, par)
     tg, gm = outs[:2]
     return tg, gm[:, TEXT - TAIL + MEM :].astype(BF), outs[2], outs[3]
 
@@ -827,7 +829,7 @@
     S = S.reshape(8, 4, 8, 128)[..., :rw]
     rows = jnp.transpose(S, (2, 1, 0, 3)).reshape(8, 4, d)
     ub = jnp.transpose(S[:, :, 4:6], (2, 0, 1, 3)).reshape(2, ff)
-    return Q, O, U, D, rows[0:2], ub, rows[2:4]
+    return Q, O, U, D, rows, ub
 
 
 def accumulate(dst, src, rows, step=48):
@@ -1293,7 +1295,7 @@
     wide = [(wqkv, 2), (wo, 1), (wup, 1), (wdn, 1), (bias, 2), (norm, 2)]
     wqkv, wo, wup, wdn, bias, norm = (lax.all_gather(w, "wide", axis=k, tiled=True) for w, k in wide)
     ubias = lax.all_gather(ubias, ("wide", "narrow"), axis=1, tiled=True)
-    return wqkv, wo, wup, wdn, bias, ubias, norm
+    return wqkv, wo, wup, wdn, jnp.concatenate([bias, norm], axis=0).astype(F32), ubias
 
 
 def scatter_two(grad, row_axis, col_axis):

time: 445 us -> 444 us (level)
  no operation moved by 1% of the time
where the time goes in v8:
time: 444 us; the launch traced here: 443 us
  Pallas kernels  409 us (92%)
  local copies, waits for them, and re-layouts  29.6 us (7%)
    pallas_call x1, Pallas kernels, scatter_fast(): pl.pallas_call(scatter_kernel, in_specs=[hbm, hbm, hbm, vmem], out_specs=...  137 us
    pallas_call x1, Pallas kernels, gather_fast(): pl.pallas_call(gather_kernel, in_specs=[vmem] * 5, out_specs=[hbm] * 5, o...  118 us
    pallas_call x1, Pallas kernels, forward_local(): pl.pallas_call(fwd_kernel, grid=(SEGS, LAYERS), in_specs=[smem, smem, pl....  67.1 us
    pallas_call x1, Pallas kernels, backward_local(): pl.pallas_call(bwd_kernel, grid=(SEGS, LAYERS), in_specs=[smem, smem, pl....  64 us
    pallas_call x1, Pallas kernels, weight_grads(): pl.pallas_call(product_kernel, grid_spec=pltpu.PrefetchScalarGridSpec(num...  23.5 us
    unnamed x16, local copies, waits for them, and re-layouts  23.2 us

profile of v8, /device:TPU:0, one launch (start us, length us, event | category | flops | bytes accessed | tf_op | source)
XLA Modules:
  0.0 443.3 jit_solution(17189300730705662217)
XLA Ops:
  0.6 2.6 copy.45
  3.3 0.8 bitcast_convert_fusion
  4.0 0.7 pad_maximum_fusion.mem0
  4.8 1.9 copy.26.d_in
  6.7 0.1 pad.13.clone
  6.7 0.8 maximum_maximum_fusion
  7.5 0.6 pad_convert_fusion.1.s_in
  8.1 118.2 %weight_gather.1 = (bf16[2,3,768,768]{3,2,1,0:T(8,128)(2,1)}, bf16[2,768,768]{2,1,0:T(8,128)(2,1)}, bf16[2,768,3072]{2,1,0:T(8,128)(2,1)}, bf16[2,3072,768]{2,1,0:T(8,128)(2,1)}, f32[4,2,2,2,8,128]{5,4,3,2,1,0:T(8,128)}) custom-call(bf16[2,3,96,192]{3,2,1,0:T(8,128)(2,1)} %q_in.1, bf16[2,96,192]{2,1,0:T(8,128)(2,1)} %o_in.1, bf16[2,96,768]{2,1,0:T(8,128)(2,1)} %u_in.1, ...), custom_call_target="tpu_custom_call" | custom-call | tf_op jit(solution)/shard_map/weight_gather/pallas_call | solution.py:809
  126.3 1.0 copy.46
  127.3 0.8 reshape.42.par
  128.0 0.9 slice.32
  129.0 0.7 broadcast_in_dim_reshape.3.ubias
  129.7 0.0 copy-start
  129.7 67.1 %rmt_forward.1 = (bf16[2,4,108,768]{3,2,1,0:T(8,128)(2,1)}, f32[2,24,768]{2,1,0:T(8,128)}, bf16[2,1024,5376]{2,1,0:T(8,128)(2,1)}, bf16[2,1024,2304]{2,1,0:T(8,1...) custom-call(s32[2]{0:T(128)} %bitcast.42, ...), custom_call_target="tpu_custom_call" | custom-call | tf_op jit(solution)/shard_map/rmt_forward/pallas_call | solution.py:201
  196.8 3.1 copy.31
  199.9 0.9 fusion
  200.8 0.6 copy.32
  201.5 2.6 copy.44
  204.1 0.0 copy-done
  204.1 0.7 pad_convert_fusion.gm0
  204.7 64.0 %rmt_backward.1 = (bf16[2,4,108,768]{3,2,1,0:T(8,128)(2,1)}, f32[2,24,768]{2,1,0:T(8,128)}, bf16[2,1024,6912]{2,1,0:T(8,128)(2,1)}, f32[24,768]{1,0:T(8,128)}) custom-call(s32[2]{0:T(128)} %bitcast.43, s32[2]{0:T(128)} %bitcast.45, bf16[2,4,108,768]{3,2,1,0:T(8,128)(2,1)} %bitcast.33, f32[2,24,768]{2,1,0:T(8,128)} %pad_convert_fusion.gm0, ...), custom_call_target="tpu_custom_call" | custom-call | tf_op jit(solution)/shard_map/rmt_backward/pallas_call | solution.py:391
  268.7 3.1 copy.33
  271.8 0.9 fusion.1
  272.7 0.6 copy.34
  273.4 23.5 %weight_products.1.gw = bf16[1,12,768,768]{3,2,1,0:T(8,128)(2,1)} custom-call(s32[1]{0:T(128)} %bitcast.15.ids, bf16[2,1024,5376]{2,1,0:T(8,128)(2,1)} %get-tuple-element.49.lhs, bf16[2,1024,6912]{2,1,0:T(8,128)(2,1)} %get-tuple-element.50.rhs), custom_call_target="tpu_custom_call" | custom-call | tf_op jit(solution)/shard_map/weight_products/pallas_call | solution.py:444
  296.9 136.6 %gradient_scatter.1 = (f32[2,3,96,192]{3,2,1,0:T(8,128)}, f32[2,96,192]{2,1,0:T(8,128)}, f32[2,96,768]{2,1,0:T(8,128)}, f32[2,384,192]{2,1,0:T(8,128)}, f32[24,768]{1,0:T(8,128)}) custom-call(bf16[1,12,768,768]{3,2,1,0:T(8,128)(2,1)} %weight_products.1.gw, bf16[2,1024,5376]{2,1,0:T(8,128)(2,1)} %get-tuple-element.49.lhs, ...), custom_call_target="tpu_custom_call" | custom-call | tf_op jit(solution)/shard_map/gradient_scatter/pallas_call | solution.py:1268
  433.5 2.2 copy.35
  435.7 0.8 fusion.2
  436.5 0.6 constant_dynamic-slice_fusion
  437.2 0.6 constant_dynamic-slice_fusion.1
  437.8 1.9 copy.52
  439.8 1.6 copy.53
  441.4 1.9 copy.54
  (8 shorter events, 0.1 us)
Async XLA Ops:
  129.7 74.4 %copy-start = (bf16[2,1,10,768]{3,0,2,1:T(2,128)(2,1)S(1)}, bf16[2,1,10,768]{3,0,2,1:T(2,128)(2,1)}, u32[]{:S(2)}) copy-start(bf16[2,1,10,768]{3,0,2,1:T(2,128)(2,1)} %param.18) | copy-start | bytes 92164
